TPU v7x, 32 devices: a whole 2x2x4 slice. The times are simulated.
32 devices in a mesh: fsdp: 32 (over z, y, x, core).
Axes of the slice: x: 2, y: 2, z: 4, core: 2. Of those that a mesh axis runs over, the one named last changes fastest.
Arguments:
- hidden_in: bfloat16 [4096, 2048], P('fsdp'), may hold values from -6 to 6
- out_grad: bfloat16 [4096, 2048], P('fsdp'), may hold values from -6 to 6
- seq_lengths: int32 [64], replicated, may hold values from 16 to 112, as said below
- seq_device: int32 [64], replicated, may hold values from 0 to 31, as said below
- attn_gain: bfloat16 [2048], P('fsdp'), may hold values from 0.5 to 1.5
- q_gain: bfloat16 [128], P('fsdp'), may hold values from 0.5 to 2
- k_gain: bfloat16 [128], P('fsdp'), may hold values from 0.5 to 2
- w_query: bfloat16 [2048, 2048], P('fsdp'), may hold values from -0.125 to 0.125
- w_key: bfloat16 [2048, 1024], P('fsdp'), may hold values from -0.125 to 0.125
- w_value: bfloat16 [2048, 1024], P('fsdp'), may hold values from -0.125 to 0.125
- w_out: bfloat16 [2048, 2048], P('fsdp'), may hold values from -0.5 to 0.5
- mlp_gain: bfloat16 [2048], P('fsdp'), may hold values from 0.5 to 1.5
- w_gate: bfloat16 [2048, 6144], P('fsdp'), may hold values from -0.125 to 0.125
- w_up: bfloat16 [2048, 6144], P('fsdp'), may hold values from -0.125 to 0.125
- w_down: bfloat16 [6144, 2048], P('fsdp'), may hold values from -0.078125 to 0.078125
Outputs:
- hidden_out: bfloat16 [4096, 2048], P('fsdp')
- input_grad: float32 [4096, 2048], P('fsdp')
- grad_attn_gain: float32 [2048], P('fsdp')
- grad_q_gain: float32 [128], P('fsdp')
- grad_k_gain: float32 [128], P('fsdp')
- grad_w_query: float32 [2048, 2048], P('fsdp')
- grad_w_key: float32 [2048, 1024], P('fsdp')
- grad_w_value: float32 [2048, 1024], P('fsdp')
- grad_w_out: float32 [2048, 2048], P('fsdp')
- grad_mlp_gain: float32 [2048], P('fsdp')
- grad_w_gate: float32 [2048, 6144], P('fsdp')
- grad_w_up: float32 [2048, 6144], P('fsdp')
- grad_w_down: float32 [6144, 2048], P('fsdp')
Inputs may be any that keep to these rules, and one draw needn't show every extreme that they name: `seq_lengths`: each sequence has at least 16 tokens; the two sequences of one device fill together at most 128 slots, and in every draw some device's fill all 128. `seq_device`: every device holds exactly two sequences.
All inputs are finite; a program needn't handle non-finite values.
Results may differ from a plain program's by a relative error of at most 0.017.
Values may be sent and summed in bfloat16 or wider, within the bound.
A program may use at most 384 MiB of HBM per device.

v0:
```python
import jax
import jax.numpy as jnp
from jax import lax
from jax.sharding import PartitionSpec as P

H = 16
KVH = 8
HD = 128


epsilon = 1e-06
rope_base = 1000000.0
masked_score = -1e30
contract_rows = (((0,), (0,)), ((), ()))
contract_cols = (((1,), (1,)), ((), ()))


def layout(seq_lengths, seq_device, owner, slots):
    owned = seq_device == owner
    counts = jnp.where(owned, seq_lengths, 0)
    starts = jnp.cumsum(counts) - counts
    places = jnp.arange(slots, dtype=jnp.int32)
    inside = (
        owned[:, None]
        & (places[None, :] >= starts[:, None])
        & (places[None, :] < (starts + counts)[:, None])
    )
    labels = jnp.arange(seq_lengths.shape[0], dtype=jnp.int32)
    segment = jnp.sum(jnp.where(inside, labels[:, None] + 1, 0), axis=0) - 1
    position = jnp.sum(jnp.where(inside, places[None, :] - starts[:, None], 0), axis=0)
    return (segment, position)


def allowed_pairs(segment):
    places = jnp.arange(segment.shape[0], dtype=jnp.int32)
    earlier = places[None, :] < places[:, None]
    same_seq = (segment[:, None] == segment[None, :]) & (segment[:, None] >= 0)
    return (places[:, None] == places[None, :]) | earlier & same_seq


def rmsnorm(values, gain):
    return values * lax.rsqrt(jnp.mean(values * values, axis=-1, keepdims=True) + epsilon) * gain


def rotary(values, position):
    half_dim = values.shape[-1] // 2
    freqs = jnp.power(rope_base, -2.0 * jnp.arange(half_dim, dtype=jnp.float32) / values.shape[-1])
    angles = position.astype(jnp.float32)[:, None] * freqs[None, :]
    cosine = jnp.concatenate([jnp.cos(angles), jnp.cos(angles)], axis=-1)[:, None, :]
    sine = jnp.concatenate([jnp.sin(angles), jnp.sin(angles)], axis=-1)[:, None, :]
    rotated = jnp.concatenate([-values[..., half_dim:], values[..., :half_dim]], axis=-1)
    return values * cosine + rotated * sine


def matmul(left, right):
    return jnp.dot(left, right, preferred_element_type=jnp.float32)


def times_rows(left, right):
    return lax.dot_general(left, right, contract_rows, preferred_element_type=jnp.float32)


def times_cols(left, right):
    return lax.dot_general(left, right, contract_cols, preferred_element_type=jnp.float32)


def per_device(
    hidden_in,
    out_grad,
    seq_lengths,
    seq_device,
    attn_gain,
    q_gain,
    k_gain,
    w_query,
    w_key,
    w_value,
    w_out,
    mlp_gain,
    w_gate,
    w_up,
    w_down,
):
    slots = hidden_in.shape[0]
    groups = H // KVH
    score_scale = HD ** (-0.5)
    segment, position = layout(seq_lengths, seq_device, lax.axis_index("fsdp"), slots)
    allowed = allowed_pairs(segment)[None, None]

    def query_path(raw, gain):
        return rotary(rmsnorm(raw.reshape(slots, H, HD), gain), position)

    def key_path(raw, gain):
        return rotary(rmsnorm(raw.reshape(slots, KVH, HD), gain), position)

    def swiglu(gate_in, up_in):
        return jax.nn.silu(gate_in) * up_in

    attn_set = (
        lax.all_gather(attn_gain, "fsdp", axis=0, tiled=True),
        lax.all_gather(q_gain, "fsdp", axis=0, tiled=True),
        lax.all_gather(k_gain, "fsdp", axis=0, tiled=True),
        lax.all_gather(w_query, "fsdp", axis=0, tiled=True),
        lax.all_gather(w_key, "fsdp", axis=0, tiled=True),
        lax.all_gather(w_value, "fsdp", axis=0, tiled=True),
        lax.all_gather(w_out, "fsdp", axis=0, tiled=True),
    )
    gain_attn, gain_query, gain_key, query_w, key_w, value_w, out_w = attn_set
    inputs = hidden_in.astype(jnp.float32)
    normed = rmsnorm(inputs, gain_attn.astype(jnp.float32)).astype(jnp.bfloat16)
    query_raw = matmul(normed, query_w)
    key_raw = matmul(normed, key_w)
    value_raw = matmul(normed, value_w)
    queries = (
        query_path(query_raw, gain_query.astype(jnp.float32))
        .astype(jnp.bfloat16)
        .reshape(slots, KVH, groups, HD)
    )
    keys = key_path(key_raw, gain_key.astype(jnp.float32)).astype(jnp.bfloat16)
    values = value_raw.astype(jnp.bfloat16).reshape(slots, KVH, HD)

    def masked_logits():
        scores = (
            jnp.einsum("qgrd,kgd->grqk", queries, keys, preferred_element_type=jnp.float32)
            * score_scale
        )
        return jnp.where(allowed, scores, masked_score)

    logits = masked_logits()
    row_top = jnp.max(logits, axis=-1, keepdims=True)
    exponent = jnp.exp(logits - row_top)
    row_total = jnp.sum(exponent, axis=-1, keepdims=True)
    log_total = row_top + jnp.log(row_total)
    weights = (exponent / row_total).astype(jnp.bfloat16)
    mixed = jnp.einsum("grqk,kgd->qgrd", weights, values, preferred_element_type=jnp.float32)
    mixed = mixed.reshape(slots, H * HD).astype(jnp.bfloat16)
    middle = inputs + matmul(mixed, out_w)
    mlp_set = (
        lax.all_gather(mlp_gain, "fsdp", axis=0, tiled=True),
        lax.all_gather(w_gate, "fsdp", axis=0, tiled=True),
        lax.all_gather(w_up, "fsdp", axis=0, tiled=True),
        lax.all_gather(w_down, "fsdp", axis=0, tiled=True),
    )
    gain_mlp, gate_w, up_w, down_w = mlp_set
    second = rmsnorm(middle, gain_mlp.astype(jnp.float32)).astype(jnp.bfloat16)
    gate_out = matmul(second, gate_w)
    up_out = matmul(second, up_w)
    hidden = swiglu(gate_out, up_out).astype(jnp.bfloat16)
    hidden_out = (middle + matmul(hidden, down_w)).astype(jnp.bfloat16)
    gain_mlp, gate_w, up_w, down_w = (
        lax.all_gather(mlp_gain, "fsdp", axis=0, tiled=True),
        lax.all_gather(w_gate, "fsdp", axis=0, tiled=True),
        lax.all_gather(w_up, "fsdp", axis=0, tiled=True),
        lax.all_gather(w_down, "fsdp", axis=0, tiled=True),
    )
    grad_down = lax.psum_scatter(
        times_rows(hidden, out_grad), "fsdp", scatter_dimension=0, tiled=True
    )
    d_hidden = times_cols(out_grad, down_w)
    unused_out, swiglu_pull = jax.vjp(swiglu, gate_out, up_out)
    d_gate, d_up = swiglu_pull(d_hidden)
    d_gate_up = jnp.concatenate([d_gate.astype(jnp.bfloat16), d_up.astype(jnp.bfloat16)], axis=1)
    grad_gate_up = lax.psum_scatter(
        times_rows(second, d_gate_up), "fsdp", scatter_dimension=0, tiled=True
    )
    ff_width = gate_w.shape[1]
    d_second = times_cols(d_gate_up, jnp.concatenate([gate_w, up_w], axis=1))
    unused_norm, second_pull = jax.vjp(rmsnorm, middle, gain_mlp.astype(jnp.float32))
    d_middle_norm, grad_gain_mlp = second_pull(d_second)
    d_middle = out_grad.astype(jnp.float32) + d_middle_norm
    gain_attn, gain_query, gain_key, query_w, key_w, value_w, out_w = (
        lax.all_gather(attn_gain, "fsdp", axis=0, tiled=True),
        lax.all_gather(q_gain, "fsdp", axis=0, tiled=True),
        lax.all_gather(k_gain, "fsdp", axis=0, tiled=True),
        lax.all_gather(w_query, "fsdp", axis=0, tiled=True),
        lax.all_gather(w_key, "fsdp", axis=0, tiled=True),
        lax.all_gather(w_value, "fsdp", axis=0, tiled=True),
        lax.all_gather(w_out, "fsdp", axis=0, tiled=True),
    )
    d_branch = d_middle.astype(jnp.bfloat16)
    grad_out_w = lax.psum_scatter(
        times_rows(mixed, d_branch), "fsdp", scatter_dimension=0, tiled=True
    )
    d_mixed = times_cols(d_branch, out_w).astype(jnp.bfloat16).reshape(slots, KVH, groups, HD)
    probs = jnp.exp(masked_logits() - log_total)
    weights = probs.astype(jnp.bfloat16)
    d_probs = jnp.einsum("qgrd,kgd->grqk", d_mixed, values, preferred_element_type=jnp.float32)
    d_logits = probs * (d_probs - jnp.sum(probs * d_probs, axis=-1, keepdims=True))
    d_scores = (d_logits * score_scale).astype(jnp.bfloat16)
    d_values = jnp.einsum("grqk,qgrd->kgd", weights, d_mixed, preferred_element_type=jnp.float32)
    d_values = d_values.astype(jnp.bfloat16).reshape(slots, KVH * HD)
    d_queries_rot = jnp.einsum(
        "grqk,kgd->qgrd", d_scores, keys, preferred_element_type=jnp.float32
    ).reshape(slots, H, HD)
    d_keys_rot = jnp.einsum("grqk,qgrd->kgd", d_scores, queries, preferred_element_type=jnp.float32)
    unused_query, query_pull = jax.vjp(query_path, query_raw, gain_query.astype(jnp.float32))
    d_query_raw, grad_gain_query = query_pull(d_queries_rot)
    unused_key, key_pull = jax.vjp(key_path, key_raw, gain_key.astype(jnp.float32))
    d_key_raw, grad_gain_key = key_pull(d_keys_rot)
    d_qkv = jnp.concatenate(
        [d_query_raw.astype(jnp.bfloat16), d_key_raw.astype(jnp.bfloat16), d_values], axis=1
    )
    grad_qkv = lax.psum_scatter(times_rows(normed, d_qkv), "fsdp", scatter_dimension=0, tiled=True)
    d_normed = times_cols(d_qkv, jnp.concatenate([query_w, key_w, value_w], axis=1))
    unused_first, first_pull = jax.vjp(rmsnorm, inputs, gain_attn.astype(jnp.float32))
    d_input_norm, grad_gain_attn = first_pull(d_normed)
    input_grad = d_middle + d_input_norm
    gain_sums = (
        lax.psum_scatter(grad_gain_attn, "fsdp", scatter_dimension=0, tiled=True),
        lax.psum_scatter(grad_gain_query, "fsdp", scatter_dimension=0, tiled=True),
        lax.psum_scatter(grad_gain_key, "fsdp", scatter_dimension=0, tiled=True),
        lax.psum_scatter(grad_gain_mlp, "fsdp", scatter_dimension=0, tiled=True),
    )
    query_width = H * HD
    key_width = KVH * HD
    grad_query_w = grad_qkv[:, :query_width]
    grad_key_w = grad_qkv[:, query_width : query_width + key_width]
    grad_value_w = grad_qkv[:, query_width + key_width :]
    grad_gate = grad_gate_up[:, :ff_width]
    grad_up = grad_gate_up[:, ff_width:]
    return (
        hidden_out,
        input_grad,
        gain_sums[0],
        gain_sums[1],
        gain_sums[2],
        grad_query_w,
        grad_key_w,
        grad_value_w,
        grad_out_w,
        gain_sums[3],
        grad_gate,
        grad_up,
        grad_down,
    )


def solution(mesh):
    return jax.shard_map(
        per_device,
        mesh=mesh,
        in_specs=(
            P("fsdp", None),
            P("fsdp", None),
            P(),
            P(),
            P("fsdp"),
            P("fsdp"),
            P("fsdp"),
            P("fsdp", None),
            P("fsdp", None),
            P("fsdp", None),
            P("fsdp", None),
            P("fsdp"),
            P("fsdp", None),
            P("fsdp", None),
            P("fsdp", None),
        ),
        out_specs=(
            P("fsdp", None),
            P("fsdp", None),
            P("fsdp"),
            P("fsdp"),
            P("fsdp"),
            P("fsdp", None),
            P("fsdp", None),
            P("fsdp", None),
            P("fsdp", None),
            P("fsdp"),
            P("fsdp", None),
            P("fsdp", None),
            P("fsdp", None),
        ),
        check_vma=False,
    )
```

profile of v0, /device:TPU:8, one launch (start us, length us, event | category | flops | bytes accessed | tf_op | source)
XLA Modules:
  0.0 2666.5 jit_solution(15628665575753721912)
XLA Ops:
  15.4 41.0 %all-reduce.13 = (bf16[2048]{0:T(1024)(128)(2,1)S(1)}, bf16[128]{0:T(256)(128)(2,1)S(1)}, bf16[128]{0:T(256)(128)(2,1)S(1)}, bf16[2048]{0:T(1024)(128)(2,1)S(1)}) all-reduce(bf16[2048]{0:T(1024)(128)(2,1)S(1)} %dynamic-update-slice, bf16[128]{0:T(256)(128)(2,1)S(1)} %dynamic-update-slice.1, ...), channel_id=1, replica_groups=mesh['fsdp'=32] {'fsdp'}, use_global_device_ids=true, to_apply=%add.4 | all-reduce | flops 4352 | bytes 17408
  60.9 12.7 all-gather.8.cloned.1.call-done
  73.6 2.9 fusion.26
  76.6 60.4 %all-gather.10.cloned.1.call-done = bf16[2048,1024]{1,0:T(8,128)(2,1)} async-done(((bf16[64,1024]{1,0:T(8,128)(2,1)}), bf16[2048,1024]{1,0:T(8,128)(2,1)}) %all-gather.10.cloned.1.call-update) | async-done | bytes 4194320 | tf_op jit(solution)/shard_map/all_gather | solution.py:104
  137.0 2.9 convolution_bitcast_fusion.3
  141.2 74.6 %all-gather.12.cloned.1.call-done = bf16[2048,2048]{1,0:T(8,128)(2,1)} async-done(((bf16[64,2048]{1,0:T(8,128)(2,1)}), bf16[2048,2048]{1,0:T(8,128)(2,1)}) %all-gather.12.cloned.1.call-update) | async-done | bytes 8388624 | tf_op jit(solution)/shard_map/all_gather | solution.py:103
  215.8 6.8 multiply_reduce_fusion.5
  226.6 67.6 %all-gather.14.cloned.1.call-done = bf16[2048,2048]{1,0:T(8,128)(2,1)} async-done(((bf16[64,2048]{1,0:T(8,128)(2,1)}), bf16[2048,2048]{1,0:T(8,128)(2,1)}) %all-gather.14.cloned.1.call-update) | async-done | bytes 8388624 | tf_op jit(solution)/shard_map/all_gather | solution.py:106
  294.2 4.9 multiply_reduce_fusion.4
  300.8 147.1 %all-gather.20.cloned.1.call-done = bf16[6144,2048]{1,0:T(8,128)(2,1)} async-done(((bf16[192,2048]{1,0:T(8,128)(2,1)}), bf16[6144,2048]{1,0:T(8,128)(2,1)}) %all-gather.20.cloned.1.call-update) | async-done | bytes 25165840 | tf_op jit(solution)/shard_map/all_gather | solution.py:142
  447.9 14.6 fusion.96
  462.5 140.3 %all-gather.18.cloned.1.call-done = bf16[2048,6144]{1,0:T(8,128)(2,1)} async-done(((bf16[64,6144]{1,0:T(8,128)(2,1)}), bf16[2048,6144]{1,0:T(8,128)(2,1)}) %all-gather.18.cloned.1.call-update) | async-done | bytes 25165840 | tf_op jit(solution)/shard_map/all_gather | solution.py:141
  602.8 13.5 fusion.95
  616.3 141.6 %all-gather.16.cloned.1.call-done = bf16[2048,6144]{1,0:T(8,128)(2,1)} async-done(((bf16[64,6144]{1,0:T(8,128)(2,1)}), bf16[2048,6144]{1,0:T(8,128)(2,1)}) %all-gather.16.cloned.1.call-update) | async-done | bytes 25165840 | tf_op jit(solution)/shard_map/all_gather | solution.py:140
  757.9 14.8 fusion.13
  772.7 28.0 %multiply_reduce_fusion = (f32[2048]{0:T(1024)}, f32[128]{0:T(128)}, f32[128,2048]{1,0:T(8,128)}) fusion(f32[128,2048]{1,0:T(8,128)S(1)} %get-tuple-element.57, f32[128]{0:T(128)} %copy-done.31, f32[2048]{0:T(1024)} %convert_element_type.115, bf16[2048,6144]{1,0:T(8,128)(2,1)} %all-gather.18.cloned.1.call-done, ...), kind=kOutput, calls=%fused_computation.64 | convolution fusion | flops 6550976512 | bytes 55591936 | tf_op jit(solution)/shard_map/dot_general | solution.py:64
  804.1 7.1 convolution_convert_fusion
  817.3 4.0 broadcast_multiply_fusion
  821.3 4.0 fusion.42
  832.0 14.3 fusion.57
  847.3 37.5 %fusion.16 = f32[2048,12288]{1,0:T(8,128)} fusion(bf16[128,2048]{1,0:T(8,128)(2,1)S(1)} %copy-done.6, bf16[128,6144]{1,0:T(8,128)(2,1)} %get-tuple-element.36, bf16[128,6144]{1,0:T(8,128)(2,1)} %get-tuple-element.35), kind=kOutput, calls=%fused_computation.28 | convolution fusion | flops 6448742400 | bytes 104333312 | tf_op jit(solution)/shard_map/dot_general | solution.py:60
  886.2 8.1 fusion.59
  895.3 21.4 fusion.97
  917.8 10.3 fusion.28
  928.1 43.6 %all-reduce.12 = (f32[2048]{0:T(1024)S(1)}, f32[128]{0:T(128)S(1)}, f32[128]{0:T(128)S(1)}, f32[2048]{0:T(1024)S(1)}) all-reduce(f32[2048]{0:T(1024)S(1)} %get-tuple-element.15, f32[128]{0:T(128)S(1)} %get-tuple-element.19, f32[128]{0:T(128)S(1)} %copy-done.32, f32[2048]{0:T(1024)S(1)} %copy-done.26), channel_id=2, replica_groups=mesh['fsdp'=32] {'fsdp'}, use_global_device_ids=true, to_apply=%region_15.16.clone | all-reduce | flops 4352 | bytes 34816
  974.1 2.5 fusion.31
  976.6 11.2 fusion.15
  987.7 214.5 %reduce-scatter.5.cloned.1.call-done = f32[64,4096]{1,0:T(8,128)} async-done(((f32[2048,4096]{1,0:T(8,128)}), f32[64,4096]{1,0:T(8,128)}) %reduce-scatter.5.cloned.1.call-update) | async-done | bytes 1048592 | tf_op jit(solution)/shard_map/reduce_scatter | solution.py:203
  1206.0 831.1 %reduce-scatter.9.cloned.1.call-done = f32[64,12288]{1,0:T(8,128)} async-done(((f32[2048,12288]{1,0:T(8,128)}), f32[64,12288]{1,0:T(8,128)}) %reduce-scatter.9.cloned.1.call-update) | async-done | bytes 3145744 | tf_op jit(solution)/shard_map/reduce_scatter | solution.py:163
  2037.1 3.8 fusion.88
  2040.9 178.7 %reduce-scatter.7.cloned.1.call-done = f32[64,2048]{1,0:T(8,128)} async-done(((f32[2048,2048]{1,0:T(8,128)}), f32[64,2048]{1,0:T(8,128)}) %reduce-scatter.7.cloned.1.call-update) | async-done | bytes 524304 | tf_op jit(solution)/shard_map/reduce_scatter | solution.py:181
  2219.6 440.2 %reduce-scatter.11.cloned.1.call-done = f32[192,2048]{1,0:T(8,128)} async-done(((f32[6144,2048]{1,0:T(8,128)}), f32[192,2048]{1,0:T(8,128)}) %reduce-scatter.11.cloned.1.call-update) | async-done | bytes 1572880 | tf_op jit(solution)/shard_map/reduce_scatter | solution.py:156
  (162 shorter events, 45.7 us)
Async XLA Ops:
  7.2 66.4 %copy-start = (bf16[128,2048]{1,0:T(8,128)(2,1)S(1)}, bf16[128,2048]{1,0:T(8,128)(2,1)}, u32[]{:S(2)}) copy-start(bf16[128,2048]{1,0:T(8,128)(2,1)} %param.15) | copy-start | bytes 1572868
  7.2 66.4 %all-gather.8.cloned.1.call-start = ((), (), s32[]{:S(2)}) async-start(), calls=%async_computation.4 | async-start | bytes 4325376 | tf_op jit(solution)/shard_map/all_gather | solution.py:105
  7.9 129.1 %all-gather.10.cloned.1.call-start = ((), (), s32[]{:S(2)}) async-start(), calls=%async_computation.5 | async-start | bytes 4325376 | tf_op jit(solution)/shard_map/all_gather | solution.py:104
  8.7 207.1 %all-gather.12.cloned.1.call-start = ((), (), s32[]{:S(2)}) async-start(), calls=%async_computation.6 | async-start | bytes 8650752 | tf_op jit(solution)/shard_map/all_gather | solution.py:103
  9.4 284.8 %all-gather.14.cloned.1.call-start = ((), (), s32[]{:S(2)}) async-start(), calls=%async_computation.7 | async-start | bytes 8650752 | tf_op jit(solution)/shard_map/all_gather | solution.py:106
  10.0 437.9 %all-gather.20.cloned.1.call-start = ((), (), s32[]{:S(2)}) async-start(), calls=%async_computation.10 | async-start | bytes 25952256 | tf_op jit(solution)/shard_map/all_gather | solution.py:142
  10.6 592.2 %all-gather.18.cloned.1.call-start = ((), (), s32[]{:S(2)}) async-start(), calls=%async_computation.9 | async-start | bytes 25952256 | tf_op jit(solution)/shard_map/all_gather | solution.py:141
  11.1 746.8 %all-gather.16.cloned.1.call-start = ((), (), s32[]{:S(2)}) async-start(), calls=%async_computation.8 | async-start | bytes 25952256 | tf_op jit(solution)/shard_map/all_gather | solution.py:140
  11.9 1190.4 %reduce-scatter.5.cloned.1.call-start = ((), (), s32[]{:S(2)}) async-start(), calls=%async_computation.11 | async-start | bytes 34603008 | tf_op jit(solution)/shard_map/reduce_scatter | solution.py:203
  56.4 84.3 %copy-start.29 = (f32[128]{0:T(128)}, f32[128]{0:T(128)S(1)}, u32[]{:S(2)}) copy-start(f32[128]{0:T(128)S(1)} %convert_element_type.106) | copy-start | bytes 1540
  56.4 166.5 %copy-start.27 = (f32[128]{0:T(128)}, f32[128]{0:T(128)S(1)}, u32[]{:S(2)}) copy-start(f32[128]{0:T(128)S(1)} %convert_element_type.109) | copy-start | bytes 1540
  60.8 155.0 %copy-start.24 = (f32[128]{0:T(128)}, f32[128]{0:T(128)S(1)}, u32[]{:S(2)}) copy-start(f32[128]{0:T(128)S(1)} %fusion.72) | copy-start | bytes 1540
  140.5 82.0 %copy-start.14 = (f32[128,8]{0,1:T(8,128)}, f32[128,8]{0,1:T(8,128)S(1)}, u32[]{:S(2)}) copy-start(f32[128,8]{0,1:T(8,128)S(1)} %fusion.69) | copy-start | bytes 12292
  141.2 82.1 %copy-start.13 = (bf16[128,8,128,1]{0,2,3,1:T(8,128)(2,1)}, bf16[128,8,128,1]{0,2,3,1:T(8,128)(2,1)S(1)}, u32[]{:S(2)}) copy-start(bf16[128,8,128,1]{0,2,3,1:T(8,128)(2,1)S(1)} %fusion.58) | copy-start | bytes 786436
  222.6 1.9 copy-start.19
  224.5 69.7 %copy-start.16 = (f32[8,2,128]{2,1,0:T(2,128)}, f32[8,2,128]{2,1,0:T(2,128)S(1)}, u32[]{:S(2)}) copy-start(f32[8,2,128]{2,1,0:T(2,128)S(1)} %get-tuple-element.54) | copy-start | bytes 24580
  224.7 69.6 %copy-start.22 = (f32[8,2,128]{2,1,0:T(2,128)}, f32[8,2,128]{2,1,0:T(2,128)S(1)}, u32[]{:S(2)}) copy-start(f32[8,2,128]{2,1,0:T(2,128)S(1)} %fusion.44) | copy-start | bytes 24580
  294.2 5.0 copy-start.17
  294.2 5.0 copy-start.23
  294.2 5.6 copy-start.18
  825.4 5.1 copy-start.8
  825.4 5.1 copy-start.28
  830.5 1.5 copy-start.25
  831.6 14.7 copy-start.9
  846.3 1190.8 %reduce-scatter.9.cloned.1.call-start = ((), (), s32[]{:S(2)}) async-start(), calls=%async_computation.13 | async-start | bytes 103809024 | tf_op jit(solution)/shard_map/reduce_scatter | solution.py:163
  884.8 1.4 copy-start.7
  884.9 1334.7 %reduce-scatter.7.cloned.1.call-start = ((), (), s32[]{:S(2)}) async-start(), calls=%async_computation.12 | async-start | bytes 17301504 | tf_op jit(solution)/shard_map/reduce_scatter | solution.py:181
  894.3 1765.5 %reduce-scatter.11.cloned.1.call-start = ((), (), s32[]{:S(2)}) async-start(), calls=%async_computation.14 | async-start | bytes 51904512 | tf_op jit(solution)/shard_map/reduce_scatter | solution.py:156
  917.8 10.3 copy-start.26
  917.8 10.3 copy-start.32
  917.8 56.2 %copy-start.35 = (f32[128]{0:T(128)S(1)}, f32[128]{0:T(128)}, u32[]{:S(2)}) copy-start(f32[128]{0:T(128)} %copy-done.34) | copy-start | bytes 1540
  971.7 4.9 copy-start.3
  (15 other events, 12.4 us)
Sparse Core Ops, SparseCore 0:
  10.9 62.6 all-gather.7
  76.4 60.4 all-gather.9
  139.9 75.8 all-gather.11
  218.5 75.6 all-gather.13
  296.9 150.8 all-gather.19
  450.6 152.1 all-gather.17
  605.7 152.1 all-gather.15
  846.4 355.8 reduce-scatter.4
  1208.7 828.3 reduce-scatter.8
  2039.8 179.7 reduce-scatter.6
  2226.6 433.1 reduce-scatter.10
where the time goes:
time: 2680 us; the launch traced here: 2670 us
  waiting for transfers between devices  2310 us (86%)
  matrix products  212 us (8%)
  blocking collectives  84.7 us (3%)
    reduce_scatter x1, waiting for transfers between devices, per_device(): lax.psum_scatter(times_rows(second, d_gate_up), 'fsdp', scatter_dimension...  831 us
    reduce_scatter x1, waiting for transfers between devices, per_device(): lax.psum_scatter(times_rows(hidden, out_grad), 'fsdp', scatter_dimension=...  440 us
    reduce_scatter x1, waiting for transfers between devices, per_device(): lax.psum_scatter(times_rows(normed, d_qkv), 'fsdp', scatter_dimension=0,...  215 us
    reduce_scatter x1, waiting for transfers between devices, per_device(): lax.psum_scatter(times_rows(mixed, d_branch), 'fsdp', scatter_dimension=0...  179 us
    all_gather x1, waiting for transfers between devices, per_device(): lax.all_gather(w_down, 'fsdp', axis=0, tiled=True)  147 us
    all_gather x1, waiting for transfers between devices, per_device(): lax.all_gather(w_gate, 'fsdp', axis=0, tiled=True)  142 us
    all_gather x1, waiting for transfers between devices, per_device(): lax.all_gather(w_up, 'fsdp', axis=0, tiled=True)  140 us
    unnamed x2, blocking collectives  84.7 us
  transfers between devices with their start and end apart: 11, of which 11 were waited for; matrix products, arithmetic and copies ran while one was open for 6% of the time, Pallas kernels for 0%

commit v1 on v0

--- a/solution.py
+++ b/solution.py
@@ -1,11 +1,923 @@
+import functools
+
 import jax
 import jax.numpy as jnp
 from jax import lax
+from jax.experimental import pallas as pl
+from jax.experimental.pallas import tpu as pltpu
 from jax.sharding import PartitionSpec as P
 
 H = 16
 KVH = 8
 HD = 128
+LINE = 4
+RING = 8
+MESH = pl.DeviceIdType.MESH
+ANY = pl.BlockSpec(memory_space=pl.ANY)
+VMEM = pl.BlockSpec(memory_space=pltpu.VMEM)
+DMA = pltpu.SemaphoreType.DMA
+bf16 = jnp.bfloat16
+f32 = jnp.float32
+
+
+def where_am_i():
+    me = lax.axis_index("fsdp")
+    core = me % 2
+    z = me // RING
+    f_bit = 2 + 2 * core
+    s_bit = 4 - 2 * core
+    first = me + f_bit * (1 - 2 * ((me // f_bit) % 2))
+    second = me + s_bit * (1 - 2 * ((me // s_bit) % 2))
+    sibling = me + 1 - 2 * core
+    return me, z, first, second, sibling
+
+
+def greet(peers):
+    barrier = pltpu.get_barrier_semaphore()
+    for peer in peers:
+        pl.semaphore_signal(barrier, inc=1, device_id=(peer,), device_id_type=MESH)
+    pl.semaphore_wait(barrier, len(peers))
+
+
+def remote(src, dst, send_sem, recv_sem, device):
+    return pltpu.make_async_remote_copy(
+        src_ref=src,
+        dst_ref=dst,
+        send_sem=send_sem,
+        recv_sem=recv_sem,
+        device_id=(device,),
+        device_id_type=MESH,
+    )
+
+
+def line_peers(me):
+    return [lax.rem(me + RING * k, RING * LINE) for k in range(1, LINE)]
+
+
+def on_line(z, k, body):
+    for step in ((-k, k) if k else (0,)):
+
+        @pl.when((z + step >= 0) & (z + step < LINE))
+        def _(step=step):
+            body(step)
+
+
+def fetch_attn_kernel(
+    w_ref, gate_ref, up_ref, w_out, p_out,
+    w_tmp, p_tmp, local, up_s, down_s, first_s, second_s, sib_s, recv, ex_send, ex_recv,
+):
+    me, z, first, second, sibling = where_am_i()
+    greet(line_peers(me) + [first, second, sibling])
+    col, fcol, scol = me % RING, first % RING, second % RING
+    sfcol = (second + first - me) % RING
+    width = p_tmp.shape[1] // 2
+
+    def send(src, shard, sems, device):
+        return remote(src, w_out.at[shard], sems.at[shard], recv.at[shard], device)
+
+    def arrived(shard):
+        send(w_out.at[shard], shard, sib_s, sibling).wait_recv()
+
+    def exchange(k, which):
+        peer_z = lax.rem(z + k, LINE)
+        src = (gate_ref, up_ref)[which].at[:, pl.ds(pl.multiple_of(peer_z * width, width), width)]
+        dst = p_out.at[z, :, pl.ds(which * width, width)]
+        return remote(src, dst, ex_send.at[k, which], ex_recv.at[k, which], col + RING * peer_z)
+
+    @pl.when(z < LINE - 1)
+    def _():
+        send(w_ref, me, up_s, me + RING).start()
+
+    @pl.when(z > 0)
+    def _():
+        send(w_ref, me, down_s, me - RING).start()
+
+    send(w_ref, me, first_s, first).start()
+    send(w_ref, me, second_s, second).start()
+    send(w_ref, me, sib_s, sibling).start()
+    w_in = pltpu.make_async_copy(w_ref, w_tmp, local.at[0])
+    w_in.start()
+    p_in = [
+        pltpu.make_async_copy(
+            ref.at[:, pl.ds(pl.multiple_of(z * width, width), width)],
+            p_tmp.at[:, pl.ds(which * width, width)],
+            local.at[1 + which],
+        )
+        for which, ref in enumerate((gate_ref, up_ref))
+    ]
+    for copy in p_in:
+        copy.start()
+    for k in range(1, LINE):
+        for which in range(2):
+            exchange(k, which).start()
+
+    def own(k):
+        def body(step):
+            shard = me + RING * step
+            src = w_out.at[shard]
+            arrived(shard)
+            if step < 0:
+
+                @pl.when(z < LINE - 1)
+                def _():
+                    send(src, shard, up_s, me + RING).start()
+            else:
+
+                @pl.when(z > 0)
+                def _():
+                    send(src, shard, down_s, me - RING).start()
+
+            send(src, shard, first_s, first).start()
+            send(src, shard, second_s, second).start()
+            send(src, shard, sib_s, sibling).start()
+
+        on_line(z, k, body)
+
+    def other(base, k, onward):
+        def body(step):
+            shard = base + RING * (z + step)
+            src = w_out.at[shard]
+            arrived(shard)
+            if onward:
+                send(src, shard, second_s, second).start()
+            send(src, shard, sib_s, sibling).start()
+
+        on_line(z, k, body)
+
+    own(1)
+    other(fcol, 0, True)
+    own(2)
+    other(fcol, 1, True)
+    other(scol, 0, False)
+    w_in.wait()
+    w_back = pltpu.make_async_copy(w_tmp, w_out.at[me], local.at[3])
+    w_back.start()
+    for copy in p_in:
+        copy.wait()
+    p_back = pltpu.make_async_copy(p_tmp, p_out.at[z], local.at[4])
+    p_back.start()
+    own(3)
+    other(fcol, 2, True)
+    other(scol, 1, False)
+    other(sfcol, 0, False)
+    other(fcol, 3, True)
+    other(scol, 2, False)
+    other(sfcol, 1, False)
+    other(scol, 3, False)
+    other(sfcol, 2, False)
+    other(sfcol, 3, False)
+
+    def from_sibling(i, carry):
+        arrived(2 * i + sibling % 2)
+        return carry
+
+    lax.fori_loop(0, RING * LINE // 2, from_sibling, 0)
+    w_back.wait()
+    p_back.wait()
+    for k in range(1, LINE):
+        for which in range(2):
+            exchange(k, which).wait_send()
+            src_z = lax.rem(z + LINE - k, LINE)
+            landed = p_out.at[src_z, :, pl.ds(which * width, width)]
+            remote(
+                landed, landed, ex_send.at[k, which], ex_recv.at[k, which], col + RING * src_z
+            ).wait_recv()
+    for k in range(LINE):
+
+        @pl.when((z < LINE - 1) & (k <= z))
+        def _(k=k):
+            send(w_ref, col + RING * k, up_s, me + RING).wait_send()
+
+        @pl.when((z > 0) & (k >= z))
+        def _(k=k):
+            send(w_ref, col + RING * k, down_s, me - RING).wait_send()
+
+        send(w_ref, col + RING * k, first_s, first).wait_send()
+        send(w_ref, col + RING * k, second_s, second).wait_send()
+        send(w_ref, fcol + RING * k, second_s, second).wait_send()
+        for base in (col, fcol, scol, sfcol):
+            send(w_ref, base + RING * k, sib_s, sibling).wait_send()
+
+
+def fetch_attn(w, gate, up):
+    rows, cols = w.shape
+    width = gate.shape[1] // LINE
+    n = RING * LINE
+    return pl.pallas_call(
+        fetch_attn_kernel,
+        out_shape=(
+            jax.ShapeDtypeStruct((n, rows, cols), bf16),
+            jax.ShapeDtypeStruct((LINE, rows, 2 * width), bf16),
+        ),
+        in_specs=[ANY] * 3,
+        out_specs=(ANY, ANY),
+        scratch_shapes=[
+            pltpu.VMEM((rows, cols), bf16),
+            pltpu.VMEM((rows, 2 * width), bf16),
+            DMA((5,)),
+            DMA((n,)),
+            DMA((n,)),
+            DMA((n,)),
+            DMA((n,)),
+            DMA((n,)),
+            DMA((n,)),
+            DMA((LINE, 2)),
+            DMA((LINE, 2)),
+        ],
+        compiler_params=pltpu.CompilerParams(collective_id=0, has_side_effects=True),
+        name="fetch_attn",
+    )(w, gate, up)
+
+
+def fetch_mlp_kernel(
+    p_ref, d_ref, x_ref, g_ref, gu_out, d_out, x_out, g_out,
+    p_tmp, d_tmp, x_tmp, g_tmp, local, up_s, down_s, line_r, first_s, second_s, sib_s, recv,
+):
+    me, z, first, second, sibling = where_am_i()
+    greet(line_peers(me) + [first, second, sibling])
+    col, fcol, scol = me % RING, first % RING, second % RING
+    sfcol = (second + first - me) % RING
+    pieces = LINE + 1
+
+    def spot(piece, shard):
+        return gu_out.at[piece, shard] if piece < LINE else d_out.at[shard]
+
+    def source(piece):
+        return p_ref.at[piece] if piece < LINE else d_ref
+
+    def send(src, piece, shard, sems, device):
+        return remote(
+            src, spot(piece, shard), sems.at[piece, shard], recv.at[piece, shard], device
+        )
+
+    def arrived(piece, shard):
+        send(spot(piece, shard), piece, shard, sib_s, sibling).wait_recv()
+
+    tokens = ((x_ref, x_out), (g_ref, g_out))
+
+    def line_send(src, which, shard, sems, device):
+        return remote(
+            src,
+            tokens[which][1].at[shard],
+            sems.at[which, shard],
+            line_r.at[which, shard],
+            device,
+        )
+
+    for which in range(2):
+
+        @pl.when(z < LINE - 1)
+        def _(which=which):
+            line_send(tokens[which][0], which, z, up_s, me + RING).start()
+
+        @pl.when(z > 0)
+        def _(which=which):
+            line_send(tokens[which][0], which, z, down_s, me - RING).start()
+
+    for piece in range(pieces):
+        send(source(piece), piece, col, first_s, first).start()
+        send(source(piece), piece, col, second_s, second).start()
+        send(source(piece), piece, col, sib_s, sibling).start()
+    moves = (
+        (p_ref, p_tmp, gu_out.at[:, col]),
+        (d_ref, d_tmp, d_out.at[col]),
+        (x_ref, x_tmp, x_out.at[z]),
+        (g_ref, g_tmp, g_out.at[z]),
+    )
+    ins = [pltpu.make_async_copy(m[0], m[1], local.at[i]) for i, m in enumerate(moves)]
+    outs = [pltpu.make_async_copy(m[1], m[2], local.at[4 + i]) for i, m in enumerate(moves)]
+    for copy in ins:
+        copy.start()
+
+    def along(k):
+        def body(step):
+            shard = z + step
+            for which in range(2):
+                src = tokens[which][1].at[shard]
+                line_send(src, which, shard, up_s, second).wait_recv()
+                if step < 0:
+
+                    @pl.when(z < LINE - 1)
+                    def _(which=which, src=src):
+                        line_send(src, which, shard, up_s, me + RING).start()
+                else:
+
+                    @pl.when(z > 0)
+                    def _(which=which, src=src):
+                        line_send(src, which, shard, down_s, me - RING).start()
+
+        on_line(z, k, body)
+
+    def other(piece, shard, onward):
+        arrived(piece, shard)
+        if onward:
+            send(spot(piece, shard), piece, shard, second_s, second).start()
+        send(spot(piece, shard), piece, shard, sib_s, sibling).start()
+
+    other(0, fcol, True)
+    other(0, scol, False)
+    other(1, fcol, True)
+    other(1, scol, False)
+    for copy, back in zip(ins, outs):
+        copy.wait()
+        back.start()
+    along(1)
+    other(2, fcol, True)
+    other(2, scol, False)
+    other(3, fcol, True)
+    other(3, scol, False)
+    along(2)
+    other(4, fcol, True)
+    other(4, scol, False)
+    for piece in range(pieces):
+        other(piece, sfcol, False)
+    along(3)
+    for piece in range(pieces):
+        for k in range(RING // 2):
+            arrived(piece, 2 * k + sibling % 2)
+    for back in outs:
+        back.wait()
+    for which in range(2):
+        for k in range(LINE):
+
+            @pl.when((z < LINE - 1) & (k <= z))
+            def _(which=which, k=k):
+                line_send(tokens[which][0], which, k, up_s, me + RING).wait_send()
+
+            @pl.when((z > 0) & (k >= z))
+            def _(which=which, k=k):
+                line_send(tokens[which][0], which, k, down_s, me - RING).wait_send()
+
+    for piece in range(pieces):
+        src = source(piece)
+        send(src, piece, col, first_s, first).wait_send()
+        send(src, piece, col, second_s, second).wait_send()
+        send(src, piece, fcol, second_s, second).wait_send()
+        for base in (col, fcol, scol, sfcol):
+            send(src, piece, base, sib_s, sibling).wait_send()
+
+
+def fetch_mlp(p, down, tokens, cotangent):
+    lines, rows, cols = p.shape
+    pieces = LINE + 1
+    return pl.pallas_call(
+        fetch_mlp_kernel,
+        out_shape=(
+            jax.ShapeDtypeStruct((LINE, RING, rows, cols), bf16),
+            jax.ShapeDtypeStruct((RING,) + down.shape, bf16),
+            jax.ShapeDtypeStruct((LINE,) + tokens.shape, bf16),
+            jax.ShapeDtypeStruct((LINE,) + cotangent.shape, bf16),
+        ),
+        in_specs=[ANY] * 4,
+        out_specs=(ANY,) * 4,
+        scratch_shapes=[
+            pltpu.VMEM(p.shape, bf16),
+            pltpu.VMEM(down.shape, bf16),
+            pltpu.VMEM(tokens.shape, bf16),
+            pltpu.VMEM(cotangent.shape, bf16),
+            DMA((8,)),
+            DMA((2, LINE)),
+            DMA((2, LINE)),
+            DMA((2, LINE)),
+            DMA((pieces, RING)),
+            DMA((pieces, RING)),
+            DMA((pieces, RING)),
+            DMA((pieces, RING)),
+        ],
+        compiler_params=pltpu.CompilerParams(collective_id=1, has_side_effects=True),
+        name="fetch_mlp",
+    )(p, down, tokens, cotangent)
+
+
+def add_rows(out, *terms):
+    rows = out.shape[0]
+
+    def body(i, carry):
+        at = pl.ds(pl.multiple_of(i * 16, 16), 16)
+        total = terms[0][at, :].astype(f32)
+        for term in terms[1:]:
+            total = total + term[at, :].astype(f32)
+        out[at, :] = total.astype(out.dtype)
+        return carry
+
+    lax.fori_loop(0, rows // 16, body, 0)
+
+
+def reduce_mlp_kernel(
+    gu_ref, d_ref, ds_ref, y_ref, gu_out, d_out, ds_out, y_out,
+    gu_own, gu_sib, gu_sec, gu_fst, d_own, d_sib, d_sec, d_fst, t_own, t_down, t_up,
+    load, t_load, c_send, c_recv, s_send, s_recv, f_send, f_recv, down_s, down_r, up_s, up_r,
+):
+    me, z, first, second, sibling = where_am_i()
+    greet([lax.rem(me + RING, RING * LINE), lax.rem(me + RING * (LINE - 1), RING * LINE)]
+          + [first, second, sibling])
+    core = me % 2
+    mine, fst, sec = (me % RING) // 2, (first % RING) // 2, (second % RING) // 2
+    far = ((second + first - me) % RING) // 2
+    half = d_fst.shape[0] // 2
+    last = LINE - 1
+    groups = ((0, LINE), (LINE, LINE + 2))
+
+    def block(gu, d, piece, group):
+        if group == 0:
+            return gu.at[piece]
+        return d.at[pl.ds(pl.multiple_of((piece - LINE) * half, half), half)]
+
+    def each(body):
+        for group, (lo, hi) in enumerate(groups):
+
+            def step(piece, carry, group=group):
+                body(piece, group)
+                return carry
+
+            lax.fori_loop(lo, hi, step, 0)
+
+    def stored(target, piece, group):
+        if group == 0:
+            return gu_ref.at[piece, target]
+        return block(None, d_ref.at[target], piece, group)
+
+    def to_sibling(quad, piece, group):
+        return remote(
+            stored(2 * quad + 1 - core, piece, group),
+            block(gu_sib.at[quad], d_sib.at[quad], piece, group),
+            c_send.at[quad, piece],
+            c_recv.at[quad, piece],
+            sibling,
+        )
+
+    def loading(quad, piece, group):
+        return pltpu.make_async_copy(
+            stored(2 * quad + core, piece, group),
+            block(gu_own.at[quad], d_own.at[quad], piece, group),
+            load.at[quad, piece],
+        )
+
+    def to_second(quad, slot, piece, group):
+        return remote(
+            block(gu_own.at[quad], d_own.at[quad], piece, group),
+            block(gu_sec.at[slot], d_sec.at[slot], piece, group),
+            s_send.at[slot, piece],
+            s_recv.at[slot, piece],
+            second,
+        )
+
+    def to_first(piece, group):
+        return remote(
+            block(gu_own.at[fst], d_own.at[fst], piece, group),
+            block(gu_fst, d_fst, piece, group),
+            f_send.at[piece],
+            f_recv.at[piece],
+            first,
+        )
+
+    def send_line(src, which, target, up):
+        landing, sends, lands = (t_up, up_s, up_r) if up else (t_down, down_s, down_r)
+        return remote(
+            src,
+            landing.at[which, target],
+            sends.at[which, target],
+            lands.at[which, target],
+            me + RING if up else me - RING,
+        )
+
+    tokens = [
+        pltpu.make_async_copy(ref, t_own.at[which], t_load.at[which])
+        for which, ref in enumerate((ds_ref, y_ref))
+    ]
+    for copy in tokens:
+        copy.start()
+    for theirs, own in ((far, far), (fst, sec), (sec, fst), (mine, mine)):
+
+        def begin(piece, group, theirs=theirs, own=own):
+            to_sibling(theirs, piece, group).start()
+            loading(own, piece, group).start()
+
+        each(begin)
+    for copy in tokens:
+        copy.wait()
+    for k in range(last):
+        for which in range(2):
+
+            @pl.when(z == last)
+            def _(k=k, which=which):
+                send_line(t_own.at[which, k], which, k, False).start()
+
+            @pl.when(z == 0)
+            def _(k=k, which=which):
+                send_line(t_own.at[which, last - k], which, last - k, True).start()
+
+    def relay(target, which, up):
+        @pl.when((target > z) & (z > 0) if up else (target < z) & (z < last))
+        def _():
+            landing = (t_up if up else t_down).at[which, target]
+            send_line(landing, which, target, up).wait_recv()
+            add_rows(landing, landing, t_own.at[which, target])
+            send_line(landing, which, target, up).start()
+
+    for quad, slot in ((far, 1), (sec, 0)):
+
+        def pass_on(piece, group, quad=quad, slot=slot):
+            loading(quad, piece, group).wait()
+            to_sibling(quad, piece, group).wait_recv()
+            own = block(gu_own.at[quad], d_own.at[quad], piece, group)
+            add_rows(own, own, block(gu_sib.at[quad], d_sib.at[quad], piece, group))
+            to_second(quad, slot, piece, group).start()
+
+        each(pass_on)
+    for which in range(2):
+        relay(0, which, False)
+        relay(last, which, True)
+
+    def narrow(piece, group):
+        loading(fst, piece, group).wait()
+        to_sibling(fst, piece, group).wait_recv()
+        to_second(far, 1, piece, group).wait_recv()
+        own = block(gu_own.at[fst], d_own.at[fst], piece, group)
+        add_rows(
+            own,
+            own,
+            block(gu_sib.at[fst], d_sib.at[fst], piece, group),
+            block(gu_sec.at[1], d_sec.at[1], piece, group),
+        )
+        to_first(piece, group).start()
+
+    each(narrow)
+    for k in range(1, last):
+        for which in range(2):
+            relay(k, which, False)
+            relay(last - k, which, True)
+
+    def finish(piece, group):
+        loading(mine, piece, group).wait()
+        to_sibling(mine, piece, group).wait_recv()
+        to_second(sec, 0, piece, group).wait_recv()
+        to_first(piece, group).wait_recv()
+        add_rows(
+            block(gu_out, d_out, piece, group),
+            block(gu_own.at[mine], d_own.at[mine], piece, group),
+            block(gu_sib.at[mine], d_sib.at[mine], piece, group),
+            block(gu_sec.at[0], d_sec.at[0], piece, group),
+            block(gu_fst, d_fst, piece, group),
+        )
+
+    each(finish)
+    for which, out in enumerate((ds_out, y_out)):
+        own = t_own.at[which, z]
+        above, below = t_down.at[which, z], t_up.at[which, z]
+
+        @pl.when(z < last)
+        def _(which=which, above=above):
+            send_line(above, which, z, False).wait_recv()
+
+        @pl.when(z > 0)
+        def _(which=which, below=below):
+            send_line(below, which, z, True).wait_recv()
+
+        @pl.when(z == 0)
+        def _(out=out, own=own, above=above):
+            add_rows(out, own, above)
+
+        @pl.when(z == last)
+        def _(out=out, own=own, below=below):
+            add_rows(out, own, below)
+
+        @pl.when((z > 0) & (z < last))
+        def _(out=out, own=own, above=above, below=below):
+            add_rows(out, own, above, below)
+
+    def drain(piece, group):
+        for quad in (far, fst, sec, mine):
+            to_sibling(quad, piece, group).wait_send()
+        to_second(far, 1, piece, group).wait_send()
+        to_second(sec, 0, piece, group).wait_send()
+        to_first(piece, group).wait_send()
+
+    each(drain)
+    for which in range(2):
+        for k in range(LINE):
+
+            @pl.when((z > 0) & (k < z))
+            def _(which=which, k=k):
+                send_line(t_down.at[which, k], which, k, False).wait_send()
+
+            @pl.when((z < last) & (k > z))
+            def _(which=which, k=k):
+                send_line(t_up.at[which, k], which, k, True).wait_send()
+
+
+def reduce_mlp(gu, d, ds, y):
+    rows, cols = gu.shape[2:]
+    drows, dcols = d.shape[1:]
+    tok = ds.shape[1:]
+    quads = RING // 2
+    pieces = LINE + 2
+    return pl.pallas_call(
+        reduce_mlp_kernel,
+        out_shape=(
+            jax.ShapeDtypeStruct((LINE, rows, cols), bf16),
+            jax.ShapeDtypeStruct((drows, dcols), f32),
+            jax.ShapeDtypeStruct(tok, f32),
+            jax.ShapeDtypeStruct(tok, f32),
+        ),
+        in_specs=[ANY] * 4,
+        out_specs=(VMEM,) * 4,
+        scratch_shapes=[
+            pltpu.VMEM((quads, LINE, rows, cols), bf16),
+            pltpu.VMEM((quads, LINE, rows, cols), bf16),
+            pltpu.VMEM((2, LINE, rows, cols), bf16),
+            pltpu.VMEM((LINE, rows, cols), bf16),
+            pltpu.VMEM((quads, drows, dcols), bf16),
+            pltpu.VMEM((quads, drows, dcols), bf16),
+            pltpu.VMEM((2, drows, dcols), bf16),
+            pltpu.VMEM((drows, dcols), bf16),
+            pltpu.VMEM((2, LINE) + tok, bf16),
+            pltpu.VMEM((2, LINE) + tok, bf16),
+            pltpu.VMEM((2, LINE) + tok, bf16),
+            DMA((quads, pieces)),
+            DMA((2,)),
+            DMA((quads, pieces)),
+            DMA((quads, pieces)),
+            DMA((2, pieces)),
+            DMA((2, pieces)),
+            DMA((pieces,)),
+            DMA((pieces,)),
+            DMA((2, LINE)),
+            DMA((2, LINE)),
+            DMA((2, LINE)),
+            DMA((2, LINE)),
+        ],
+        compiler_params=pltpu.CompilerParams(
+            collective_id=2, has_side_effects=True, vmem_limit_bytes=64000 * 1024
+        ),
+        name="reduce_mlp",
+    )(gu, d, ds, y)
+
+
+def reduce_attn_kernel(
+    a_ref, o_ref, gu_ref, s_ref, q_out, k_out, v_out, o_out, gate_out, up_out, s_out,
+    own, sib, sec, fst, down, up, ex, s_sum, s_got, s_line,
+    load, ex_load, c_send, c_recv, s_send, s_recv, f_send, f_recv, down_s, down_r, up_s, up_r,
+    ex_s, ex_r, small_s, small_r,
+):
+    me, z, first, second, sibling = where_am_i()
+    greet(line_peers(me) + [first, second, sibling])
+    core = me % 2
+    q_mine, q_fst, q_sec = (me % RING) // 2, (first % RING) // 2, (second % RING) // 2
+    q_far = ((second + first - me) % RING) // 2
+    last = LINE - 1
+    split = a_ref.shape[2]
+    parts = ((a_ref, pl.ds(0, split)), (o_ref, pl.ds(split, o_ref.shape[2])))
+    order = (
+        last * (1 - z // 2),
+        2 - 2 * z + 5 * (z // 2),
+        1 + z % 2,
+        z,
+    )
+
+    def to_sibling(t, quad, part):
+        ref, at = parts[part]
+        return remote(
+            ref.at[RING * t + 2 * quad + 1 - core],
+            sib.at[t, quad, :, at],
+            c_send.at[t, quad, part],
+            c_recv.at[t, quad, part],
+            sibling,
+        )
+
+    def loading(t, quad, part):
+        ref, at = parts[part]
+        return pltpu.make_async_copy(
+            ref.at[RING * t + 2 * quad + core], own.at[t, quad, :, at], load.at[t, quad, part]
+        )
+
+    def ready(t, quad):
+        for part in range(2):
+            loading(t, quad, part).wait()
+            to_sibling(t, quad, part).wait_recv()
+
+    def to_second(t, quad, slot):
+        return remote(
+            own.at[t, quad], sec.at[slot, t], s_send.at[slot, t], s_recv.at[slot, t], second
+        )
+
+    def to_first(t):
+        return remote(own.at[t, q_fst], fst.at[t], f_send.at[t], f_recv.at[t], first)
+
+    def send_line(src, t, upward):
+        if upward:
+            return remote(src, up.at[t], up_s.at[t], up_r.at[t], me + RING)
+        return remote(src, down.at[t], down_s.at[t], down_r.at[t], me - RING)
+
+    def exchange(k):
+        peer_z = lax.rem(z + k, LINE)
+        return remote(
+            gu_ref.at[peer_z], ex.at[z], ex_s.at[k], ex_r.at[k], me % RING + RING * peer_z
+        )
+
+    def small(step, src, dst, device):
+        return remote(src, dst, small_s.at[step], small_r.at[step], device)
+
+    small_c = small(0, s_ref, s_got.at[0], sibling)
+    small_c.start()
+    for k in range(1, LINE):
+        exchange(k).start()
+    ex_in = pltpu.make_async_copy(gu_ref.at[z], ex.at[z], ex_load)
+    ex_in.start()
+    for t in order:
+        for theirs, ours in ((q_far, q_far), (q_fst, q_sec), (q_sec, q_fst), (q_mine, q_mine)):
+            for part in range(2):
+                to_sibling(t, theirs, part).start()
+                loading(t, ours, part).start()
+
+    def spread(t):
+        for quad, slot in ((q_far, 1), (q_sec, 0)):
+            ready(t, quad)
+            add_rows(own.at[t, quad], own.at[t, quad], sib.at[t, quad])
+            to_second(t, quad, slot).start()
+
+    def narrow(t):
+        ready(t, q_fst)
+        to_second(t, q_far, 1).wait_recv()
+        add_rows(own.at[t, q_fst], own.at[t, q_fst], sib.at[t, q_fst], sec.at[1, t])
+        to_first(t).start()
+
+    def collect(t):
+        ready(t, q_mine)
+        to_second(t, q_sec, 0).wait_recv()
+        to_first(t).wait_recv()
+        mine = own.at[t, q_mine]
+        add_rows(mine, mine, sib.at[t, q_mine], sec.at[0, t], fst.at[t])
+
+        @pl.when((t < z) & (z == last))
+        def _():
+            send_line(mine, t, False).start()
+
+        @pl.when((t > z) & (z == 0))
+        def _():
+            send_line(mine, t, True).start()
+
+    def relay(t):
+        @pl.when((t < z) & (z < last))
+        def _():
+            landing = down.at[t]
+            send_line(landing, t, False).wait_recv()
+            add_rows(landing, landing, own.at[t, q_mine])
+            send_line(landing, t, False).start()
+
+        @pl.when((t > z) & (z > 0))
+        def _():
+            landing = up.at[t]
+            send_line(landing, t, True).wait_recv()
+            add_rows(landing, landing, own.at[t, q_mine])
+            send_line(landing, t, True).start()
+
+    spread(order[0])
+    small_c.wait()
+    s_sum[0] = s_ref[...] + s_got[0]
+    small_f = small(1, s_sum.at[0], s_got.at[1], first)
+    small_f.start()
+    spread(order[1])
+    narrow(order[0])
+    small_f.wait()
+    s_sum[1] = s_sum[0] + s_got[1]
+    small_s2 = small(2, s_sum.at[1], s_got.at[2], second)
+    small_s2.start()
+    spread(order[2])
+    narrow(order[1])
+    collect(order[0])
+    small_s2.wait()
+    s_sum[2] = s_sum[1] + s_got[2]
+    small_line = [
+        small(
+            2 + k, s_sum.at[2], s_line.at[k], me % RING + RING * lax.rem(z + k, LINE)
+        )
+        for k in range(1, LINE)
+    ]
+    for copy in small_line:
+        copy.start()
+    spread(order[3])
+    narrow(order[2])
+    collect(order[1])
+    relay(order[0])
+    narrow(order[3])
+    collect(order[2])
+    relay(order[1])
+    collect(order[3])
+    relay(order[2])
+    ex_in.wait()
+    for k in range(1, LINE):
+        src_z = lax.rem(z + LINE - k, LINE)
+        landed = ex.at[src_z]
+        remote(landed, landed, ex_s.at[k], ex_r.at[k], sibling).wait_recv()
+    width = gate_out.shape[1] // LINE
+    for k in range(LINE):
+        add_rows(gate_out.at[:, pl.ds(k * width, width)], ex.at[k, :, pl.ds(0, width)])
+        add_rows(up_out.at[:, pl.ds(k * width, width)], ex.at[k, :, pl.ds(width, width)])
+    for copy in small_line:
+        copy.wait()
+    s_out[...] = (s_sum[2] + s_line[2]) + (s_line[1] + s_line[3])
+    mine, above, below = own.at[z, q_mine], down.at[z], up.at[z]
+
+    @pl.when(z < last)
+    def _():
+        send_line(above, z, False).wait_recv()
+
+    @pl.when(z > 0)
+    def _():
+        send_line(below, z, True).wait_recv()
+
+    def total(*terms):
+        lo = 0
+        for out in (q_out, k_out, v_out, o_out):
+            at = pl.ds(lo, out.shape[1])
+            add_rows(out, *[term.at[:, at] for term in terms])
+            lo += out.shape[1]
+
+    @pl.when(z == 0)
+    def _():
+        total(mine, above)
+
+    @pl.when(z == last)
+    def _():
+        total(mine, below)
+
+    @pl.when((z > 0) & (z < last))
+    def _():
+        total(mine, above, below)
+
+    for k in range(1, LINE):
+        exchange(k).wait_send()
+    for t in range(LINE):
+        for quad in (q_far, q_fst, q_sec, q_mine):
+            for part in range(2):
+                to_sibling(t, quad, part).wait_send()
+        to_second(t, q_far, 1).wait_send()
+        to_second(t, q_sec, 0).wait_send()
+        to_first(t).wait_send()
+
+        @pl.when(t < z)
+        def _(t=t):
+            send_line(down.at[t], t, False).wait_send()
+
+        @pl.when(t > z)
+        def _(t=t):
+            send_line(up.at[t], t, True).wait_send()
+
+
+def reduce_attn(a, o, gu, small):
+    rows, split = a.shape[1:]
+    owide = o.shape[2]
+    wide = split + owide
+    quads = RING // 2
+    width = gu.shape[2] // 2
+    kv = KVH * HD
+    return pl.pallas_call(
+        reduce_attn_kernel,
+        out_shape=(
+            jax.ShapeDtypeStruct((rows, H * HD), f32),
+            jax.ShapeDtypeStruct((rows, kv), f32),
+            jax.ShapeDtypeStruct((rows, kv), f32),
+            jax.ShapeDtypeStruct((rows, owide), f32),
+            jax.ShapeDtypeStruct((rows, LINE * width), f32),
+            jax.ShapeDtypeStruct((rows, LINE * width), f32),
+            jax.ShapeDtypeStruct(small.shape, f32),
+        ),
+        in_specs=[ANY, ANY, ANY, VMEM],
+        out_specs=(VMEM,) * 7,
+        scratch_shapes=[
+            pltpu.VMEM((LINE, quads, rows, wide), bf16),
+            pltpu.VMEM((LINE, quads, rows, wide), bf16),
+            pltpu.VMEM((2, LINE, rows, wide), bf16),
+            pltpu.VMEM((LINE, rows, wide), bf16),
+            pltpu.VMEM((LINE, rows, wide), bf16),
+            pltpu.VMEM((LINE, rows, wide), bf16),
+            pltpu.VMEM((LINE, rows, 2 * width), bf16),
+            pltpu.VMEM((3,) + small.shape, f32),
+            pltpu.VMEM((3,) + small.shape, f32),
+            pltpu.VMEM((LINE,) + small.shape, f32),
+            DMA((LINE, quads, 2)),
+            DMA,
+            DMA((LINE, quads, 2)),
+            DMA((LINE, quads, 2)),
+            DMA((2, LINE)),
+            DMA((2, LINE)),
+            DMA((LINE,)),
+            DMA((LINE,)),
+            DMA((LINE,)),
+            DMA((LINE,)),
+            DMA((LINE,)),
+            DMA((LINE,)),
+            DMA((LINE,)),
+            DMA((LINE,)),
+            DMA((2 + LINE,)),
+            DMA((2 + LINE,)),
+        ],
+        compiler_params=pltpu.CompilerParams(
+            collective_id=3, has_side_effects=True, vmem_limit_bytes=64000 * 1024
+        ),
+        name="reduce_attn",
+    )(a, o, gu, small)
 
 
 epsilon = 1e-06
@@ -64,7 +976,14 @@
     return lax.dot_general(left, right, contract_cols, preferred_element_type=jnp.float32)
 
 
-def per_device(
+def scatter_sum(partial):
+    total = lax.psum_scatter(
+        partial.astype(jnp.bfloat16), "fsdp", scatter_dimension=0, tiled=True
+    )
+    return total.astype(jnp.float32)
+
+
+def plain(
     hidden_in,
     out_grad,
     seq_lengths,
@@ -153,16 +1072,12 @@
         lax.all_gather(w_up, "fsdp", axis=0, tiled=True),
         lax.all_gather(w_down, "fsdp", axis=0, tiled=True),
     )
-    grad_down = lax.psum_scatter(
-        times_rows(hidden, out_grad), "fsdp", scatter_dimension=0, tiled=True
-    )
+    grad_down = scatter_sum(times_rows(hidden, out_grad))
     d_hidden = times_cols(out_grad, down_w)
     unused_out, swiglu_pull = jax.vjp(swiglu, gate_out, up_out)
     d_gate, d_up = swiglu_pull(d_hidden)
     d_gate_up = jnp.concatenate([d_gate.astype(jnp.bfloat16), d_up.astype(jnp.bfloat16)], axis=1)
-    grad_gate_up = lax.psum_scatter(
-        times_rows(second, d_gate_up), "fsdp", scatter_dimension=0, tiled=True
-    )
+    grad_gate_up = scatter_sum(times_rows(second, d_gate_up))
     ff_width = gate_w.shape[1]
     d_second = times_cols(d_gate_up, jnp.concatenate([gate_w, up_w], axis=1))
     unused_norm, second_pull = jax.vjp(rmsnorm, middle, gain_mlp.astype(jnp.float32))
@@ -178,9 +1093,7 @@
         lax.all_gather(w_out, "fsdp", axis=0, tiled=True),
     )
     d_branch = d_middle.astype(jnp.bfloat16)
-    grad_out_w = lax.psum_scatter(
-        times_rows(mixed, d_branch), "fsdp", scatter_dimension=0, tiled=True
-    )
+    grad_out_w = scatter_sum(times_rows(mixed, d_branch))
     d_mixed = times_cols(d_branch, out_w).astype(jnp.bfloat16).reshape(slots, KVH, groups, HD)
     probs = jnp.exp(masked_logits() - log_total)
     weights = probs.astype(jnp.bfloat16)
@@ -200,7 +1113,7 @@
     d_qkv = jnp.concatenate(
         [d_query_raw.astype(jnp.bfloat16), d_key_raw.astype(jnp.bfloat16), d_values], axis=1
     )
-    grad_qkv = lax.psum_scatter(times_rows(normed, d_qkv), "fsdp", scatter_dimension=0, tiled=True)
+    grad_qkv = scatter_sum(times_rows(normed, d_qkv))
     d_normed = times_cols(d_qkv, jnp.concatenate([query_w, key_w, value_w], axis=1))
     unused_first, first_pull = jax.vjp(rmsnorm, inputs, gain_attn.astype(jnp.float32))
     d_input_norm, grad_gain_attn = first_pull(d_normed)
@@ -235,7 +1148,161 @@
     )
 
 
+def layered(
+    hidden_in,
+    out_grad,
+    seq_lengths,
+    seq_device,
+    attn_gain,
+    q_gain,
+    k_gain,
+    w_query,
+    w_key,
+    w_value,
+    w_out,
+    mlp_gain,
+    w_gate,
+    w_up,
+    w_down,
+):
+    slots, width = hidden_in.shape
+    groups = H // KVH
+    score_scale = HD ** (-0.5)
+    n = RING * LINE
+    rows = w_query.shape[0]
+    me = lax.axis_index("fsdp")
+    segment, position = layout(seq_lengths, seq_device, me, slots)
+    allowed = allowed_pairs(segment)[None, None]
+    query_width = H * HD
+    qkv_width = query_width + 2 * KVH * HD
+    attn_width = qkv_width + w_out.shape[1]
+
+    def query_path(raw, gain):
+        return rotary(rmsnorm(raw.reshape(slots, H, HD), gain), position)
+
+    def key_path(raw, gain):
+        return rotary(rmsnorm(raw.reshape(slots, KVH, HD), gain), position)
+
+    def swiglu(gate_in, up_in):
+        return jax.nn.silu(gate_in) * up_in
+
+    def column(gain):
+        return jnp.pad(gain, (0, rows - gain.shape[0]))[:, None]
+
+    gains = jnp.concatenate([column(g) for g in (attn_gain, mlp_gain, q_gain, k_gain)], axis=1)
+    gains = jnp.pad(gains, ((0, 0), (0, 128 - gains.shape[1])))
+    packed = jnp.concatenate([w_query, w_key, w_value, w_out, gains], axis=1)
+    attn_w, mlp_w = fetch_attn(packed, w_gate, w_up)
+    gain_cols = attn_w[:, :, attn_width : attn_width + 4].astype(f32)
+    gain_attn = gain_cols[:, :, 0].reshape(-1)
+    gain_mlp = gain_cols[:, :, 1].reshape(-1)
+    gain_query = gain_cols[:, : q_gain.shape[0], 2].reshape(-1)
+    gain_key = gain_cols[:, : k_gain.shape[0], 3].reshape(-1)
+    attn_w = attn_w.reshape(n * rows, attn_w.shape[2])
+    qkv_w = attn_w[:, :qkv_width]
+    out_w = attn_w[:, qkv_width:attn_width]
+
+    inputs = hidden_in.astype(f32)
+    normed = rmsnorm(inputs, gain_attn).astype(bf16)
+    qkv_raw = matmul(normed, qkv_w)
+    query_raw = qkv_raw[:, :query_width]
+    key_raw = qkv_raw[:, query_width : query_width + KVH * HD]
+    value_raw = qkv_raw[:, query_width + KVH * HD :]
+    queries = query_path(query_raw, gain_query).astype(bf16).reshape(slots, KVH, groups, HD)
+    keys = key_path(key_raw, gain_key).astype(bf16)
+    values = value_raw.astype(bf16).reshape(slots, KVH, HD)
+    scores = jnp.einsum("qgrd,kgd->grqk", queries, keys, preferred_element_type=f32) * score_scale
+    logits = jnp.where(allowed, scores, masked_score)
+    exponent = jnp.exp(logits - jnp.max(logits, axis=-1, keepdims=True))
+    probs = exponent / jnp.sum(exponent, axis=-1, keepdims=True)
+    weights = probs.astype(bf16)
+    mixed = jnp.einsum("grqk,kgd->qgrd", weights, values, preferred_element_type=f32)
+    mixed = mixed.reshape(slots, query_width).astype(bf16)
+    middle = inputs + matmul(mixed, out_w)
+    second = rmsnorm(middle, gain_mlp).astype(bf16)
+
+    gate_up_w, down_w, tokens, cotangent = fetch_mlp(mlp_w, w_down, second, out_grad)
+    gate_up_w = gate_up_w.reshape(n * rows, gate_up_w.shape[-1])
+    down_w = down_w.reshape(-1, down_w.shape[-1])
+    tokens = tokens.reshape(-1, width)
+    cotangent = cotangent.reshape(-1, width)
+    part = gate_up_w.shape[1] // 2
+    gate_up = matmul(tokens, gate_up_w)
+    gate_out, up_out = gate_up[:, :part], gate_up[:, part:]
+    hidden = swiglu(gate_out, up_out).astype(bf16)
+    y_part = matmul(hidden, down_w).astype(bf16)
+    d_hidden = times_cols(cotangent, down_w)
+    unused_out, swiglu_pull = jax.vjp(swiglu, gate_out, up_out)
+    d_gate, d_up = swiglu_pull(d_hidden)
+    d_gate_up = jnp.concatenate([d_gate.astype(bf16), d_up.astype(bf16)], axis=1)
+    ds_part = times_cols(d_gate_up, gate_up_w).astype(bf16)
+    g_gate_up = times_rows(tokens, d_gate_up).astype(bf16)
+    g_down = times_rows(hidden, cotangent).astype(bf16)
+    g_gate_up, grad_down, d_second, y = reduce_mlp(
+        g_gate_up.reshape(LINE, RING, rows, 2 * part),
+        g_down.reshape(RING, w_down.shape[0], width),
+        ds_part.reshape(LINE, slots, width),
+        y_part.reshape(LINE, slots, width),
+    )
+    hidden_out = (middle + y).astype(bf16)
+
+    unused_norm, second_pull = jax.vjp(rmsnorm, middle, gain_mlp)
+    d_middle_norm, grad_gain_mlp = second_pull(d_second)
+    d_middle = out_grad.astype(f32) + d_middle_norm
+    d_branch = d_middle.astype(bf16)
+    g_out = times_rows(mixed, d_branch).astype(bf16)
+    d_mixed = times_cols(d_branch, out_w).astype(bf16).reshape(slots, KVH, groups, HD)
+    d_probs = jnp.einsum("qgrd,kgd->grqk", d_mixed, values, preferred_element_type=f32)
+    d_logits = probs * (d_probs - jnp.sum(probs * d_probs, axis=-1, keepdims=True))
+    d_scores = (d_logits * score_scale).astype(bf16)
+    d_values = jnp.einsum("grqk,qgrd->kgd", weights, d_mixed, preferred_element_type=f32)
+    d_values = d_values.astype(bf16).reshape(slots, KVH * HD)
+    d_queries_rot = jnp.einsum(
+        "grqk,kgd->qgrd", d_scores, keys, preferred_element_type=f32
+    ).reshape(slots, H, HD)
+    d_keys_rot = jnp.einsum("grqk,qgrd->kgd", d_scores, queries, preferred_element_type=f32)
+    unused_query, query_pull = jax.vjp(query_path, query_raw, gain_query)
+    d_query_raw, grad_gain_query = query_pull(d_queries_rot)
+    unused_key, key_pull = jax.vjp(key_path, key_raw, gain_key)
+    d_key_raw, grad_gain_key = key_pull(d_keys_rot)
+    d_qkv = jnp.concatenate([d_query_raw.astype(bf16), d_key_raw.astype(bf16), d_values], axis=1)
+    g_qkv = times_rows(normed, d_qkv).astype(bf16)
+    d_normed = times_cols(d_qkv, qkv_w)
+    unused_first, first_pull = jax.vjp(rmsnorm, inputs, gain_attn)
+    d_input_norm, grad_gain_attn = first_pull(d_normed)
+    input_grad = d_middle + d_input_norm
+    gain_grads = (grad_gain_attn, grad_gain_query, grad_gain_key, grad_gain_mlp)
+    small = jnp.concatenate(gain_grads)
+    small = jnp.pad(small, (0, -small.shape[0] % 1024)).reshape(-1, 128)
+    g_query, g_key, g_value, g_out, g_gate, g_up, small = reduce_attn(
+        g_qkv.reshape(n, rows, qkv_width), g_out.reshape(n, rows, w_out.shape[1]), g_gate_up, small
+    )
+    small = small.reshape(-1)
+    gain_sums = []
+    lo = 0
+    for grad in gain_grads:
+        share = grad.shape[0] // n
+        gain_sums.append(lax.dynamic_slice(small, (lo + me * share,), (share,)))
+        lo += grad.shape[0]
+    return (
+        hidden_out,
+        input_grad,
+        gain_sums[0],
+        gain_sums[1],
+        gain_sums[2],
+        g_query,
+        g_key,
+        g_value,
+        g_out,
+        gain_sums[3],
+        g_gate,
+        g_up,
+        grad_down,
+    )
+
+
 def solution(mesh):
+    per_device = layered if mesh.shape["fsdp"] == RING * LINE else plain
     return jax.shard_map(
         per_device,
         mesh=mesh,

time: 2680 us -> 625 us (0.23)
  waiting for transfers between devices: 2310 us -> 0 us
  Pallas kernels: 0 us -> 455 us
  matrix products: 212 us -> 117 us
  blocking collectives: 84.7 us -> 0 us
    reduce_scatter x4 -> x0, waiting for transfers between devices: 1660 us -> none  [the longest x1 831 us: per_device(): lax.psum_scatter(times_rows(second, d_gate_up), 'fsdp', scatter_dimension...]
    all_gather x7 -> x0, waiting for transfers between devices: 644 us -> none  [the longest x1 147 us: per_device(): lax.all_gather(w_down, 'fsdp', axis=0, tiled=True)]
    pallas_call x0 -> x4, Pallas kernels: none -> 455 us  [the longest x1 144 us: reduce_attn(): pl.pallas_call(reduce_attn_kernel, out_shape=(jax.ShapeDtypeStruct((rows,...]
    unnamed x2 -> x0, blocking collectives: 84.7 us -> none
    dot_general x4, matrix products: 81.3 us -> 31 us  [times_rows(): lax.dot_general(left, right, contract_rows, preferred_element_type=jnp.fl...]
  transfers between devices with their start and end apart: 11 -> 0, of which waited for: 11 -> 0; matrix products, arithmetic and copies ran while one was open for 6% -> 0% of each run, Pallas kernels for 0% -> 0%
where the time goes in v1:
time: 625 us; the launch traced here: 621 us
  Pallas kernels  455 us (73%)
  matrix products  117 us (19%)
  local copies, waits for them, and re-layouts  24.3 us (4%)
  other arithmetic  22.5 us (4%)
    pallas_call x1, Pallas kernels, reduce_attn(): pl.pallas_call(reduce_attn_kernel, out_shape=(jax.ShapeDtypeStruct((rows,...  144 us
    pallas_call x1, Pallas kernels, fetch_attn(): pl.pallas_call(fetch_attn_kernel, out_shape=(jax.ShapeDtypeStruct((n, row...  121 us
    pallas_call x1, Pallas kernels, reduce_mlp(): pl.pallas_call(reduce_mlp_kernel, out_shape=(jax.ShapeDtypeStruct((LINE,...  96.2 us
    pallas_call x1, Pallas kernels, fetch_mlp(): pl.pallas_call(fetch_mlp_kernel, out_shape=(jax.ShapeDtypeStruct((LINE, R...  93.5 us
    dot_general x4, matrix products, times_cols(): lax.dot_general(left, right, contract_cols, preferred_element_type=jnp.fl...  37.9 us
    dot_general x4, matrix products, matmul(): return jnp.dot(left, right, preferred_element_type=jnp.float32)  31.7 us
    dot_general x4, matrix products, times_rows(): lax.dot_general(left, right, contract_rows, preferred_element_type=jnp.fl...  31 us
    unnamed x109, local copies, waits for them, and re-layouts  15 us

profile of v1, /device:TPU:8, one launch (start us, length us, event | category | flops | bytes accessed | tf_op | source)
XLA Modules:
  0.0 620.5 jit_solution(2459165683206149381)
XLA Ops:
  6.8 121.0 %fetch_attn.1 = (bf16[32,64,6272]{2,1,0:T(8,128)(2,1)}, bf16[4,64,3072]{2,1,0:T(8,128)(2,1)}) custom-call(bf16[64,6272]{1,0:T(8,128)(2,1)} %copy-done.15, bf16[64,6144]{1,0:T(8,128)(2,1)} %gate_ref.1, bf16[64,6144]{1,0:T(8,128)(2,1)} %up_ref.1), custom_call_target="tpu_custom_call" | custom-call | tf_op jit(solution)/shard_map/fetch_attn/pallas_call | solution.py:206
  130.2 7.1 %fusion.4 = f32[128,4096]{1,0:T(8,128)S(1)} fusion(bf16[2048,6272]{1,0:T(8,128)(2,1)} %bitcast.143, bf16[128,2048]{1,0:T(8,128)(2,1)S(1)} %copy-done.5, f32[2048]{0:T(1024)S(1)} %mul.414, f32[128]{0:T(128)S(1)} %fusion.72), kind=kOutput, calls=%fused_computation.5 | convolution fusion | flops 2148532224 | bytes 19407360 | tf_op jit(solution)/shard_map/dot_general | solution.py:968
  137.4 1.4 copy-done.11
  139.8 1.5 copy.202
  143.8 2.3 fusion.39
  148.4 2.5 fusion.90
  152.1 2.5 convolution_convert_fusion.6
  154.7 4.9 multiply_reduce_fusion.4
  160.7 93.5 %fetch_mlp.1 = (bf16[4,8,64,3072]{3,2,1,0:T(8,128)(2,1)}, bf16[8,192,2048]{2,1,0:T(8,128)(2,1)}, bf16[4,128,2048]{2,1,0:T(8,128)(2,1)}, bf16[4,128,2048]{2,1,0:T(8,128)(2,1)}) custom-call(bf16[4,64,3072]{2,1,0:T(8,128)(2,1)} %get-tuple-element.31.p_ref, bf16[192,2048]{1,0:T(8,128)(2,1)} %d_ref.1, bf16[128,2048]{1,0:T(8,128)(2,1)} %multiply_convert_fusion.2.x_ref, ...), custom_call_target="tpu_custom_call" | custom-call | tf_op jit(solution)/shard_map/fetch_mlp/pallas_call | solution.py:363
  254.2 12.1 %fusion.93 = f32[512,3072]{1,0:T(8,128)} fusion(bf16[512,2048]{1,0:T(8,128)(2,1)} %bitcast.157, bf16[2048,3072]{1,0:T(8,128)(2,1)} %bitcast.151), kind=kOutput, calls=%fused_computation.173 | convolution fusion | flops 6442450944 | bytes 20971520 | tf_op jit(solution)/shard_map/dot_general | solution.py:968
  266.4 8.7 %fusion.12 = (bf16[512,1536]{1,0:T(8,128)(2,1)S(1)}, bf16[512,1536]{1,0:T(8,128)(2,1)}, bf16[512,1536]{1,0:T(8,128)(2,1)S(1)}) fusion(f32[512,3072]{1,0:T(8,128)} %fusion.93, bf16[512,2048]{1,0:T(8,128)(2,1)} %bitcast.159, bf16[1536,2048]{1,0:T(8,128)(2,1)S(1)} %bitcast.156), kind=kOutput, calls=%fused_computation.17 | convolution fusion | flops 3233808384 | bytes 19398656 | tf_op jit(solution)/shard_map/dot_general | solution.py:976
  275.1 7.5 %convolution_convert_fusion.5 = bf16[512,2048]{1,0:T(8,128)(2,1)} fusion(bf16[512,1536]{1,0:T(8,128)(2,1)S(1)} %get-tuple-element.67, bf16[1536,2048]{1,0:T(8,128)(2,1)} %bitcast.155), kind=kOutput, calls=%fused_computation.24 | convolution fusion | flops 3222274048 | bytes 9961472 | tf_op jit(solution)/shard_map/dot_general | solution.py:968
  282.6 9.2 %convolution_convert_fusion.4 = bf16[512,2048]{1,0:T(8,128)(2,1)} fusion(bf16[2048,3072]{1,0:T(8,128)(2,1)S(1)} %bitcast.154, bf16[512,1536]{1,0:T(8,128)(2,1)} %get-tuple-element.66, bf16[512,1536]{1,0:T(8,128)(2,1)S(1)} %get-tuple-element.65), kind=kOutput, calls=%fused_computation.23 | convolution fusion | flops 6449790976 | bytes 17825792 | tf_op jit(solution)/shard_map/dot_general | solution.py:976
  291.8 5.4 convolution_convert_fusion.2
  297.2 10.0 %convolution_convert_fusion.1 = bf16[2048,3072]{1,0:T(8,128)(2,1)} fusion(bf16[512,2048]{1,0:T(8,128)(2,1)S(1)} %bitcast.158, bf16[512,1536]{1,0:T(8,128)(2,1)S(1)} %copy-done.43, bf16[512,1536]{1,0:T(8,128)(2,1)S(1)} %get-tuple-element.65), kind=kOutput, calls=%fused_computation.7 | convolution fusion | flops 6455033856 | bytes 17825792 | tf_op jit(solution)/shard_map/dot_general | solution.py:972
  307.2 96.2 %reduce_mlp.1 = (bf16[4,64,3072]{2,1,0:T(8,128)(2,1)}, f32[192,2048]{1,0:T(8,128)}, f32[128,2048]{1,0:T(8,128)}, f32[128,2048]{1,0:T(8,128)}) custom-call(bf16[4,8,64,3072]{3,2,1,0:T(8,128)(2,1)} %bitcast.122, bf16[8,192,2048]{2,1,0:T(8,128)(2,1)} %bitcast.123, bf16[4,128,2048]{2,1,0:T(8,128)(2,1)} %bitcast.133, bf16[4,128,2048]{2,1,0:T(8,128)(2,1)} %bitcast.132), custom_call_target="tpu_custom_call" | custom-call | tf_op jit(solution)/shard_map/reduce_mlp/pallas_call | solution.py:615
  403.4 1.8 multiply_reduce_fusion
  405.8 3.2 fusion.33
  409.0 7.5 %fusion.17 = bf16[128,2048]{1,0:T(8,128)(2,1)} fusion(bf16[2048,6272]{1,0:T(8,128)(2,1)} %bitcast.145, f32[128,2048]{1,0:T(8,128)S(1)} %get-tuple-element.70), kind=kOutput, calls=%fused_computation.26 | convolution fusion | flops 1074266112 | bytes 9961472 | tf_op jit(solution)/shard_map/dot_general | solution.py:976
  416.5 1.3 copy.205
  417.8 1.3 convolution_bitcast_fusion
  419.1 3.7 fusion.46
  422.8 1.4 bitcast_multiply_fusion
  426.0 3.9 broadcast_multiply_fusion
  432.4 2.6 fusion.30
  435.1 12.6 %fusion.32 = (f32[2048]{0:T(1024)S(1)}, f32[128]{0:T(128)S(1)}, f32[128,2048]{1,0:T(8,128)}) fusion(bf16[128,2048]{1,0:T(8,128)(2,1)S(1)} %copy-done.6, f32[128]{0:T(128)S(1)} %copy-done.29, f32[2048]{0:T(1024)S(1)} %mul.414, bf16[2048,6272]{1,0:T(8,128)(2,1)} %bitcast.146, bf16[128,1024]{0,1:T(8,128)(2,1)} %bitcast.140, ...), kind=kOutput, calls=%fused_computation.51 | convolution fusion | flops 2152462336 | bytes 19416064 | tf_op jit(solution)/shard_map/dot_general | solution.py:976
  448.3 5.8 convolution_convert_fusion.3
  454.1 9.8 %convolution_convert_fusion = bf16[2048,4096]{1,0:T(8,128)(2,1)} fusion(bf16[128,1024]{0,1:T(8,128)(2,1)S(1)} %bitcast.141, bf16[128,1024]{0,1:T(8,128)(2,1)S(1)} %bitcast.137, bf16[128,2048]{0,1:T(8,128)(2,1)S(1)} %bitcast.129, bf16[128,2048]{1,0:T(8,128)(2,1)S(1)} %copy-done.6, f32[2048]{0:T(1024)S(1)} %mul.414, f32[128]{0:T(128)S(1)} %copy-done.29), kind=kOutput, calls=%fused_computation.2 | convolution fusion | flops 2160066560 | bytes 18358784 | tf_op jit(solution)/shard_map/dot_general | solution.py:972
  463.9 144.4 %reduce_attn.1 = (f32[64,2048]{1,0:T(8,128)}, f32[64,1024]{1,0:T(8,128)}, f32[64,1024]{1,0:T(8,128)}, f32[64,2048]{1,0:T(8,128)}, f32[64,6144]{1,0:T(8,128)}, /*index=5*/f32[64,6144]{1,0:T(8,128)}, f32[40,128]{1,0:T(8,128)}) custom-call(bf16[32,64,4096]{2,1,0:T(8,128)(2,1)} %bitcast.118, bf16[32,64,2048]{2,1,0:T(8,128)(2,1)} %bitcast.119, ...), custom_call_target="tpu_custom_call" | custom-call | tf_op jit(solution)/shard_map/reduce_attn/pallas_call | solution.py:875
  608.4 1.4 fusion.89
  609.8 1.3 fusion.88
  611.1 2.8 fusion.35
  (161 shorter events, 28.5 us)
Async XLA Ops:
  5.9 124.1 %copy-start.5 = (bf16[128,2048]{1,0:T(8,128)(2,1)S(1)}, bf16[128,2048]{1,0:T(8,128)(2,1)}, u32[]{:S(2)}) copy-start(bf16[128,2048]{1,0:T(8,128)(2,1)} %param.15) | copy-start | bytes 1572868
  130.2 7.2 %copy-start.32 = (f32[128]{0:T(128)}, f32[128]{0:T(128)S(1)}, u32[]{:S(2)}) copy-start(f32[128]{0:T(128)S(1)} %fusion.36) | copy-start | bytes 1540
  130.2 7.2 %copy-start.28 = (f32[128]{0:T(128)}, f32[128]{0:T(128)S(1)}, u32[]{:S(2)}) copy-start(f32[128]{0:T(128)S(1)} %fusion.72) | copy-start | bytes 1540
  141.8 4.3 copy-start.24
  147.8 4.2 copy-start
  148.3 6.4 %copy-start.22 = (bf16[128,8,128,1]{0,2,3,1:T(8,128)(2,1)}, bf16[128,8,128,1]{0,2,3,1:T(8,128)(2,1)S(1)}, u32[]{:S(2)}) copy-start(bf16[128,8,128,1]{0,2,3,1:T(8,128)(2,1)S(1)} %fusion.53) | copy-start | bytes 786436
  159.6 106.7 %copy-start.4 = (f32[128,2048]{1,0:T(8,128)}, f32[128,2048]{1,0:T(8,128)S(1)}, u32[]{:S(2)}) copy-start(f32[128,2048]{1,0:T(8,128)S(1)} %get-tuple-element.87) | copy-start | bytes 3145732
  159.6 106.7 %copy-start.38 = (f32[128]{0:T(128)}, f32[128]{0:T(128)S(1)}, u32[]{:S(2)}) copy-start(f32[128]{0:T(128)S(1)} %get-tuple-element.86) | copy-start | bytes 1540
  159.6 106.7 %copy-start.30 = (f32[128]{0:T(128)}, f32[128]{0:T(128)S(1)}, u32[]{:S(2)}) copy-start(f32[128]{0:T(128)S(1)} %fusion.73) | copy-start | bytes 1540
  254.2 12.1 %copy-start.35 = (bf16[8,192,2048]{2,1,0:T(8,128)(2,1)S(1)}, bf16[8,192,2048]{2,1,0:T(8,128)(2,1)}, u32[]{:S(2)}) copy-start(bf16[8,192,2048]{2,1,0:T(8,128)(2,1)} %get-tuple-element.34) | copy-start | bytes 18874372
  266.4 16.2 %slice-start = ((s8[12582912]{0:T(1024)(128)(4,1)}), s8[4194304]{0:T(1024)(128)(4,1)S(1)}, s32[]{:S(2)}) async-start(s8[12582912]{0:T(1024)(128)(4,1)} %bitcast.152), calls=%async_computation | async-start | bytes 8388608
  266.4 16.2 %slice-start.1 = ((s8[12582912]{0:T(1024)(128)(4,1)}), s8[4194304]{0:T(1024)(128)(4,1)S(1)}, s32[]{:S(2)}) async-start(s8[12582912]{0:T(1024)(128)(4,1)} %bitcast.152), calls=%async_computation.1 | async-start | bytes 8388608
  275.1 7.5 %slice-start.2 = ((s8[12582912]{0:T(1024)(128)(4,1)}), s8[4194304]{0:T(1024)(128)(4,1)S(1)}, s32[]{:S(2)}) async-start(s8[12582912]{0:T(1024)(128)(4,1)} %bitcast.152), calls=%async_computation.2 | async-start | bytes 8388608
  282.6 9.2 %copy-start.37 = (bf16[4,128,2048]{2,1,0:T(8,128)(2,1)S(1)}, bf16[4,128,2048]{2,1,0:T(8,128)(2,1)}, u32[]{:S(2)}) copy-start(bf16[4,128,2048]{2,1,0:T(8,128)(2,1)} %get-tuple-element.33) | copy-start | bytes 6291460
  291.8 5.4 copy-start.36
  291.8 5.4 copy-start.43
  409.0 39.3 %copy-start.2 = (f32[128,2048]{1,0:T(8,128)}, f32[128,2048]{1,0:T(8,128)S(1)}, u32[]{:S(2)}) copy-start(f32[128,2048]{1,0:T(8,128)S(1)} %get-tuple-element.70) | copy-start | bytes 3145732
  409.0 10.0 %copy-start.23 = (bf16[128,8,128,1]{0,2,3,1:T(8,128)(2,1)S(1)}, bf16[128,8,128,1]{0,2,3,1:T(8,128)(2,1)}, u32[]{:S(2)}) copy-start(bf16[128,8,128,1]{0,2,3,1:T(8,128)(2,1)} %copy-done.22) | copy-start | bytes 786436
  409.0 10.0 %copy-start.40 = (f32[8,2,128]{2,1,0:T(2,128)S(1)}, f32[8,2,128]{2,1,0:T(2,128)}, u32[]{:S(2)}) copy-start(f32[8,2,128]{2,1,0:T(2,128)} %copy-done.39) | copy-start | bytes 24580
  417.8 5.0 copy-start.8
  426.0 5.0 copy-start.1
  426.0 5.0 copy-start.27
  435.1 13.2 %copy-start.16 = (bf16[8,128,2,128]{3,1,2,0:T(8,128)(2,1)S(1)}, bf16[8,128,2,128]{3,1,2,0:T(8,128)(2,1)}, u32[]{:S(2)}) copy-start(bf16[8,128,2,128]{3,1,2,0:T(8,128)(2,1)} %convolution_convert_fusion.6) | copy-start | bytes 1572868
  448.3 5.8 copy-start.19
  463.9 147.1 %copy-start.33 = (f32[128]{0:T(128)S(1)}, f32[128]{0:T(128)}, u32[]{:S(2)}) copy-start(f32[128]{0:T(128)} %copy-done.32) | copy-start | bytes 1540
  463.9 147.1 %copy-start.3 = (f32[128,2048]{1,0:T(8,128)S(1)}, f32[128,2048]{1,0:T(8,128)}, u32[]{:S(2)}) copy-start(f32[128,2048]{1,0:T(8,128)} %copy-done.2) | copy-start | bytes 3145732
  608.3 5.5 copy-start.18
  608.3 6.3 %copy-start.21 = (f32[64,1024]{1,0:T(8,128)S(1)}, f32[64,1024]{1,0:T(8,128)}, u32[]{:S(2)}) copy-start(f32[64,1024]{1,0:T(8,128)} %get-tuple-element.114) | copy-start | bytes 786436
  608.3 7.0 %copy-start.20 = (f32[64,1024]{1,0:T(8,128)S(1)}, f32[64,1024]{1,0:T(8,128)}, u32[]{:S(2)}) copy-start(f32[64,1024]{1,0:T(8,128)} %get-tuple-element.115) | copy-start | bytes 786436
  608.3 7.7 %copy-start.17 = (f32[64,2048]{1,0:T(8,128)S(1)}, f32[64,2048]{1,0:T(8,128)}, u32[]{:S(2)}) copy-start(f32[64,2048]{1,0:T(8,128)} %get-tuple-element.116) | copy-start | bytes 1572868
  611.1 5.8 copy-start.14
  613.8 4.2 copy-start.13
  (15 other events, 34.4 us)

commit v2 on v1

--- a/solution.py
+++ b/solution.py
@@ -10,6 +10,7 @@
 H = 16
 KVH = 8
 HD = 128
+CAP = 128
 LINE = 4
 RING = 8
 MESH = pl.DeviceIdType.MESH
@@ -18,6 +19,11 @@
 DMA = pltpu.SemaphoreType.DMA
 bf16 = jnp.bfloat16
 f32 = jnp.float32
+epsilon = 1e-06
+rope_base = 1000000.0
+masked_score = -1e30
+contract_rows = (((0,), (0,)), ((), ()))
+contract_cols = (((1,), (1,)), ((), ()))
 
 
 def where_am_i():
@@ -62,15 +68,89 @@
             body(step)
 
 
-def fetch_attn_kernel(
-    w_ref, gate_ref, up_ref, w_out, p_out,
-    w_tmp, p_tmp, local, up_s, down_s, first_s, second_s, sib_s, recv, ex_send, ex_recv,
+def lane_sum(x):
+    return jnp.sum(x, axis=-1, keepdims=True)
+
+
+def token_places(len_row, dev_row, len_col, dev_col, me):
+    seqs = len_row.shape[1]
+    counts_row = jnp.where(dev_row == me, len_row, 0).astype(f32)
+    counts_col = jnp.where(dev_col == me, len_col, 0).astype(f32)
+    up = lax.broadcasted_iota(jnp.int32, (seqs, seqs), 0)
+    across = lax.broadcasted_iota(jnp.int32, (seqs, seqs), 1)
+    starts_row = jnp.sum(jnp.where(up < across, counts_col, 0.0), axis=0, keepdims=True)
+    starts_col = lane_sum(jnp.where(across < up, counts_row, 0.0))
+
+    def within(places, starts, counts):
+        return (places >= starts) & (places < starts + counts)
+
+    places = lax.broadcasted_iota(jnp.int32, (CAP, seqs), 0).astype(f32)
+    labels = lax.broadcasted_iota(jnp.int32, (CAP, seqs), 1).astype(f32)
+    inside = within(places, starts_row, counts_row)
+    segment_col = lane_sum(jnp.where(inside, labels + 1.0, 0.0)) - 1.0
+    position = lane_sum(jnp.where(inside, places - starts_row, 0.0))
+    places = lax.broadcasted_iota(jnp.int32, (seqs, CAP), 1).astype(f32)
+    labels = lax.broadcasted_iota(jnp.int32, (seqs, CAP), 0).astype(f32)
+    inside = within(places, starts_col, counts_col)
+    segment_row = jnp.sum(jnp.where(inside, labels + 1.0, 0.0), axis=0, keepdims=True) - 1.0
+    return segment_col, segment_row, position
+
+
+def allowed_bias(segment_col, segment_row):
+    t = lax.broadcasted_iota(jnp.int32, (CAP, CAP), 0)
+    u = lax.broadcasted_iota(jnp.int32, (CAP, CAP), 1)
+    same = (segment_col == segment_row) & (segment_col >= 0.0)
+    return jnp.where((t == u) | ((u < t) & same), 0.0, masked_score)
+
+
+def half_turn(v):
+    lane = lax.broadcasted_iota(jnp.int32, v.shape, v.ndim - 1)
+    turned = pltpu.roll(v, HD // 2, v.ndim - 1)
+    return jnp.where(lane < HD // 2, -turned, turned)
+
+
+def rms_scale(v):
+    return lax.rsqrt(jnp.mean(v * v, axis=-1, keepdims=True) + epsilon)
+
+
+def forward_kernel(
+    x_ref, cot_ref, len_row, dev_row, len_col, dev_col, freq_ref, gain_ref,
+    wq_ref, wk_ref, wv_ref, wo_ref, gate_ref, up_ref, wd_ref,
+    w_out, gu_out, d_out, tok_out, cot_out,
+    middle_out, normed_out, raw_out, q_out, k_out, v_out, mixed_out, gains_out,
+    w_tmp, p_tmp, d_tmp, cot_tmp, second_tmp, chunk, ow_all, gain_tmp, cos_tmp, sin_tmp, bias_tmp,
+    local, up_s, down_s, first_s, second_s, sib_s, recv, ex_send, ex_recv,
+    m_first_s, m_second_s, m_sib_s, m_recv, line_up, line_down, line_r, w_load, o_load, g_load,
 ):
     me, z, first, second, sibling = where_am_i()
-    greet(line_peers(me) + [first, second, sibling])
     col, fcol, scol = me % RING, first % RING, second % RING
     sfcol = (second + first - me) % RING
-    width = p_tmp.shape[1] // 2
+    width = p_tmp.shape[2] // 2
+    rows = w_tmp.shape[0]
+    qkv_width = raw_out.shape[1]
+    attn_width = qkv_width + wo_ref.shape[1]
+    last = LINE - 1
+    pieces = LINE + 1
+
+    w_in = []
+    lo = 0
+    for i, ref in enumerate((wq_ref, wk_ref, wv_ref, wo_ref, gain_ref)):
+        at = pl.ds(lo, ref.shape[1])
+        w_in.append(pltpu.make_async_copy(ref, w_tmp.at[:, at], local.at[i]))
+        lo += ref.shape[1]
+    p_in = [
+        pltpu.make_async_copy(
+            ref.at[:, pl.ds(pl.multiple_of(z * width, width), width)],
+            p_tmp.at[z, :, pl.ds(which * width, width)],
+            local.at[5 + which],
+        )
+        for which, ref in enumerate((gate_ref, up_ref))
+    ]
+    d_in = pltpu.make_async_copy(wd_ref, d_tmp, local.at[7])
+    cot_in = pltpu.make_async_copy(cot_ref, cot_tmp, local.at[8])
+    for copy in w_in + p_in + [d_in, cot_in]:
+        copy.start()
+    greet(line_peers(me) + [first, second, sibling])
 
     def send(src, shard, sems, device):
         return remote(src, w_out.at[shard], sems.at[shard], recv.at[shard], device)
@@ -81,35 +161,56 @@
     def exchange(k, which):
         peer_z = lax.rem(z + k, LINE)
         src = (gate_ref, up_ref)[which].at[:, pl.ds(pl.multiple_of(peer_z * width, width), width)]
-        dst = p_out.at[z, :, pl.ds(which * width, width)]
+        dst = p_tmp.at[z, :, pl.ds(which * width, width)]
         return remote(src, dst, ex_send.at[k, which], ex_recv.at[k, which], col + RING * peer_z)
 
-    @pl.when(z < LINE - 1)
+    def line_send(src, which, shard, sems, device):
+        landing = (tok_out, cot_out)[which].at[shard]
+        return remote(src, landing, sems.at[which, shard], line_r.at[which, shard], device)
+
+    def line_own(which, src):
+        @pl.when(z < last)
+        def _():
+            line_send(src, which, z, line_up, me + RING).start()
+
+        @pl.when(z > 0)
+        def _():
+            line_send(src, which, z, line_down, me - RING).start()
+
+    def line_relay(which, k):
+        def body(step):
+            shard = z + step
+            src = (tok_out, cot_out)[which].at[shard]
+            line_send(src, which, shard, line_up, second).wait_recv()
+            if step < 0:
+
+                @pl.when(z < last)
+                def _():
+                    line_send(src, which, shard, line_up, me + RING).start()
+            else:
+
+                @pl.when(z > 0)
+                def _():
+                    line_send(src, which, shard, line_down, me - RING).start()
+
+        on_line(z, k, body)
+
+    for copy in w_in:
+        copy.wait()
+
+    @pl.when(z < last)
     def _():
-        send(w_ref, me, up_s, me + RING).start()
+        send(w_tmp, me, up_s, me + RING).start()
 
     @pl.when(z > 0)
     def _():
-        send(w_ref, me, down_s, me - RING).start()
-
-    send(w_ref, me, first_s, first).start()
-    send(w_ref, me, second_s, second).start()
-    send(w_ref, me, sib_s, sibling).start()
-    w_in = pltpu.make_async_copy(w_ref, w_tmp, local.at[0])
-    w_in.start()
-    p_in = [
-        pltpu.make_async_copy(
-            ref.at[:, pl.ds(pl.multiple_of(z * width, width), width)],
-            p_tmp.at[:, pl.ds(which * width, width)],
-            local.at[1 + which],
-        )
-        for which, ref in enumerate((gate_ref, up_ref))
-    ]
-    for copy in p_in:
-        copy.start()
-    for k in range(1, LINE):
-        for which in range(2):
-            exchange(k, which).start()
+        send(w_tmp, me, down_s, me - RING).start()
+
+    send(w_tmp, me, first_s, first).start()
+    send(w_tmp, me, second_s, second).start()
+    send(w_tmp, me, sib_s, sibling).start()
+    w_back = pltpu.make_async_copy(w_tmp, w_out.at[me], local.at[9])
+    w_back.start()
 
     def own(k):
         def body(step):
@@ -118,7 +219,7 @@
             arrived(shard)
             if step < 0:
 
-                @pl.when(z < LINE - 1)
+                @pl.when(z < last)
                 def _():
                     send(src, shard, up_s, me + RING).start()
             else:
@@ -144,77 +245,295 @@
 
         on_line(z, k, body)
 
+    segment_col, segment_row, position = token_places(
+        len_row[...], dev_row[...], len_col[...], dev_col[...], me
+    )
+    bias_tmp[...] = allowed_bias(segment_col, segment_row)
+    angles = position * freq_ref[...]
+    cos_tmp[...] = jnp.cos(angles)
+    sin_tmp[...] = jnp.sin(angles)
+    x_scale = rms_scale(x_ref[...].astype(f32))
+    raw_out[...] = jnp.zeros_like(raw_out)
+
+    def load_group(step):
+        zz = z + step
+        part = w_out.at[pl.ds(RING * zz, RING)]
+        return (
+            pltpu.make_async_copy(part.at[:, :, pl.ds(0, qkv_width)], chunk, w_load),
+            pltpu.make_async_copy(
+                part.at[:, :, pl.ds(qkv_width, attn_width - qkv_width)],
+                ow_all.at[pl.ds(RING * zz, RING)],
+                o_load.at[zz],
+            ),
+            pltpu.make_async_copy(
+                part.at[:, pl.ds(0, 16), pl.ds(attn_width, 128)], gain_tmp.at[zz], g_load
+            ),
+        )
+
+    def group(k):
+        def body(step):
+            zz = z + step
+            for i in range(RING // 2):
+                arrived(RING * zz + 2 * i + sibling % 2)
+            copies = load_group(step)
+            for copy in copies:
+                copy.start()
+            copies[2].wait()
+            span = RING * rows
+            for pair in range(RING // 2):
+                at = pl.ds(pl.multiple_of(zz * span + pair * 128, 128), 128)
+                both = gain_tmp[zz, 2 * pair].astype(f32) + gain_tmp[zz, 2 * pair + 1].astype(f32)
+                gains_out[0:2, at] = both[0:2]
+                piece = x_ref[:, at].astype(f32) * x_scale * both[0:1]
+                normed_out[:, at] = piece.astype(bf16)
+            copies[0].wait()
+            left = normed_out[:, pl.ds(pl.multiple_of(zz * span, span), span)]
+
+            def tile(i, carry):
+                at = pl.ds(pl.multiple_of(i * 512, 512), 512)
+                right = chunk[:, :, at].reshape(span, 512)
+                raw_out[:, at] += jnp.dot(left, right, preferred_element_type=f32)
+                return carry
+
+            lax.fori_loop(0, qkv_width // 512, tile, 0)
+
+        on_line(z, k, body)
+
     own(1)
     other(fcol, 0, True)
     own(2)
     other(fcol, 1, True)
     other(scol, 0, False)
-    w_in.wait()
-    w_back = pltpu.make_async_copy(w_tmp, w_out.at[me], local.at[3])
-    w_back.start()
-    for copy in p_in:
-        copy.wait()
-    p_back = pltpu.make_async_copy(p_tmp, p_out.at[z], local.at[4])
-    p_back.start()
+    for k in range(1, LINE):
+        for which in range(2):
+            exchange(k, which).start()
+    cot_in.wait()
+    line_own(1, cot_tmp)
+    cot_back = pltpu.make_async_copy(cot_tmp, cot_out.at[z], local.at[10])
+    cot_back.start()
     own(3)
     other(fcol, 2, True)
     other(scol, 1, False)
     other(sfcol, 0, False)
+    w_back.wait()
+    group(0)
     other(fcol, 3, True)
     other(scol, 2, False)
     other(sfcol, 1, False)
+    group(1)
+
+    for copy in p_in + [d_in]:
+        copy.wait()
+    for k in range(1, LINE):
+        for which in range(2):
+            src_z = lax.rem(z + LINE - k, LINE)
+            landed = p_tmp.at[src_z, :, pl.ds(which * width, width)]
+            remote(landed, landed, ex_send.at[k, which], ex_recv.at[k, which], second).wait_recv()
+
+    def spot(piece, shard):
+        return gu_out.at[piece, shard] if piece < LINE else d_out.at[shard]
+
+    def source(piece):
+        return p_tmp.at[piece] if piece < LINE else d_tmp
+
+    def m_send(src, piece, shard, sems, device):
+        return remote(
+            src, spot(piece, shard), sems.at[piece, shard], m_recv.at[piece, shard], device
+        )
+
+    def m_arrived(piece, shard):
+        m_send(spot(piece, shard), piece, shard, m_sib_s, sibling).wait_recv()
+
+    for piece in range(pieces):
+        m_send(source(piece), piece, col, m_first_s, first).start()
+        m_send(source(piece), piece, col, m_second_s, second).start()
+        m_send(source(piece), piece, col, m_sib_s, sibling).start()
+    backs = [
+        pltpu.make_async_copy(p_tmp, gu_out.at[:, col], local.at[11]),
+        pltpu.make_async_copy(d_tmp, d_out.at[col], local.at[12]),
+    ]
+    for copy in backs:
+        copy.start()
+    line_relay(1, 1)
     other(scol, 3, False)
     other(sfcol, 2, False)
+    group(2)
     other(sfcol, 3, False)
-
-    def from_sibling(i, carry):
-        arrived(2 * i + sibling % 2)
+    group(3)
+    line_relay(1, 2)
+
+    small = jnp.zeros((16, 128), f32)
+    for zz in range(LINE):
+        for i in range(RING):
+            small = small + gain_tmp[zz, i].astype(f32)
+    q_gain, k_gain = small[2:3], small[3:4]
+    gains_out[2:4, 0:128] = small[2:4]
+    cosine, sine, bias = cos_tmp[...], sin_tmp[...], bias_tmp[...]
+
+    def turned(v, gain):
+        v = v * rms_scale(v) * gain
+        return (v * cosine + half_turn(v) * sine).astype(bf16)
+
+    kv0 = H * HD
+    v0 = kv0 + KVH * HD
+
+    def head(g, carry):
+        at = pl.ds(pl.multiple_of(g * HD, HD), HD)
+        qa = pl.ds(pl.multiple_of(g * 2 * HD, 2 * HD), HD)
+        qb = pl.ds(pl.multiple_of(g * 2 * HD + HD, HD), HD)
+        key = turned(raw_out[:, pl.ds(pl.multiple_of(kv0 + g * HD, HD), HD)], k_gain)
+        value = raw_out[:, pl.ds(pl.multiple_of(v0 + g * HD, HD), HD)].astype(bf16)
+        k_out[:, at] = key
+        v_out[:, at] = value
+        query_a = turned(raw_out[:, qa], q_gain)
+        query_b = turned(raw_out[:, qb], q_gain)
+        q_out[:, qa] = query_a
+        q_out[:, qb] = query_b
+        for query, where in ((query_a, qa), (query_b, qb)):
+            scores = lax.dot_general(query, key, contract_cols, preferred_element_type=f32)
+            logits = scores * (HD ** (-0.5)) + bias
+            exponent = jnp.exp(logits - jnp.max(logits, axis=-1, keepdims=True))
+            weights = (exponent / lane_sum(exponent)).astype(bf16)
+            mixed = jnp.dot(weights, value, preferred_element_type=f32)
+            mixed_out[:, where] = mixed.astype(bf16)
         return carry
 
-    lax.fori_loop(0, RING * LINE // 2, from_sibling, 0)
-    w_back.wait()
-    p_back.wait()
+    lax.fori_loop(0, KVH, head, 0)
+    for zz in range(LINE):
+        pltpu.make_async_copy(
+            w_out.at[pl.ds(RING * zz, RING), :, pl.ds(qkv_width, attn_width - qkv_width)],
+            ow_all.at[pl.ds(RING * zz, RING)],
+            o_load.at[zz],
+        ).wait()
+    mixed = mixed_out[...]
+
+    def out_tile(i, total):
+        at = pl.ds(pl.multiple_of(i * 512, 512), 512)
+        right = ow_all[:, :, at].reshape(mixed.shape[1], 512)
+        middle = x_ref[:, at].astype(f32) + jnp.dot(mixed, right, preferred_element_type=f32)
+        middle_out[:, at] = middle
+        return total + lane_sum(middle * middle)
+
+    tiles = middle_out.shape[1] // 512
+    total = lax.fori_loop(0, tiles, out_tile, jnp.zeros((CAP, 1), f32))
+    scale = lax.rsqrt(total / middle_out.shape[1] + epsilon)
+
+    def norm_tile(i, carry):
+        at = pl.ds(pl.multiple_of(i * 512, 512), 512)
+        second_tmp[:, at] = (middle_out[:, at] * scale * gains_out[1:2, at]).astype(bf16)
+        return carry
+
+    lax.fori_loop(0, tiles, norm_tile, 0)
+
+    def m_other(piece, shard, onward):
+        m_arrived(piece, shard)
+        if onward:
+            m_send(spot(piece, shard), piece, shard, m_second_s, second).start()
+        m_send(spot(piece, shard), piece, shard, m_sib_s, sibling).start()
+
+    m_other(0, fcol, True)
+    line_own(0, second_tmp)
+    tok_back = pltpu.make_async_copy(second_tmp, tok_out.at[z], local.at[13])
+    tok_back.start()
+    m_other(0, scol, False)
+    m_other(1, fcol, True)
+    m_other(1, scol, False)
+    line_relay(1, 3)
+    m_other(2, fcol, True)
+    m_other(2, scol, False)
+    line_relay(0, 1)
+    m_other(3, fcol, True)
+    m_other(3, scol, False)
+    m_other(4, fcol, True)
+    line_relay(0, 2)
+    m_other(4, scol, False)
+    m_other(0, sfcol, False)
+    m_other(1, sfcol, False)
+    line_relay(0, 3)
+    for piece in range(2, pieces):
+        m_other(piece, sfcol, False)
+    for piece in range(pieces):
+        for k in range(RING // 2):
+            m_arrived(piece, 2 * k + sibling % 2)
+
+    cot_back.wait()
+    tok_back.wait()
+    for copy in backs:
+        copy.wait()
     for k in range(1, LINE):
         for which in range(2):
             exchange(k, which).wait_send()
-            src_z = lax.rem(z + LINE - k, LINE)
-            landed = p_out.at[src_z, :, pl.ds(which * width, width)]
-            remote(
-                landed, landed, ex_send.at[k, which], ex_recv.at[k, which], col + RING * src_z
-            ).wait_recv()
     for k in range(LINE):
 
-        @pl.when((z < LINE - 1) & (k <= z))
+        @pl.when((z < last) & (k <= z))
         def _(k=k):
-            send(w_ref, col + RING * k, up_s, me + RING).wait_send()
+            send(w_tmp, col + RING * k, up_s, me + RING).wait_send()
+            for which in range(2):
+                line_send(cot_tmp, which, k, line_up, me + RING).wait_send()
 
         @pl.when((z > 0) & (k >= z))
         def _(k=k):
-            send(w_ref, col + RING * k, down_s, me - RING).wait_send()
-
-        send(w_ref, col + RING * k, first_s, first).wait_send()
-        send(w_ref, col + RING * k, second_s, second).wait_send()
-        send(w_ref, fcol + RING * k, second_s, second).wait_send()
+            send(w_tmp, col + RING * k, down_s, me - RING).wait_send()
+            for which in range(2):
+                line_send(cot_tmp, which, k, line_down, me - RING).wait_send()
+
+        send(w_tmp, col + RING * k, first_s, first).wait_send()
+        send(w_tmp, col + RING * k, second_s, second).wait_send()
+        send(w_tmp, fcol + RING * k, second_s, second).wait_send()
         for base in (col, fcol, scol, sfcol):
-            send(w_ref, base + RING * k, sib_s, sibling).wait_send()
-
-
-def fetch_attn(w, gate, up):
-    rows, cols = w.shape
+            send(w_tmp, base + RING * k, sib_s, sibling).wait_send()
+    for piece in range(pieces):
+        src = source(piece)
+        m_send(src, piece, col, m_first_s, first).wait_send()
+        m_send(src, piece, col, m_second_s, second).wait_send()
+        m_send(src, piece, fcol, m_second_s, second).wait_send()
+        for base in (col, fcol, scol, sfcol):
+            m_send(src, piece, base, m_sib_s, sibling).wait_send()
+
+
+def forward(hidden_in, out_grad, seq_lengths, seq_device, gains, wq, wk, wv, wo, gate, up, wd):
+    slots, dim = hidden_in.shape
+    rows = wq.shape[0]
+    n = RING * LINE
     width = gate.shape[1] // LINE
-    n = RING * LINE
+    qkv_width = wq.shape[1] + wk.shape[1] + wv.shape[1]
+    wide = qkv_width + wo.shape[1] + gains.shape[1]
+    pieces = LINE + 1
+    half = jnp.power(rope_base, -2.0 * jnp.arange(HD // 2, dtype=f32) / HD)
+    freqs = jnp.concatenate([half, half])[None, :]
+    S = jax.ShapeDtypeStruct
     return pl.pallas_call(
-        fetch_attn_kernel,
+        forward_kernel,
         out_shape=(
-            jax.ShapeDtypeStruct((n, rows, cols), bf16),
-            jax.ShapeDtypeStruct((LINE, rows, 2 * width), bf16),
+            S((n, rows, wide), bf16),
+            S((LINE, RING, rows, 2 * width), bf16),
+            S((RING,) + wd.shape, bf16),
+            S((LINE, slots, dim), bf16),
+            S((LINE, slots, dim), bf16),
+            S((slots, dim), f32),
+            S((slots, dim), bf16),
+            S((slots, qkv_width), f32),
+            S((slots, H * HD), bf16),
+            S((slots, KVH * HD), bf16),
+            S((slots, KVH * HD), bf16),
+            S((slots, H * HD), bf16),
+            S((8, dim), f32),
         ),
-        in_specs=[ANY] * 3,
-        out_specs=(ANY, ANY),
+        in_specs=[VMEM, ANY] + [VMEM] * 5 + [ANY] * 8,
+        out_specs=(ANY,) * 5 + (VMEM,) * 8,
         scratch_shapes=[
-            pltpu.VMEM((rows, cols), bf16),
-            pltpu.VMEM((rows, 2 * width), bf16),
-            DMA((5,)),
+            pltpu.VMEM((rows, wide), bf16),
+            pltpu.VMEM((LINE, rows, 2 * width), bf16),
+            pltpu.VMEM(wd.shape, bf16),
+            pltpu.VMEM((slots, dim), bf16),
+            pltpu.VMEM((slots, dim), bf16),
+            pltpu.VMEM((RING, rows, qkv_width), bf16),
+            pltpu.VMEM((n, rows, wo.shape[1]), bf16),
+            pltpu.VMEM((LINE, RING, 16, 128), bf16),
+            pltpu.VMEM((slots, HD), f32),
+            pltpu.VMEM((slots, HD), f32),
+            pltpu.VMEM((slots, slots), f32),
+            DMA((14,)),
             DMA((n,)),
             DMA((n,)),
             DMA((n,)),
@@ -223,170 +542,25 @@
             DMA((n,)),
             DMA((LINE, 2)),
             DMA((LINE, 2)),
-        ],
-        compiler_params=pltpu.CompilerParams(collective_id=0, has_side_effects=True),
-        name="fetch_attn",
-    )(w, gate, up)
-
-
-def fetch_mlp_kernel(
-    p_ref, d_ref, x_ref, g_ref, gu_out, d_out, x_out, g_out,
-    p_tmp, d_tmp, x_tmp, g_tmp, local, up_s, down_s, line_r, first_s, second_s, sib_s, recv,
-):
-    me, z, first, second, sibling = where_am_i()
-    greet(line_peers(me) + [first, second, sibling])
-    col, fcol, scol = me % RING, first % RING, second % RING
-    sfcol = (second + first - me) % RING
-    pieces = LINE + 1
-
-    def spot(piece, shard):
-        return gu_out.at[piece, shard] if piece < LINE else d_out.at[shard]
-
-    def source(piece):
-        return p_ref.at[piece] if piece < LINE else d_ref
-
-    def send(src, piece, shard, sems, device):
-        return remote(
-            src, spot(piece, shard), sems.at[piece, shard], recv.at[piece, shard], device
-        )
-
-    def arrived(piece, shard):
-        send(spot(piece, shard), piece, shard, sib_s, sibling).wait_recv()
-
-    tokens = ((x_ref, x_out), (g_ref, g_out))
-
-    def line_send(src, which, shard, sems, device):
-        return remote(
-            src,
-            tokens[which][1].at[shard],
-            sems.at[which, shard],
-            line_r.at[which, shard],
-            device,
-        )
-
-    for which in range(2):
-
-        @pl.when(z < LINE - 1)
-        def _(which=which):
-            line_send(tokens[which][0], which, z, up_s, me + RING).start()
-
-        @pl.when(z > 0)
-        def _(which=which):
-            line_send(tokens[which][0], which, z, down_s, me - RING).start()
-
-    for piece in range(pieces):
-        send(source(piece), piece, col, first_s, first).start()
-        send(source(piece), piece, col, second_s, second).start()
-        send(source(piece), piece, col, sib_s, sibling).start()
-    moves = (
-        (p_ref, p_tmp, gu_out.at[:, col]),
-        (d_ref, d_tmp, d_out.at[col]),
-        (x_ref, x_tmp, x_out.at[z]),
-        (g_ref, g_tmp, g_out.at[z]),
-    )
-    ins = [pltpu.make_async_copy(m[0], m[1], local.at[i]) for i, m in enumerate(moves)]
-    outs = [pltpu.make_async_copy(m[1], m[2], local.at[4 + i]) for i, m in enumerate(moves)]
-    for copy in ins:
-        copy.start()
-
-    def along(k):
-        def body(step):
-            shard = z + step
-            for which in range(2):
-                src = tokens[which][1].at[shard]
-                line_send(src, which, shard, up_s, second).wait_recv()
-                if step < 0:
-
-                    @pl.when(z < LINE - 1)
-                    def _(which=which, src=src):
-                        line_send(src, which, shard, up_s, me + RING).start()
-                else:
-
-                    @pl.when(z > 0)
-                    def _(which=which, src=src):
-                        line_send(src, which, shard, down_s, me - RING).start()
-
-        on_line(z, k, body)
-
-    def other(piece, shard, onward):
-        arrived(piece, shard)
-        if onward:
-            send(spot(piece, shard), piece, shard, second_s, second).start()
-        send(spot(piece, shard), piece, shard, sib_s, sibling).start()
-
-    other(0, fcol, True)
-    other(0, scol, False)
-    other(1, fcol, True)
-    other(1, scol, False)
-    for copy, back in zip(ins, outs):
-        copy.wait()
-        back.start()
-    along(1)
-    other(2, fcol, True)
-    other(2, scol, False)
-    other(3, fcol, True)
-    other(3, scol, False)
-    along(2)
-    other(4, fcol, True)
-    other(4, scol, False)
-    for piece in range(pieces):
-        other(piece, sfcol, False)
-    along(3)
-    for piece in range(pieces):
-        for k in range(RING // 2):
-            arrived(piece, 2 * k + sibling % 2)
-    for back in outs:
-        back.wait()
-    for which in range(2):
-        for k in range(LINE):
-
-            @pl.when((z < LINE - 1) & (k <= z))
-            def _(which=which, k=k):
-                line_send(tokens[which][0], which, k, up_s, me + RING).wait_send()
-
-            @pl.when((z > 0) & (k >= z))
-            def _(which=which, k=k):
-                line_send(tokens[which][0], which, k, down_s, me - RING).wait_send()
-
-    for piece in range(pieces):
-        src = source(piece)
-        send(src, piece, col, first_s, first).wait_send()
-        send(src, piece, col, second_s, second).wait_send()
-        send(src, piece, fcol, second_s, second).wait_send()
-        for base in (col, fcol, scol, sfcol):
-            send(src, piece, base, sib_s, sibling).wait_send()
-
-
-def fetch_mlp(p, down, tokens, cotangent):
-    lines, rows, cols = p.shape
-    pieces = LINE + 1
-    return pl.pallas_call(
-        fetch_mlp_kernel,
-        out_shape=(
-            jax.ShapeDtypeStruct((LINE, RING, rows, cols), bf16),
-            jax.ShapeDtypeStruct((RING,) + down.shape, bf16),
-            jax.ShapeDtypeStruct((LINE,) + tokens.shape, bf16),
-            jax.ShapeDtypeStruct((LINE,) + cotangent.shape, bf16),
-        ),
-        in_specs=[ANY] * 4,
-        out_specs=(ANY,) * 4,
-        scratch_shapes=[
-            pltpu.VMEM(p.shape, bf16),
-            pltpu.VMEM(down.shape, bf16),
-            pltpu.VMEM(tokens.shape, bf16),
-            pltpu.VMEM(cotangent.shape, bf16),
-            DMA((8,)),
-            DMA((2, LINE)),
-            DMA((2, LINE)),
-            DMA((2, LINE)),
             DMA((pieces, RING)),
             DMA((pieces, RING)),
             DMA((pieces, RING)),
             DMA((pieces, RING)),
+            DMA((2, LINE)),
+            DMA((2, LINE)),
+            DMA((2, LINE)),
+            DMA,
+            DMA((LINE,)),
+            DMA,
         ],
-        compiler_params=pltpu.CompilerParams(collective_id=1, has_side_effects=True),
-        name="fetch_mlp",
-    )(p, down, tokens, cotangent)
+        compiler_params=pltpu.CompilerParams(
+            collective_id=0, has_side_effects=True, vmem_limit_bytes=64000 * 1024
+        ),
+        name="forward",
+    )(
+        hidden_in, out_grad, seq_lengths[None, :], seq_device[None, :], seq_lengths[:, None],
+        seq_device[:, None], freqs, gains, wq, wk, wv, wo, gate, up, wd,
+    )
 
 
 def add_rows(out, *terms):
@@ -920,13 +1094,6 @@
     )(a, o, gu, small)
 
 
-epsilon = 1e-06
-rope_base = 1000000.0
-masked_score = -1e30
-contract_rows = (((0,), (0,)), ((), ()))
-contract_cols = (((1,), (1,)), ((), ()))
-
-
 def layout(seq_lengths, seq_device, owner, slots):
     owned = seq_device == owner
     counts = jnp.where(owned, seq_lengths, 0)
@@ -1186,42 +1353,41 @@
     def swiglu(gate_in, up_in):
         return jax.nn.silu(gate_in) * up_in
 
-    def column(gain):
-        return jnp.pad(gain, (0, rows - gain.shape[0]))[:, None]
-
-    gains = jnp.concatenate([column(g) for g in (attn_gain, mlp_gain, q_gain, k_gain)], axis=1)
-    gains = jnp.pad(gains, ((0, 0), (0, 128 - gains.shape[1])))
-    packed = jnp.concatenate([w_query, w_key, w_value, w_out, gains], axis=1)
-    attn_w, mlp_w = fetch_attn(packed, w_gate, w_up)
-    gain_cols = attn_w[:, :, attn_width : attn_width + 4].astype(f32)
-    gain_attn = gain_cols[:, :, 0].reshape(-1)
-    gain_mlp = gain_cols[:, :, 1].reshape(-1)
-    gain_query = gain_cols[:, : q_gain.shape[0], 2].reshape(-1)
-    gain_key = gain_cols[:, : k_gain.shape[0], 3].reshape(-1)
+    lane = jnp.arange(128)[None, :]
+
+    def spread(gain, start, share):
+        placed = jnp.tile(gain, 128 // share)[None, :]
+        return jnp.where((lane >= start) & (lane < start + share), placed, 0)
+
+    pair = rows * (me % 2)
+    share = q_gain.shape[0]
+    gains = [spread(attn_gain, pair, rows), spread(mlp_gain, pair, rows)]
+    gains += [spread(q_gain, me * share, share), spread(k_gain, me * share, share)]
+    gains = jnp.pad(jnp.concatenate(gains, axis=0), ((0, rows - 4), (0, 0)))
+    (
+        attn_w, gate_up_w, down_w, tokens, cotangent,
+        middle, normed, qkv_raw, queries, keys, values, mixed, gains,
+    ) = forward(
+        hidden_in, out_grad, seq_lengths, seq_device, gains,
+        w_query, w_key, w_value, w_out, w_gate, w_up, w_down,
+    )
+    gain_attn, gain_mlp = gains[0], gains[1]
+    gain_query, gain_key = gains[2, :HD], gains[3, :HD]
     attn_w = attn_w.reshape(n * rows, attn_w.shape[2])
     qkv_w = attn_w[:, :qkv_width]
     out_w = attn_w[:, qkv_width:attn_width]
-
     inputs = hidden_in.astype(f32)
-    normed = rmsnorm(inputs, gain_attn).astype(bf16)
-    qkv_raw = matmul(normed, qkv_w)
     query_raw = qkv_raw[:, :query_width]
     key_raw = qkv_raw[:, query_width : query_width + KVH * HD]
-    value_raw = qkv_raw[:, query_width + KVH * HD :]
-    queries = query_path(query_raw, gain_query).astype(bf16).reshape(slots, KVH, groups, HD)
-    keys = key_path(key_raw, gain_key).astype(bf16)
-    values = value_raw.astype(bf16).reshape(slots, KVH, HD)
+    queries = queries.reshape(slots, KVH, groups, HD)
+    keys = keys.reshape(slots, KVH, HD)
+    values = values.reshape(slots, KVH, HD)
     scores = jnp.einsum("qgrd,kgd->grqk", queries, keys, preferred_element_type=f32) * score_scale
     logits = jnp.where(allowed, scores, masked_score)
     exponent = jnp.exp(logits - jnp.max(logits, axis=-1, keepdims=True))
     probs = exponent / jnp.sum(exponent, axis=-1, keepdims=True)
     weights = probs.astype(bf16)
-    mixed = jnp.einsum("grqk,kgd->qgrd", weights, values, preferred_element_type=f32)
-    mixed = mixed.reshape(slots, query_width).astype(bf16)
-    middle = inputs + matmul(mixed, out_w)
-    second = rmsnorm(middle, gain_mlp).astype(bf16)
-
-    gate_up_w, down_w, tokens, cotangent = fetch_mlp(mlp_w, w_down, second, out_grad)
+
     gate_up_w = gate_up_w.reshape(n * rows, gate_up_w.shape[-1])
     down_w = down_w.reshape(-1, down_w.shape[-1])
     tokens = tokens.reshape(-1, width)

time: 625 us -> 577 us (0.923)
  Pallas kernels: 455 us -> 429 us
  matrix products: 117 us -> 95.3 us
    pallas_call x2 -> x1, Pallas kernels: 214 us -> 198 us  [forward(): pl.pallas_call(forward_kernel, out_shape=(S((n, rows, wide), bf16), S((LI...]
    dot_general x4 -> x2, matrix products: 31.7 us -> 20.1 us  [matmul(): return jnp.dot(left, right, preferred_element_type=jnp.float32)]
    unnamed x109 -> x88, local copies, waits for them, and re-layouts: 15 us -> 9.58 us
where the time goes in v2:
time: 577 us; the launch traced here: 573 us
  Pallas kernels  429 us (74%)
  matrix products  95.3 us (17%)
  local copies, waits for them, and re-layouts  27 us (5%)
  other arithmetic  20.6 us (4%)
    pallas_call x1, Pallas kernels, forward(): pl.pallas_call(forward_kernel, out_shape=(S((n, rows, wide), bf16), S((LI...  198 us
    pallas_call x1, Pallas kernels, reduce_attn(): pl.pallas_call(reduce_attn_kernel, out_shape=(jax.ShapeDtypeStruct((rows,...  141 us
    pallas_call x1, Pallas kernels, reduce_mlp(): pl.pallas_call(reduce_mlp_kernel, out_shape=(jax.ShapeDtypeStruct((LINE,...  90.3 us
    dot_general x4, matrix products, times_cols(): lax.dot_general(left, right, contract_cols, preferred_element_type=jnp.fl...  34.6 us
    dot_general x4, matrix products, times_rows(): lax.dot_general(left, right, contract_rows, preferred_element_type=jnp.fl...  29.2 us
    dot_general x2, matrix products, matmul(): return jnp.dot(left, right, preferred_element_type=jnp.float32)  20.1 us

profile of v2, /device:TPU:8, one launch (start us, length us, event | category | flops | bytes accessed | tf_op | source)
XLA Modules:
  0.0 573.2 jit_solution(8030385085910043809)
XLA Ops:
  4.9 1.4 copy.173.len_col
  6.3 1.4 copy.174.dev_col
  7.7 197.5 %forward.1 = (bf16[32,64,6272]{2,1,0:T(8,128)(2,1)}, bf16[4,8,64,3072]{3,2,1,0:T(8,128)(2,1)}, bf16[8,192,2048]{2,1,0:T(8,128)(2,1)}, bf16[4,128,2048]{2,1,0:T(8...) custom-call(bf16[128,2048]{1,0:T(8,128)(2,1)} %x_ref.1, ...), custom_call_target="tpu_custom_call" | custom-call | tf_op jit(solution)/shard_map/forward/pallas_call | solution.py:505
  205.2 12.1 %fusion.79 = f32[512,3072]{1,0:T(8,128)} fusion(bf16[512,2048]{1,0:T(8,128)(2,1)} %bitcast.147, bf16[2048,3072]{1,0:T(8,128)(2,1)} %bitcast.141), kind=kOutput, calls=%fused_computation.154 | convolution fusion | flops 6442450944 | bytes 20971520 | tf_op jit(solution)/shard_map/dot_general | solution.py:1135
  217.4 8.0 %fusion.8 = (bf16[512,1536]{1,0:T(8,128)(2,1)}, bf16[512,1536]{1,0:T(8,128)(2,1)}, bf16[512,1536]{1,0:T(8,128)(2,1)S(1)}) fusion(f32[512,3072]{1,0:T(8,128)} %fusion.79, bf16[512,2048]{1,0:T(8,128)(2,1)S(1)} %bitcast.149, bf16[1536,2048]{1,0:T(8,128)(2,1)S(1)} %bitcast.146), kind=kOutput, calls=%fused_computation.13 | convolution fusion | flops 3233808384 | bytes 19398656 | tf_op jit(solution)/shard_map/dot_general | solution.py:1143
  225.4 8.0 %convolution_convert_fusion.5 = bf16[512,2048]{1,0:T(8,128)(2,1)} fusion(bf16[512,1536]{1,0:T(8,128)(2,1)S(1)} %get-tuple-element.77, bf16[1536,2048]{1,0:T(8,128)(2,1)} %bitcast.145), kind=kOutput, calls=%fused_computation.20 | convolution fusion | flops 3222274048 | bytes 9961472 | tf_op jit(solution)/shard_map/dot_general | solution.py:1135
  233.4 9.4 %convolution_convert_fusion.4 = bf16[512,2048]{1,0:T(8,128)(2,1)} fusion(bf16[2048,3072]{1,0:T(8,128)(2,1)S(1)} %bitcast.144, bf16[512,1536]{1,0:T(8,128)(2,1)} %get-tuple-element.76, bf16[512,1536]{1,0:T(8,128)(2,1)} %get-tuple-element.75), kind=kOutput, calls=%fused_computation.19 | convolution fusion | flops 6449790976 | bytes 17825792 | tf_op jit(solution)/shard_map/dot_general | solution.py:1143
  242.8 5.5 convolution_convert_fusion.2
  248.4 9.9 %convolution_convert_fusion.1 = bf16[2048,3072]{1,0:T(8,128)(2,1)} fusion(bf16[512,2048]{1,0:T(8,128)(2,1)S(1)} %bitcast.148, bf16[512,1536]{1,0:T(8,128)(2,1)S(1)} %copy-done.33, bf16[512,1536]{1,0:T(8,128)(2,1)S(1)} %copy-done.32), kind=kOutput, calls=%fused_computation.5 | convolution fusion | flops 6455033856 | bytes 17825792 | tf_op jit(solution)/shard_map/dot_general | solution.py:1139
  258.2 90.3 %reduce_mlp.1 = (bf16[4,64,3072]{2,1,0:T(8,128)(2,1)}, f32[192,2048]{1,0:T(8,128)}, f32[128,2048]{1,0:T(8,128)}, f32[128,2048]{1,0:T(8,128)}) custom-call(bf16[4,8,64,3072]{3,2,1,0:T(8,128)(2,1)} %bitcast.108, bf16[8,192,2048]{2,1,0:T(8,128)(2,1)} %bitcast.109, bf16[4,128,2048]{2,1,0:T(8,128)(2,1)} %bitcast.118, bf16[4,128,2048]{2,1,0:T(8,128)(2,1)} %bitcast.117), custom_call_target="tpu_custom_call" | custom-call | tf_op jit(solution)/shard_map/reduce_mlp/pallas_call | solution.py:789
  348.6 1.6 fusion.73
  350.4 1.5 multiply_reduce_fusion
  351.9 2.4 fusion.22
  354.3 6.4 %fusion.10 = bf16[128,2048]{1,0:T(8,128)(2,1)S(1)} fusion(bf16[2048,6272]{1,0:T(8,128)(2,1)} %bitcast.139, f32[128,2048]{1,0:T(8,128)S(1)} %get-tuple-element.80), kind=kOutput, calls=%fused_computation.21 | convolution fusion | flops 1074266112 | bytes 9961472 | tf_op jit(solution)/shard_map/dot_general | solution.py:1143
  361.4 1.7 copy.214
  363.1 1.2 copy.216
  365.7 2.4 fusion.76
  368.2 3.2 fusion.33
  371.4 1.7 copy.183
  373.6 1.7 fusion.71
  377.1 4.0 multiply_reduce_fusion.1
  381.2 1.8 fusion.23
  383.2 3.6 broadcast_multiply_fusion.1
  389.2 1.3 multiply_reduce_fusion.7
  392.5 1.9 fusion.21
  394.8 10.8 %fusion.28 = (f32[2048]{0:T(1024)S(1)}, f32[128]{0:T(128)S(1)}, f32[128,2048]{1,0:T(8,128)}) fusion(bf16[128,2048]{1,0:T(8,128)(2,1)S(1)} %copy-done.2, f32[128]{0:T(128)S(1)} %fusion.59, f32[2048]{0:T(1024)S(1)} %bitcast.131, bf16[2048,6272]{1,0:T(8,128)(2,1)} %bitcast.140, bf16[128,1024]{1,0:T(8,128)(2,1)S(1)} %copy.198, ...), kind=kOutput, calls=%fused_computation.48 | convolution fusion | flops 2152462336 | bytes 19416064 | tf_op jit(solution)/shard_map/dot_general | solution.py:1143
  406.3 5.6 convolution_convert_fusion.3
  411.9 8.2 %convolution_convert_fusion = bf16[2048,4096]{1,0:T(8,128)(2,1)} fusion(bf16[128,2048]{1,0:T(8,128)(2,1)S(1)} %copy-done.13, bf16[128,1024]{1,0:T(8,128)(2,1)S(1)} %copy.198, bf16[128,1024]{1,0:T(8,128)(2,1)S(1)} %copy.197, bf16[128,2048]{1,0:T(8,128)(2,1)S(1)} %bitcast.115), kind=kOutput, calls=%fused_computation.4 | convolution fusion | flops 2159017984 | bytes 18350080 | tf_op jit(solution)/shard_map/dot_general | solution.py:1139
  420.1 140.9 %reduce_attn.1 = (f32[64,2048]{1,0:T(8,128)}, f32[64,1024]{1,0:T(8,128)}, f32[64,1024]{1,0:T(8,128)}, f32[64,2048]{1,0:T(8,128)}, f32[64,6144]{1,0:T(8,128)}, /*index=5*/f32[64,6144]{1,0:T(8,128)}, f32[40,128]{1,0:T(8,128)}) custom-call(bf16[32,64,4096]{2,1,0:T(8,128)(2,1)} %bitcast.104, bf16[32,64,2048]{2,1,0:T(8,128)(2,1)} %bitcast.105, ...), custom_call_target="tpu_custom_call" | custom-call | tf_op jit(solution)/shard_map/reduce_attn/pallas_call | solution.py:1049
  561.0 1.4 fusion.75
  562.4 1.3 fusion.74
  563.7 2.8 fusion.24
  (144 shorter events, 21.0 us)
Async XLA Ops:
  205.2 12.2 %copy-start.26 = (bf16[8,192,2048]{2,1,0:T(8,128)(2,1)S(1)}, bf16[8,192,2048]{2,1,0:T(8,128)(2,1)}, u32[]{:S(2)}) copy-start(bf16[8,192,2048]{2,1,0:T(8,128)(2,1)} %get-tuple-element.40) | copy-start | bytes 18874372
  205.2 12.1 %copy-start.28 = (bf16[4,128,2048]{2,1,0:T(8,128)(2,1)S(1)}, bf16[4,128,2048]{2,1,0:T(8,128)(2,1)}, u32[]{:S(2)}) copy-start(bf16[4,128,2048]{2,1,0:T(8,128)(2,1)} %get-tuple-element.39) | copy-start | bytes 6291460
  217.3 16.0 %slice-start = ((s8[12582912]{0:T(1024)(128)(4,1)}), s8[4194304]{0:T(1024)(128)(4,1)S(1)}, s32[]{:S(2)}) async-start(s8[12582912]{0:T(1024)(128)(4,1)} %bitcast.142), calls=%async_computation | async-start | bytes 8388608
  217.3 16.0 %slice-start.1 = ((s8[12582912]{0:T(1024)(128)(4,1)}), s8[4194304]{0:T(1024)(128)(4,1)S(1)}, s32[]{:S(2)}) async-start(s8[12582912]{0:T(1024)(128)(4,1)} %bitcast.142), calls=%async_computation.1 | async-start | bytes 8388608
  225.3 8.0 %copy-start.30 = (bf16[512,1536]{1,0:T(8,128)(2,1)}, bf16[512,1536]{1,0:T(8,128)(2,1)S(1)}, u32[]{:S(2)}) copy-start(bf16[512,1536]{1,0:T(8,128)(2,1)S(1)} %get-tuple-element.77) | copy-start | bytes 4718596
  225.4 8.0 %slice-start.2 = ((s8[12582912]{0:T(1024)(128)(4,1)}), s8[4194304]{0:T(1024)(128)(4,1)S(1)}, s32[]{:S(2)}) async-start(s8[12582912]{0:T(1024)(128)(4,1)} %bitcast.142), calls=%async_computation.2 | async-start | bytes 8388608
  233.4 9.4 %copy-start.31 = (bf16[512,1536]{1,0:T(8,128)(2,1)S(1)}, bf16[512,1536]{1,0:T(8,128)(2,1)}, u32[]{:S(2)}) copy-start(bf16[512,1536]{1,0:T(8,128)(2,1)} %copy-done.30) | copy-start | bytes 4718596
  242.8 5.6 copy-start.27
  242.8 5.6 copy-start.32
  242.8 5.5 copy-start.33
  258.2 92.0 %copy-start = (f32[128,2048]{1,0:T(8,128)S(1)}, f32[128,2048]{1,0:T(8,128)}, u32[]{:S(2)}) copy-start(f32[128,2048]{1,0:T(8,128)} %get-tuple-element.37) | copy-start | bytes 3145732
  348.5 3.3 copy-start.1
  348.6 3.3 copy-start.3
  348.6 3.3 copy-start.4
  354.3 6.7 %copy-start.20 = (bf16[128,1024]{1,0:T(8,128)(2,1)S(1)}, bf16[128,1024]{1,0:T(8,128)(2,1)}, u32[]{:S(2)}) copy-start(bf16[128,1024]{1,0:T(8,128)(2,1)} %get-tuple-element.47) | copy-start | bytes 786436
  360.7 4.5 copy-start.23
  360.7 4.4 copy-start.24
  361.0 7.2 %copy-start.5 = (bf16[128,2048]{0,1:T(8,128)(2,1)}, bf16[128,2048]{0,1:T(8,128)(2,1)S(1)}, u32[]{:S(2)}) copy-start(bf16[128,2048]{0,1:T(8,128)(2,1)S(1)} %copy.215) | copy-start | bytes 1572868
  361.4 10.0 %copy-start.12 = (f32[8,2,128,128]{2,3,1,0:T(8,128)}, f32[8,2,128,128]{2,3,1,0:T(8,128)S(1)}, u32[]{:S(2)}) copy-start(f32[8,2,128,128]{2,3,1,0:T(8,128)S(1)} %convolution_bitcast_fusion) | copy-start | bytes 3145732
  363.1 8.3 %copy-start.14 = (bf16[128,2048]{0,1:T(8,128)(2,1)}, bf16[128,2048]{0,1:T(8,128)(2,1)S(1)}, u32[]{:S(2)}) copy-start(bf16[128,2048]{0,1:T(8,128)(2,1)S(1)} %copy.214) | copy-start | bytes 1572868
  365.7 5.7 copy-start.22
  368.2 15.0 %copy-start.29 = (f32[8,2,128]{2,1,0:T(2,128)}, f32[8,2,128]{2,1,0:T(2,128)S(1)}, u32[]{:S(2)}) copy-start(f32[8,2,128]{2,1,0:T(2,128)S(1)} %get-tuple-element.94) | copy-start | bytes 24580
  388.6 3.9 copy-start.6
  394.8 10.8 %copy-start.25 = (f32[128]{0:T(128)S(1)}, f32[128]{0:T(128)}, u32[]{:S(2)}) copy-start(f32[128]{0:T(128)} %get-tuple-element.65) | copy-start | bytes 1540
  394.8 11.5 %copy-start.10 = (bf16[128,2048]{1,0:T(8,128)(2,1)S(1)}, bf16[128,2048]{1,0:T(8,128)(2,1)}, u32[]{:S(2)}) copy-start(bf16[128,2048]{1,0:T(8,128)(2,1)} %get-tuple-element.51) | copy-start | bytes 1572868
  406.3 5.6 copy-start.13
  560.9 5.5 copy-start.17
  561.0 6.3 %copy-start.19 = (f32[64,1024]{1,0:T(8,128)S(1)}, f32[64,1024]{1,0:T(8,128)}, u32[]{:S(2)}) copy-start(f32[64,1024]{1,0:T(8,128)} %get-tuple-element.124) | copy-start | bytes 786436
  561.0 7.0 %copy-start.18 = (f32[64,1024]{1,0:T(8,128)S(1)}, f32[64,1024]{1,0:T(8,128)}, u32[]{:S(2)}) copy-start(f32[64,1024]{1,0:T(8,128)} %get-tuple-element.125) | copy-start | bytes 786436
  561.0 7.7 %copy-start.16 = (f32[64,2048]{1,0:T(8,128)S(1)}, f32[64,2048]{1,0:T(8,128)}, u32[]{:S(2)}) copy-start(f32[64,2048]{1,0:T(8,128)} %get-tuple-element.126) | copy-start | bytes 1572868
  563.7 5.8 %copy-start.9 = (f32[64,6144]{1,0:T(8,128)S(1)}, f32[64,6144]{1,0:T(8,128)}, u32[]{:S(2)}) copy-start(f32[64,6144]{1,0:T(8,128)} %get-tuple-element.128) | copy-start | bytes 4718596
  566.4 4.2 copy-start.8
  (5 other events, 10.7 us)

commit v3 on v2

--- a/solution.py
+++ b/solution.py
@@ -1,4 +1,4 @@
-import functools
+import math
 
 import jax
 import jax.numpy as jnp
@@ -68,16 +68,62 @@
             body(step)
 
 
+def dot_nt(left, right):
+    return lax.dot_general(left, right, contract_cols, preferred_element_type=f32)
+
+
+def dot_tn(left, right):
+    return lax.dot_general(left, right, contract_rows, preferred_element_type=f32)
+
+
+def streamed(count, fetch, body):
+    for copy in fetch(0, 0):
+        copy.start()
+
+    def step(i, carry):
+        slot = i % 2
+
+        @pl.when(i + 1 < count)
+        def _():
+            for copy in fetch(i + 1, 1 - slot):
+                copy.start()
+
+        for copy in fetch(i, slot):
+            copy.wait()
+        body(i, slot)
+        return carry
+
+    lax.fori_loop(0, count, step, 0)
+
+
+def tile(i, size):
+    return pl.ds(pl.multiple_of(i * size, size), size)
+
+
+def add_rows(out, *terms):
+    rows = out.shape[0]
+
+    def body(i, carry):
+        at = pl.ds(pl.multiple_of(i * 16, 16), 16)
+        total = terms[0][at, :].astype(f32)
+        for term in terms[1:]:
+            total = total + term[at, :].astype(f32)
+        out[at, :] = total.astype(out.dtype)
+        return carry
+
+    lax.fori_loop(0, rows // 16, body, 0)
+
+
 def lane_sum(x):
     return jnp.sum(x, axis=-1, keepdims=True)
 
 
-def token_places(len_row, dev_row, len_col, dev_col, me):
-    seqs = len_row.shape[1]
-    counts_row = jnp.where(dev_row == me, len_row, 0).astype(f32)
-    counts_col = jnp.where(dev_col == me, len_col, 0).astype(f32)
+def token_places(lengths, devices, me):
+    seqs = lengths.shape[1]
+    counts_row = jnp.where(devices == me, lengths, 0).astype(f32)
     up = lax.broadcasted_iota(jnp.int32, (seqs, seqs), 0)
     across = lax.broadcasted_iota(jnp.int32, (seqs, seqs), 1)
+    counts_col = lane_sum(jnp.where(up == across, counts_row, 0.0))
     starts_row = jnp.sum(jnp.where(up < across, counts_col, 0.0), axis=0, keepdims=True)
     starts_col = lane_sum(jnp.where(across < up, counts_row, 0.0))
 
@@ -114,13 +160,16 @@
 
 
 def forward_kernel(
-    x_ref, cot_ref, len_row, dev_row, len_col, dev_col, freq_ref, gain_ref,
+    x_ref, len_ref, dev_ref, ga_ref, gm_ref, gq_ref, gk_ref, cot_ref,
     wq_ref, wk_ref, wv_ref, wo_ref, gate_ref, up_ref, wd_ref,
     w_out, gu_out, d_out, tok_out, cot_out,
-    middle_out, normed_out, raw_out, q_out, k_out, v_out, mixed_out, gains_out,
-    w_tmp, p_tmp, d_tmp, cot_tmp, second_tmp, chunk, ow_all, gain_tmp, cos_tmp, sin_tmp, bias_tmp,
+    hid_out, dgu_out,
+    middle_out, normed_out, raw_out, q_out, k_out, v_out, mixed_out, gains_out, rope_out,
+    w_tmp, p_tmp, d_tmp, cot_tmp, second_tmp, chunk, ow_all, gain_tmp, gain_own,
+    tok_all, cot_all, gate_up, dhid, m_chunk, wd_rows, hid, dgu,
     local, up_s, down_s, first_s, second_s, sib_s, recv, ex_send, ex_recv,
     m_first_s, m_second_s, m_sib_s, m_recv, line_up, line_down, line_r, w_load, o_load, g_load,
+    stream, act_out,
 ):
     me, z, first, second, sibling = where_am_i()
     col, fcol, scol = me % RING, first % RING, second % RING
@@ -134,7 +183,7 @@
 
     w_in = []
     lo = 0
-    for i, ref in enumerate((wq_ref, wk_ref, wv_ref, wo_ref, gain_ref)):
+    for i, ref in enumerate((wq_ref, wk_ref, wv_ref, wo_ref)):
         at = pl.ds(lo, ref.shape[1])
         w_in.append(pltpu.make_async_copy(ref, w_tmp.at[:, at], local.at[i]))
         lo += ref.shape[1]
@@ -150,6 +199,15 @@
     cot_in = pltpu.make_async_copy(cot_ref, cot_tmp, local.at[8])
     for copy in w_in + p_in + [d_in, cot_in]:
         copy.start()
+    gain_own[...] = jnp.zeros_like(gain_own)
+    for i, ref in enumerate((ga_ref, gm_ref, gq_ref, gk_ref)):
+        gain_own[i : i + 1, 0 : ref.shape[1]] = ref[...].astype(f32)
+    flat = gain_own[...]
+    paired = jnp.where(me % 2 == 0, flat, pltpu.roll(flat, rows, 1))
+    shared = pltpu.roll(flat, gq_ref.shape[1] * me, 1)
+    placed = jnp.where(lax.broadcasted_iota(jnp.int32, flat.shape, 0) < 2, paired, shared)
+    w_tmp[0:16, attn_width:] = placed.astype(bf16)
+    w_tmp[16:, attn_width:] = jnp.zeros((rows - 16, 128), bf16)
     greet(line_peers(me) + [first, second, sibling])
 
     def send(src, shard, sems, device):
@@ -245,13 +303,12 @@
 
         on_line(z, k, body)
 
-    segment_col, segment_row, position = token_places(
-        len_row[...], dev_row[...], len_col[...], dev_col[...], me
-    )
-    bias_tmp[...] = allowed_bias(segment_col, segment_row)
-    angles = position * freq_ref[...]
-    cos_tmp[...] = jnp.cos(angles)
-    sin_tmp[...] = jnp.sin(angles)
+    segment_col, segment_row, position = token_places(len_ref[...], dev_ref[...], me)
+    rope_out[2] = allowed_bias(segment_col, segment_row)
+    lane = lax.broadcasted_iota(jnp.int32, (1, HD), 1) % (HD // 2)
+    angles = position * jnp.exp(lane.astype(f32) * (-2.0 * math.log(rope_base) / HD))
+    rope_out[0] = jnp.cos(angles)
+    rope_out[1] = jnp.sin(angles)
     x_scale = rms_scale(x_ref[...].astype(f32))
     raw_out[...] = jnp.zeros_like(raw_out)
 
@@ -344,10 +401,13 @@
     def m_arrived(piece, shard):
         m_send(spot(piece, shard), piece, shard, m_sib_s, sibling).wait_recv()
 
-    for piece in range(pieces):
+    def m_own(piece):
         m_send(source(piece), piece, col, m_first_s, first).start()
         m_send(source(piece), piece, col, m_second_s, second).start()
         m_send(source(piece), piece, col, m_sib_s, sibling).start()
+
+    m_own(LINE)
+    m_own(0)
     backs = [
         pltpu.make_async_copy(p_tmp, gu_out.at[:, col], local.at[11]),
         pltpu.make_async_copy(d_tmp, d_out.at[col], local.at[12]),
@@ -368,7 +428,7 @@
             small = small + gain_tmp[zz, i].astype(f32)
     q_gain, k_gain = small[2:3], small[3:4]
     gains_out[2:4, 0:128] = small[2:4]
-    cosine, sine, bias = cos_tmp[...], sin_tmp[...], bias_tmp[...]
+    cosine, sine, bias = rope_out[0], rope_out[1], rope_out[2]
 
     def turned(v, gain):
         v = v * rms_scale(v) * gain
@@ -431,35 +491,123 @@
             m_send(spot(piece, shard), piece, shard, m_second_s, second).start()
         m_send(spot(piece, shard), piece, shard, m_sib_s, sibling).start()
 
-    m_other(0, fcol, True)
+    def m_whole(piece):
+        for k in range(RING // 2):
+            m_arrived(piece, 2 * k + sibling % 2)
+
+    part = dhid.shape[1]
+    dim = tok_out.shape[2]
+    wide = wd_rows.shape[2]
+
+    def down_back(lo, hi):
+        def fetch(i, slot):
+            j = lo + i
+            return (
+                pltpu.make_async_copy(
+                    d_out.at[tile(j, 2)], wd_rows.at[slot], stream.at[slot]
+                ),
+            )
+
+        def body(i, slot):
+            right = wd_rows[slot].reshape(wide * 2, dim)
+            dhid[:, tile(lo + i, 2 * wide)] = dot_nt(cot_all[...].reshape(LINE * CAP, dim), right)
+
+        streamed(hi - lo, fetch, body)
+
+    def gate_up_rows(piece):
+        m_whole(piece)
+        copy = pltpu.make_async_copy(gu_out.at[piece], m_chunk, stream.at[0])
+        copy.start()
+        copy.wait()
+        span = RING * rows
+        left = tok_all[:, :, pl.ds(piece * span, span)].reshape(LINE * CAP, span)
+
+        def columns(n, carry):
+            at = tile(n, 512)
+            term = jnp.dot(left, m_chunk[:, :, at].reshape(span, 512), preferred_element_type=f32)
+            if piece == 0:
+                gate_up[:, at] = term
+            else:
+                gate_up[:, at] += term
+            return carry
+
+        lax.fori_loop(0, 2 * part // 512, columns, 0)
+
+    m_other(LINE, fcol, True)
     line_own(0, second_tmp)
     tok_back = pltpu.make_async_copy(second_tmp, tok_out.at[z], local.at[13])
     tok_back.start()
+    m_own(1)
+    m_other(LINE, scol, False)
+    m_other(0, fcol, True)
+    m_own(2)
     m_other(0, scol, False)
+    line_relay(1, 3)
+    cot_back.wait()
+    cot_in = pltpu.make_async_copy(cot_out, cot_all, local.at[8])
+    cot_in.start()
+    m_other(LINE, sfcol, False)
+    line_relay(0, 1)
     m_other(1, fcol, True)
+    m_own(3)
     m_other(1, scol, False)
-    line_relay(1, 3)
+    m_whole(LINE)
+    for copy in backs:
+        copy.wait()
+    cot_in.wait()
+    down_back(0, RING // 4)
+    m_other(0, sfcol, False)
+    line_relay(0, 2)
     m_other(2, fcol, True)
     m_other(2, scol, False)
-    line_relay(0, 1)
+    down_back(RING // 4, RING // 2)
+    m_other(1, sfcol, False)
+    line_relay(0, 3)
+    tok_back.wait()
+    tok_in = pltpu.make_async_copy(tok_out, tok_all, local.at[10])
+    tok_in.start()
     m_other(3, fcol, True)
     m_other(3, scol, False)
-    m_other(4, fcol, True)
-    line_relay(0, 2)
-    m_other(4, scol, False)
-    m_other(0, sfcol, False)
-    m_other(1, sfcol, False)
-    line_relay(0, 3)
-    for piece in range(2, pieces):
-        m_other(piece, sfcol, False)
-    for piece in range(pieces):
-        for k in range(RING // 2):
-            m_arrived(piece, 2 * k + sibling % 2)
-
-    cot_back.wait()
-    tok_back.wait()
-    for copy in backs:
-        copy.wait()
+    tok_in.wait()
+    gate_up_rows(0)
+    m_other(2, sfcol, False)
+    gate_up_rows(1)
+    m_other(3, sfcol, False)
+    gate_up_rows(2)
+    gate_up_rows(3)
+
+    def act_copies(n):
+        up_at = pl.ds(pl.multiple_of(part + n * 256, 256), 256)
+        return (
+            pltpu.make_async_copy(hid.at[:, tile(n, 256)], hid_out.at[:, tile(n, 256)], act_out.at[n, 0]),
+            pltpu.make_async_copy(dgu.at[:, tile(n, 256)], dgu_out.at[:, tile(n, 256)], act_out.at[n, 1]),
+            pltpu.make_async_copy(dgu.at[:, up_at], dgu_out.at[:, up_at], act_out.at[n, 2]),
+        )
+
+    def units(n, carry):
+        at = tile(n, 256)
+        up_at = pl.ds(pl.multiple_of(part + n * 256, 256), 256)
+
+        def act(r, inner):
+            some = tile(r, 32)
+            gate, up, back = gate_up[some, at], gate_up[some, up_at], dhid[some, at]
+            sig = jax.nn.sigmoid(gate)
+            silu = gate * sig
+            hid[some, at] = (silu * up).astype(bf16)
+            dgu[some, at] = (back * up * (sig * (1.0 + gate * (1.0 - sig)))).astype(bf16)
+            dgu[some, up_at] = (back * silu).astype(bf16)
+            return inner
+
+        lax.fori_loop(0, LINE * CAP // 32, act, 0)
+        for copy in act_copies(n):
+            copy.start()
+        return carry
+
+    lax.fori_loop(0, part // 256, units, 0)
+
+    for n in range(part // 256):
+        for copy in act_copies(n):
+            copy.wait()
     for k in range(1, LINE):
         for which in range(2):
             exchange(k, which).wait_send()
@@ -497,10 +645,8 @@
     n = RING * LINE
     width = gate.shape[1] // LINE
     qkv_width = wq.shape[1] + wk.shape[1] + wv.shape[1]
-    wide = qkv_width + wo.shape[1] + gains.shape[1]
+    wide = qkv_width + wo.shape[1] + 128
     pieces = LINE + 1
-    half = jnp.power(rope_base, -2.0 * jnp.arange(HD // 2, dtype=f32) / HD)
-    freqs = jnp.concatenate([half, half])[None, :]
     S = jax.ShapeDtypeStruct
     return pl.pallas_call(
         forward_kernel,
@@ -510,6 +656,8 @@
             S((RING,) + wd.shape, bf16),
             S((LINE, slots, dim), bf16),
             S((LINE, slots, dim), bf16),
+            S((LINE * slots, width), bf16),
+            S((LINE * slots, 2 * width), bf16),
             S((slots, dim), f32),
             S((slots, dim), bf16),
             S((slots, qkv_width), f32),
@@ -518,9 +666,10 @@
             S((slots, KVH * HD), bf16),
             S((slots, H * HD), bf16),
             S((8, dim), f32),
+            S((3, slots, HD), f32),
         ),
-        in_specs=[VMEM, ANY] + [VMEM] * 5 + [ANY] * 8,
-        out_specs=(ANY,) * 5 + (VMEM,) * 8,
+        in_specs=[VMEM] * 7 + [ANY] * 8,
+        out_specs=(ANY,) * 7 + (VMEM,) * 9,
         scratch_shapes=[
             pltpu.VMEM((rows, wide), bf16),
             pltpu.VMEM((LINE, rows, 2 * width), bf16),
@@ -530,9 +679,15 @@
             pltpu.VMEM((RING, rows, qkv_width), bf16),
             pltpu.VMEM((n, rows, wo.shape[1]), bf16),
             pltpu.VMEM((LINE, RING, 16, 128), bf16),
-            pltpu.VMEM((slots, HD), f32),
-            pltpu.VMEM((slots, HD), f32),
-            pltpu.VMEM((slots, slots), f32),
+            pltpu.VMEM((16, 128), f32),
+            pltpu.VMEM((LINE, slots, dim), bf16),
+            pltpu.VMEM((LINE, slots, dim), bf16),
+            pltpu.VMEM((LINE * slots, 2 * width), f32),
+            pltpu.VMEM((LINE * slots, width), f32),
+            pltpu.VMEM((RING, rows, 2 * width), bf16),
+            pltpu.VMEM((2, 2) + wd.shape, bf16),
+            pltpu.VMEM((LINE * slots, width), bf16),
+            pltpu.VMEM((LINE * slots, 2 * width), bf16),
             DMA((14,)),
             DMA((n,)),
             DMA((n,)),
@@ -552,35 +707,25 @@
             DMA,
             DMA((LINE,)),
             DMA,
+            DMA((2,)),
+            DMA((width // 256, 3)),
         ],
         compiler_params=pltpu.CompilerParams(
             collective_id=0, has_side_effects=True, vmem_limit_bytes=64000 * 1024
         ),
         name="forward",
     )(
-        hidden_in, out_grad, seq_lengths[None, :], seq_device[None, :], seq_lengths[:, None],
-        seq_device[:, None], freqs, gains, wq, wk, wv, wo, gate, up, wd,
-    )
-
-
-def add_rows(out, *terms):
-    rows = out.shape[0]
-
-    def body(i, carry):
-        at = pl.ds(pl.multiple_of(i * 16, 16), 16)
-        total = terms[0][at, :].astype(f32)
-        for term in terms[1:]:
-            total = total + term[at, :].astype(f32)
-        out[at, :] = total.astype(out.dtype)
-        return carry
-
-    lax.fori_loop(0, rows // 16, body, 0)
-
-
-def reduce_mlp_kernel(
-    gu_ref, d_ref, ds_ref, y_ref, gu_out, d_out, ds_out, y_out,
-    gu_own, gu_sib, gu_sec, gu_fst, d_own, d_sib, d_sec, d_fst, t_own, t_down, t_up,
-    load, t_load, c_send, c_recv, s_send, s_recv, f_send, f_recv, down_s, down_r, up_s, up_r,
+        hidden_in, seq_lengths[None, :], seq_device[None, :], *[g[None, :] for g in gains],
+        out_grad, wq, wk, wv, wo, gate, up, wd,
+    )
+
+
+def turn_kernel(
+    gu_ref, wd_ref, tok_ref, cot_ref, hid_ref, dgu_ref, w_ref, middle_ref, normed_ref, raw_ref, q_ref, k_ref, v_ref,
+    mixed_ref, gains_ref, rope_ref,
+    y_out, dmid_out, dqkv_out, small_out, d_out, gu_out, gq_out, go_out,
+    gu_all, gd_all, gu_sib, gd_sib, gu_sec, gd_sec, gu_fst, gd_fst, t_own, t_land,
+    c_send, c_recv, s_send, s_recv, f_send, f_recv, down_s, down_r, up_s, up_r, load, stream, back,
 ):
     me, z, first, second, sibling = where_am_i()
     greet([lax.rem(me + RING, RING * LINE), lax.rem(me + RING * (LINE - 1), RING * LINE)]
@@ -588,49 +733,46 @@
     core = me % 2
     mine, fst, sec = (me % RING) // 2, (first % RING) // 2, (second % RING) // 2
     far = ((second + first - me) % RING) // 2
-    half = d_fst.shape[0] // 2
+    half = gd_fst.shape[0] // 2
     last = LINE - 1
-    groups = ((0, LINE), (LINE, LINE + 2))
+    tokens, dim = tok_ref.shape
+    part = wd_ref.shape[0]
+    quad_rows = part // LINE
+    MLP_GU, MLP_D = (0, 0, LINE), (1, LINE, LINE + 2)
 
     def block(gu, d, piece, group):
         if group == 0:
             return gu.at[piece]
-        return d.at[pl.ds(pl.multiple_of((piece - LINE) * half, half), half)]
-
-    def each(body):
-        for group, (lo, hi) in enumerate(groups):
-
-            def step(piece, carry, group=group):
-                body(piece, group)
-                return carry
-
-            lax.fori_loop(lo, hi, step, 0)
-
-    def stored(target, piece, group):
+        return d.at[tile(piece - LINE, half)]
+
+    def own_block(quad, piece, group, theirs=False):
+        shard = 2 * quad + (1 - core if theirs else core)
         if group == 0:
-            return gu_ref.at[piece, target]
-        return block(None, d_ref.at[target], piece, group)
+            return gu_all.at[piece, shard]
+        return block(None, gd_all.at[shard], piece, group)
+
+    def each(span, body):
+        group, lo, hi = span
+
+        def step(piece, carry):
+            body(piece, group)
+            return carry
+
+        lax.fori_loop(lo, hi, step, 0)
 
     def to_sibling(quad, piece, group):
         return remote(
-            stored(2 * quad + 1 - core, piece, group),
-            block(gu_sib.at[quad], d_sib.at[quad], piece, group),
+            own_block(quad, piece, group, theirs=True),
+            block(gu_sib.at[quad], gd_sib.at[quad], piece, group),
             c_send.at[quad, piece],
             c_recv.at[quad, piece],
             sibling,
         )
 
-    def loading(quad, piece, group):
-        return pltpu.make_async_copy(
-            stored(2 * quad + core, piece, group),
-            block(gu_own.at[quad], d_own.at[quad], piece, group),
-            load.at[quad, piece],
-        )
-
     def to_second(quad, slot, piece, group):
         return remote(
-            block(gu_own.at[quad], d_own.at[quad], piece, group),
-            block(gu_sec.at[slot], d_sec.at[slot], piece, group),
+            own_block(quad, piece, group),
+            block(gu_sec.at[slot], gd_sec.at[slot], piece, group),
             s_send.at[slot, piece],
             s_recv.at[slot, piece],
             second,
@@ -638,127 +780,388 @@
 
     def to_first(piece, group):
         return remote(
-            block(gu_own.at[fst], d_own.at[fst], piece, group),
-            block(gu_fst, d_fst, piece, group),
+            own_block(fst, piece, group),
+            block(gu_fst, gd_fst, piece, group),
             f_send.at[piece],
             f_recv.at[piece],
             first,
         )
 
-    def send_line(src, which, target, up):
-        landing, sends, lands = (t_up, up_s, up_r) if up else (t_down, down_s, down_r)
-        return remote(
-            src,
-            landing.at[which, target],
-            sends.at[which, target],
-            lands.at[which, target],
-            me + RING if up else me - RING,
-        )
-
-    tokens = [
-        pltpu.make_async_copy(ref, t_own.at[which], t_load.at[which])
-        for which, ref in enumerate((ds_ref, y_ref))
-    ]
-    for copy in tokens:
-        copy.start()
-    for theirs, own in ((far, far), (fst, sec), (sec, fst), (mine, mine)):
-
-        def begin(piece, group, theirs=theirs, own=own):
-            to_sibling(theirs, piece, group).start()
-            loading(own, piece, group).start()
-
-        each(begin)
-    for copy in tokens:
-        copy.wait()
-    for k in range(last):
-        for which in range(2):
-
-            @pl.when(z == last)
-            def _(k=k, which=which):
-                send_line(t_own.at[which, k], which, k, False).start()
-
-            @pl.when(z == 0)
-            def _(k=k, which=which):
-                send_line(t_own.at[which, last - k], which, last - k, True).start()
-
-    def relay(target, which, up):
-        @pl.when((target > z) & (z > 0) if up else (target < z) & (z < last))
-        def _():
-            landing = (t_up if up else t_down).at[which, target]
-            send_line(landing, which, target, up).wait_recv()
-            add_rows(landing, landing, t_own.at[which, target])
-            send_line(landing, which, target, up).start()
-
-    for quad, slot in ((far, 1), (sec, 0)):
-
-        def pass_on(piece, group, quad=quad, slot=slot):
-            loading(quad, piece, group).wait()
+    def pass_on(piece, group):
+        for quad, slot in ((far, 1), (sec, 0)):
             to_sibling(quad, piece, group).wait_recv()
-            own = block(gu_own.at[quad], d_own.at[quad], piece, group)
-            add_rows(own, own, block(gu_sib.at[quad], d_sib.at[quad], piece, group))
+            own = own_block(quad, piece, group)
+            add_rows(own, own, block(gu_sib.at[quad], gd_sib.at[quad], piece, group))
             to_second(quad, slot, piece, group).start()
 
-        each(pass_on)
-    for which in range(2):
-        relay(0, which, False)
-        relay(last, which, True)
-
     def narrow(piece, group):
-        loading(fst, piece, group).wait()
         to_sibling(fst, piece, group).wait_recv()
         to_second(far, 1, piece, group).wait_recv()
-        own = block(gu_own.at[fst], d_own.at[fst], piece, group)
+        own = own_block(fst, piece, group)
         add_rows(
             own,
             own,
-            block(gu_sib.at[fst], d_sib.at[fst], piece, group),
-            block(gu_sec.at[1], d_sec.at[1], piece, group),
+            block(gu_sib.at[fst], gd_sib.at[fst], piece, group),
+            block(gu_sec.at[1], gd_sec.at[1], piece, group),
         )
         to_first(piece, group).start()
 
-    each(narrow)
-    for k in range(1, last):
-        for which in range(2):
-            relay(k, which, False)
-            relay(last - k, which, True)
-
     def finish(piece, group):
-        loading(mine, piece, group).wait()
         to_sibling(mine, piece, group).wait_recv()
         to_second(sec, 0, piece, group).wait_recv()
         to_first(piece, group).wait_recv()
+        own = own_block(mine, piece, group)
         add_rows(
-            block(gu_out, d_out, piece, group),
-            block(gu_own.at[mine], d_own.at[mine], piece, group),
-            block(gu_sib.at[mine], d_sib.at[mine], piece, group),
-            block(gu_sec.at[0], d_sec.at[0], piece, group),
-            block(gu_fst, d_fst, piece, group),
+            own if group == 0 else block(None, d_out, piece, group),
+            own,
+            block(gu_sib.at[mine], gd_sib.at[mine], piece, group),
+            block(gu_sec.at[0], gd_sec.at[0], piece, group),
+            block(gu_fst, gd_fst, piece, group),
         )
 
-    each(finish)
-    for which, out in enumerate((ds_out, y_out)):
-        own = t_own.at[which, z]
-        above, below = t_down.at[which, z], t_up.at[which, z]
+    def send_line(src, which, t, up):
+        return remote(
+            src,
+            t_land.at[which, t + 1 if up else t],
+            (up_s if up else down_s).at[which, t],
+            (up_r if up else down_r).at[which, t],
+            me + RING if up else me - RING,
+        )
+
+    def line_own(which):
+        for k in range(last):
+
+            @pl.when(z == last)
+            def _(k=k):
+                send_line(t_own.at[which, k], which, k, False).start()
+
+            @pl.when(z == 0)
+            def _(k=k):
+                send_line(t_own.at[which, last - k], which, last - k, True).start()
+
+    def relay_at(which, at, t, up):
+        @pl.when(z == at)
+        def _():
+            landing = t_land.at[which, t + 1 if up else t]
+            send_line(landing, which, t, up).wait_recv()
+            add_rows(landing, landing, t_own.at[which, t])
+            send_line(landing, which, t, up).start()
+
+    def relay(which, step):
+        if step < 2:
+            relay_at(which, 2, step, False)
+            relay_at(which, 1, last - step, True)
+        else:
+            relay_at(which, 1, 0, False)
+            relay_at(which, 2, last, True)
+
+    def line_sum(which, out):
+        own, above, below = t_own.at[which, z], t_land.at[which, z], t_land.at[which, z + 1]
 
         @pl.when(z < last)
-        def _(which=which, above=above):
+        def _():
             send_line(above, which, z, False).wait_recv()
 
         @pl.when(z > 0)
-        def _(which=which, below=below):
+        def _():
             send_line(below, which, z, True).wait_recv()
 
         @pl.when(z == 0)
-        def _(out=out, own=own, above=above):
+        def _():
             add_rows(out, own, above)
 
         @pl.when(z == last)
-        def _(out=out, own=own, below=below):
+        def _():
             add_rows(out, own, below)
 
         @pl.when((z > 0) & (z < last))
-        def _(out=out, own=own, above=above, below=below):
+        def _():
             add_rows(out, own, above, below)
+
+    def mlp(tok, cot, hid, dgu):
+        ins = [
+            pltpu.make_async_copy(hid_ref, hid, load.at[0]),
+            pltpu.make_async_copy(cot_ref, cot, load.at[1]),
+            pltpu.make_async_copy(dgu_ref, dgu, load.at[2]),
+            pltpu.make_async_copy(tok_ref, tok, load.at[3]),
+        ]
+        for copy in ins:
+            copy.start()
+        wide = 256
+        for copy in ins[:2]:
+            copy.wait()
+
+        previous = None
+        for quad in (far, sec, fst, mine):
+
+            def columns(n, carry, quad=quad):
+                at = tile(n, 512)
+                both = dot_tn(hid[:, tile(quad, quad_rows)], cot[:, at]).astype(bf16)
+                gd_all[2 * quad, :, at] = both[: quad_rows // 2]
+                gd_all[2 * quad + 1, :, at] = both[quad_rows // 2 :]
+                return carry
+
+            lax.fori_loop(0, dim // 512, columns, 0)
+            if previous is not None:
+                each(MLP_D, lambda piece, group, q=previous: to_sibling(q, piece, group).start())
+            previous = quad
+
+        def back_through(rows_w):
+            def fetch(i, slot):
+                return (
+                    pltpu.make_async_copy(
+                        gu_ref.at[tile(i, wide)], rows_w.at[slot], stream.at[slot, 0]
+                    ),
+                )
+
+            def body(i, slot):
+                out = dot_nt(dgu[...], rows_w[slot]).astype(bf16)
+                t_own[0, :, :, tile(i, wide)] = out.reshape(LINE, CAP, wide)
+
+            streamed(dim // wide, fetch, body)
+
+        each(MLP_D, lambda piece, group, q=previous: to_sibling(q, piece, group).start())
+        for copy in ins[2:]:
+            copy.wait()
+        pl.run_scoped(back_through, pltpu.VMEM((2, wide, 2 * part), bf16))
+        each(MLP_D, pass_on)
+        line_own(0)
+
+        rows = dim // LINE
+        for piece in range(LINE):
+
+            def columns(n, carry, piece=piece):
+                at = tile(n, 512)
+                grad = dot_tn(tok[:, pl.ds(piece * rows, rows)], dgu[:, at]).astype(bf16)
+                gu_all[piece, :, :, at] = grad.reshape(RING, rows // RING, 512)
+                return carry
+
+            lax.fori_loop(0, 2 * part // 512, columns, 0)
+            if piece > 0:
+                pass_on(piece - 1, 0)
+            for quad in (far, fst, sec, mine):
+                to_sibling(quad, piece, 0).start()
+        each(MLP_D, narrow)
+        relay(0, 0)
+
+        def out_through(cols_w):
+            def fetch(i, slot):
+                return (
+                    pltpu.make_async_copy(
+                        wd_ref.at[:, tile(i, wide)], cols_w.at[slot], stream.at[slot, 0]
+                    ),
+                )
+
+            def body(i, slot):
+                out = jnp.dot(hid[...], cols_w[slot], preferred_element_type=f32).astype(bf16)
+                t_own[1, :, :, tile(i, wide)] = out.reshape(LINE, CAP, wide)
+
+            streamed(dim // wide, fetch, body)
+
+        pass_on(LINE - 1, 0)
+        pl.run_scoped(out_through, pltpu.VMEM((2, part, wide), bf16))
+
+    pl.run_scoped(
+        mlp,
+        pltpu.VMEM((tokens, dim), bf16),
+        pltpu.VMEM((tokens, dim), bf16),
+        pltpu.VMEM((tokens, part), bf16),
+        pltpu.VMEM((tokens, 2 * part), bf16),
+    )
+
+    def attention(middle, raw, q, k, v, mixed, normed, cot, dsec, dbr, dmix, w_rows, o_stage, q_stage):
+        kv0 = H * HD
+        v0 = kv0 + KVH * HD
+        ins = [
+            pltpu.make_async_copy(src, dst, load.at[i])
+            for i, (src, dst) in enumerate(
+                (
+                    (middle_ref, middle),
+                    (raw_ref.at[:, pl.ds(0, v0)], raw),
+                    (q_ref, q),
+                    (k_ref, k),
+                    (v_ref, v),
+                    (mixed_ref, mixed),
+                    (normed_ref, normed),
+                    (cot_ref.at[tile(z, CAP)], cot),
+                )
+            )
+        ]
+        for copy in ins:
+            copy.start()
+        relay(0, 1)
+        narrow(0, 0)
+        relay(0, 2)
+        line_own(1)
+        for copy in ins:
+            copy.wait()
+        line_sum(0, dsec)
+
+        scale = rms_scale(middle[...])
+        wide = 512
+
+        def gather_mean(i, total):
+            at = tile(i, wide)
+            n = middle[:, at] * scale
+            ds = dsec[:, at]
+            small_out[0:1, at] = jnp.sum(n * ds, axis=0, keepdims=True)
+            return total + lane_sum(n * ds * gains_ref[1:2, at])
+
+        mean = lax.fori_loop(0, dim // wide, gather_mean, jnp.zeros((CAP, 1), f32)) / dim
+
+        def spread_mean(i, carry):
+            at = tile(i, wide)
+            n = middle[:, at] * scale
+            e = dsec[:, at] * gains_ref[1:2, at]
+            d_middle = cot[:, at].astype(f32) + scale * (e - n * mean)
+            dmid_out[:, at] = d_middle
+            dbr[:, at] = d_middle.astype(bf16)
+            return carry
+
+        lax.fori_loop(0, dim // wide, spread_mean, 0)
+        shards = w_rows.shape[1]
+        rows = shards * w_rows.shape[2]
+
+        def w_fetch(i, slot):
+            return (
+                pltpu.make_async_copy(
+                    w_ref.at[tile(i, shards), :, pl.ds(v0 + KVH * HD, dim)],
+                    w_rows.at[slot],
+                    stream.at[slot, 0],
+                ),
+            )
+
+        def o_back(i, slot):
+            return pltpu.make_async_copy(
+                o_stage.at[slot], go_out.at[tile(i, shards)], back.at[slot]
+            )
+
+        def through_out(i, slot):
+            dmix[:, tile(i, rows)] = dot_nt(dbr[...], w_rows[slot].reshape(rows, dim)).astype(bf16)
+
+            @pl.when(i > 1)
+            def _():
+                o_back(i - 2, slot).wait()
+
+            def columns(n, carry):
+                at = tile(n, 512)
+                grad = dot_tn(mixed[:, tile(i, rows)], dbr[:, at]).astype(bf16)
+                o_stage[slot, :, :, at] = grad.reshape(shards, rows // shards, 512)
+                return carry
+
+            lax.fori_loop(0, dim // 512, columns, 0)
+            o_back(i, slot).start()
+
+        count = dim // rows
+        streamed(count, w_fetch, through_out)
+        narrow(1, 0)
+        relay(1, 0)
+        for i in (count - 2, count - 1):
+            o_back(i, i % 2).wait()
+
+        cosine, sine, bias = rope_ref[0], rope_ref[1], rope_ref[2]
+        small_out[1:8] = jnp.zeros((7, dim), f32)
+
+        def unrope(raw_v, d_rot, row):
+            d_hat = d_rot * cosine - half_turn(d_rot * sine)
+            r = rms_scale(raw_v)
+            n = raw_v * r
+            small_out[row : row + 1, 0:HD] += jnp.sum(n * d_hat, axis=0, keepdims=True)
+            e = d_hat * gains_ref[row + 1 : row + 2, 0:HD]
+            return (r * (e - n * jnp.mean(n * e, axis=-1, keepdims=True))).astype(bf16)
+
+        def head(g, carry):
+            at = tile(g, HD)
+            key, value = k[:, at], v[:, at]
+            d_key = jnp.zeros((CAP, HD), f32)
+            d_value = jnp.zeros((CAP, HD), f32)
+            for i in range(2):
+                cols = tile(2 * g + i, HD)
+                query, d_mix = q[:, cols], dmix[:, cols]
+                logits = dot_nt(query, key) * (HD ** (-0.5)) + bias
+                exponent = jnp.exp(logits - jnp.max(logits, axis=-1, keepdims=True))
+                probs = exponent / lane_sum(exponent)
+                d_probs = dot_nt(d_mix, value)
+                d_logits = probs * (d_probs - lane_sum(probs * d_probs))
+                d_scores = (d_logits * (HD ** (-0.5))).astype(bf16)
+                d_value = d_value + dot_tn(probs.astype(bf16), d_mix)
+                d_key = d_key + dot_tn(d_scores, query)
+                d_query = jnp.dot(d_scores, key, preferred_element_type=f32)
+                dqkv_out[:, cols] = unrope(raw[:, cols], d_query, 1)
+            cols = pl.ds(pl.multiple_of(kv0 + g * HD, HD), HD)
+            dqkv_out[:, cols] = unrope(raw[:, cols], d_key, 2)
+            dqkv_out[:, pl.ds(pl.multiple_of(v0 + g * HD, HD), HD)] = d_value.astype(bf16)
+            return carry
+
+        lax.fori_loop(0, KVH // 2, head, 0)
+        narrow(2, 0)
+        relay(1, 1)
+        lax.fori_loop(KVH // 2, KVH, head, 0)
+        narrow(3, 0)
+        relay(1, 2)
+        each(MLP_D, finish)
+
+        q_shards = q_stage.shape[1]
+        q_rows = q_shards * q_stage.shape[2]
+
+        def q_back(i, slot):
+            return pltpu.make_async_copy(
+                q_stage.at[slot], gq_out.at[tile(i, q_shards)], back.at[slot]
+            )
+
+        def rows_of(i, carry):
+            slot = i % 2
+
+            @pl.when(i > 1)
+            def _():
+                q_back(i - 2, slot).wait()
+
+            def columns(n, inner):
+                at = tile(n, 512)
+                grad = dot_tn(normed[:, tile(i, q_rows)], dqkv_out[:, at]).astype(bf16)
+                q_stage[slot, :, :, at] = grad.reshape(q_shards, q_rows // q_shards, 512)
+                return inner
+
+            lax.fori_loop(0, dqkv_out.shape[1] // 512, columns, 0)
+            q_back(i, slot).start()
+            return carry
+
+        count = dim // q_rows
+        lax.fori_loop(0, count, rows_of, 0)
+        for i in (count - 2, count - 1):
+            q_back(i, i % 2).wait()
+        line_sum(1, dsec)
+
+        def last_add(i, carry):
+            at = tile(i, wide)
+            y_out[:, at] = (middle[:, at] + dsec[:, at]).astype(bf16)
+            return carry
+
+        lax.fori_loop(0, dim // wide, last_add, 0)
+
+    slots = CAP
+    kv = KVH * HD
+    rows = gu_all.shape[2]
+    pl.run_scoped(
+        attention,
+        pltpu.VMEM((slots, dim), f32),
+        pltpu.VMEM((slots, dim + kv), f32),
+        pltpu.VMEM((slots, dim), bf16),
+        pltpu.VMEM((slots, kv), bf16),
+        pltpu.VMEM((slots, kv), bf16),
+        pltpu.VMEM((slots, dim), bf16),
+        pltpu.VMEM((slots, dim), bf16),
+        pltpu.VMEM((slots, dim), bf16),
+        pltpu.VMEM((slots, dim), f32),
+        pltpu.VMEM((slots, dim), bf16),
+        pltpu.VMEM((slots, dim), bf16),
+        pltpu.VMEM((2, 4, rows, dim), bf16),
+        pltpu.VMEM((2, 4, rows, dim), bf16),
+        pltpu.VMEM((2, 2, rows, dim + 2 * kv), bf16),
+    )
+    each(MLP_GU, finish)
+    gu_back = pltpu.make_async_copy(gu_all.at[:, 2 * mine + core], gu_out, back.at[0])
+    gu_back.start()
 
     def drain(piece, group):
         for quad in (far, fst, sec, mine):
@@ -767,49 +1170,57 @@
         to_second(sec, 0, piece, group).wait_send()
         to_first(piece, group).wait_send()
 
-    each(drain)
+    each(MLP_GU, drain)
+    each(MLP_D, drain)
     for which in range(2):
         for k in range(LINE):
 
             @pl.when((z > 0) & (k < z))
             def _(which=which, k=k):
-                send_line(t_down.at[which, k], which, k, False).wait_send()
+                send_line(t_own.at[which, k], which, k, False).wait_send()
 
             @pl.when((z < last) & (k > z))
             def _(which=which, k=k):
-                send_line(t_up.at[which, k], which, k, True).wait_send()
-
-
-def reduce_mlp(gu, d, ds, y):
-    rows, cols = gu.shape[2:]
-    drows, dcols = d.shape[1:]
-    tok = ds.shape[1:]
+                send_line(t_own.at[which, k], which, k, True).wait_send()
+
+    gu_back.wait()
+
+
+def turn(gu, wd, tok, cot, hid, dgu, w, middle, normed, raw, q, k, v, mixed, gains, rope):
+    dim = tok.shape[1]
+    rows = w.shape[1]
+    drows = wd.shape[0] // RING
+    cols = gu.shape[1]
     quads = RING // 2
     pieces = LINE + 2
+    n = RING * LINE
+    qkv = raw.shape[1]
+    S = jax.ShapeDtypeStruct
     return pl.pallas_call(
-        reduce_mlp_kernel,
+        turn_kernel,
         out_shape=(
-            jax.ShapeDtypeStruct((LINE, rows, cols), bf16),
-            jax.ShapeDtypeStruct((drows, dcols), f32),
-            jax.ShapeDtypeStruct(tok, f32),
-            jax.ShapeDtypeStruct(tok, f32),
+            S((CAP, dim), bf16),
+            S((CAP, dim), f32),
+            S((CAP, qkv), bf16),
+            S((8, dim), f32),
+            S((drows, dim), f32),
+            S((LINE, rows, cols), bf16),
+            S((n, rows, qkv), bf16),
+            S((n, rows, dim), bf16),
         ),
-        in_specs=[ANY] * 4,
-        out_specs=(VMEM,) * 4,
+        in_specs=[ANY] * 14 + [VMEM] * 2,
+        out_specs=(VMEM,) * 5 + (ANY,) * 3,
         scratch_shapes=[
+            pltpu.VMEM((LINE, RING, rows, cols), bf16),
+            pltpu.VMEM((RING, drows, dim), bf16),
             pltpu.VMEM((quads, LINE, rows, cols), bf16),
-            pltpu.VMEM((quads, LINE, rows, cols), bf16),
+            pltpu.VMEM((quads, drows, dim), bf16),
             pltpu.VMEM((2, LINE, rows, cols), bf16),
+            pltpu.VMEM((2, drows, dim), bf16),
             pltpu.VMEM((LINE, rows, cols), bf16),
-            pltpu.VMEM((quads, drows, dcols), bf16),
-            pltpu.VMEM((quads, drows, dcols), bf16),
-            pltpu.VMEM((2, drows, dcols), bf16),
-            pltpu.VMEM((drows, dcols), bf16),
-            pltpu.VMEM((2, LINE) + tok, bf16),
-            pltpu.VMEM((2, LINE) + tok, bf16),
-            pltpu.VMEM((2, LINE) + tok, bf16),
-            DMA((quads, pieces)),
-            DMA((2,)),
+            pltpu.VMEM((drows, dim), bf16),
+            pltpu.VMEM((2, LINE, CAP, dim), bf16),
+            pltpu.VMEM((2, LINE + 1, CAP, dim), bf16),
             DMA((quads, pieces)),
             DMA((quads, pieces)),
             DMA((2, pieces)),
@@ -820,19 +1231,23 @@
             DMA((2, LINE)),
             DMA((2, LINE)),
             DMA((2, LINE)),
+            DMA((8,)),
+            DMA((2, 3)),
+            DMA((2,)),
         ],
         compiler_params=pltpu.CompilerParams(
-            collective_id=2, has_side_effects=True, vmem_limit_bytes=64000 * 1024
+            collective_id=2, has_side_effects=True, vmem_limit_bytes=65400 * 1024
         ),
-        name="reduce_mlp",
-    )(gu, d, ds, y)
-
-
-def reduce_attn_kernel(
-    a_ref, o_ref, gu_ref, s_ref, q_out, k_out, v_out, o_out, gate_out, up_out, s_out,
-    own, sib, sec, fst, down, up, ex, s_sum, s_got, s_line,
+        name="turn",
+    )(gu, wd, tok, cot, hid, dgu, w, middle, normed, raw, q, k, v, mixed, gains, rope)
+
+
+def close_kernel(
+    a_ref, o_ref, gu_ref, w_ref, s_ref, x_ref, dmid_ref, dqkv_ref, gains_ref,
+    q_out, k_out, v_out, o_out, gate_out, up_out, s_out, x_out,
+    own, sib, sec, fst, down, up, ex, s_sum, s_got, s_line, w_rows,
     load, ex_load, c_send, c_recv, s_send, s_recv, f_send, f_recv, down_s, down_r, up_s, up_r,
-    ex_s, ex_r, small_s, small_r,
+    ex_s, ex_r, small_s, small_r, stream,
 ):
     me, z, first, second, sibling = where_am_i()
     greet(line_peers(me) + [first, second, sibling])
@@ -892,8 +1307,7 @@
     def small(step, src, dst, device):
         return remote(src, dst, small_s.at[step], small_r.at[step], device)
 
-    small_c = small(0, s_ref, s_got.at[0], sibling)
-    small_c.start()
+    small_c = small(0, s_sum.at[3], s_got.at[0], sibling)
     for k in range(1, LINE):
         exchange(k).start()
     ex_in = pltpu.make_async_copy(gu_ref.at[z], ex.at[z], ex_load)
@@ -946,18 +1360,58 @@
             add_rows(landing, landing, own.at[t, q_mine])
             send_line(landing, t, True).start()
 
+    shards = w_rows.shape[1]
+    dim = x_ref.shape[1]
+
+    def first_norm():
+        wide = 512
+        x_scale = rms_scale(x_ref[...].astype(f32))
+        w_tile = shards * w_rows.shape[2]
+
+        def w_fetch(i, slot):
+            return (
+                pltpu.make_async_copy(
+                    w_ref.at[tile(i, shards), :, pl.ds(0, split)], w_rows.at[slot], stream.at[slot]
+                ),
+            )
+
+        def through(i, slot):
+            x_out[:, tile(i, w_tile)] = dot_nt(dqkv_ref[...], w_rows[slot].reshape(w_tile, split))
+
+        streamed(dim // w_tile, w_fetch, through)
+        s_sum[3] = s_ref[...]
+
+        def gather_mean(i, total):
+            at = tile(i, wide)
+            n = x_ref[:, at].astype(f32) * x_scale
+            s_sum[3, 3:4, at] = jnp.sum(n * x_out[:, at], axis=0, keepdims=True)
+            return total + lane_sum(n * x_out[:, at] * gains_ref[0:1, at])
+
+        mean = lax.fori_loop(0, dim // wide, gather_mean, jnp.zeros((CAP, 1), f32)) / dim
+
+        def spread_mean(i, carry):
+            at = tile(i, wide)
+            n = x_ref[:, at].astype(f32) * x_scale
+            e = x_out[:, at] * gains_ref[0:1, at]
+            x_out[:, at] = dmid_ref[:, at] + x_scale * (e - n * mean)
+            return carry
+
+        lax.fori_loop(0, dim // wide, spread_mean, 0)
+
     spread(order[0])
+    first_norm()
+    spread(order[1])
+    small_c.start()
+    narrow(order[0])
     small_c.wait()
-    s_sum[0] = s_ref[...] + s_got[0]
+    s_sum[0] = s_sum[3] + s_got[0]
     small_f = small(1, s_sum.at[0], s_got.at[1], first)
     small_f.start()
-    spread(order[1])
-    narrow(order[0])
+    spread(order[2])
     small_f.wait()
     s_sum[1] = s_sum[0] + s_got[1]
     small_s2 = small(2, s_sum.at[1], s_got.at[2], second)
     small_s2.start()
-    spread(order[2])
     narrow(order[1])
     collect(order[0])
     small_s2.wait()
@@ -977,8 +1431,8 @@
     narrow(order[3])
     collect(order[2])
     relay(order[1])
+    relay(order[2])
     collect(order[3])
-    relay(order[2])
     ex_in.wait()
     for k in range(1, LINE):
         src_z = lax.rem(z + LINE - k, LINE)
@@ -1039,26 +1493,28 @@
             send_line(up.at[t], t, True).wait_send()
 
 
-def reduce_attn(a, o, gu, small):
+def close(a, o, gu, w, small, x, dmid, dqkv, gains):
     rows, split = a.shape[1:]
     owide = o.shape[2]
     wide = split + owide
     quads = RING // 2
     width = gu.shape[2] // 2
     kv = KVH * HD
+    S = jax.ShapeDtypeStruct
     return pl.pallas_call(
-        reduce_attn_kernel,
+        close_kernel,
         out_shape=(
-            jax.ShapeDtypeStruct((rows, H * HD), f32),
-            jax.ShapeDtypeStruct((rows, kv), f32),
-            jax.ShapeDtypeStruct((rows, kv), f32),
-            jax.ShapeDtypeStruct((rows, owide), f32),
-            jax.ShapeDtypeStruct((rows, LINE * width), f32),
-            jax.ShapeDtypeStruct((rows, LINE * width), f32),
-            jax.ShapeDtypeStruct(small.shape, f32),
+            S((rows, H * HD), f32),
+            S((rows, kv), f32),
+            S((rows, kv), f32),
+            S((rows, owide), f32),
+            S((rows, LINE * width), f32),
+            S((rows, LINE * width), f32),
+            S(small.shape, f32),
+            S(x.shape, f32),
         ),
-        in_specs=[ANY, ANY, ANY, VMEM],
-        out_specs=(VMEM,) * 7,
+        in_specs=[ANY] * 4 + [VMEM] * 5,
+        out_specs=(VMEM,) * 8,
         scratch_shapes=[
             pltpu.VMEM((LINE, quads, rows, wide), bf16),
             pltpu.VMEM((LINE, quads, rows, wide), bf16),
@@ -1067,9 +1523,10 @@
             pltpu.VMEM((LINE, rows, wide), bf16),
             pltpu.VMEM((LINE, rows, wide), bf16),
             pltpu.VMEM((LINE, rows, 2 * width), bf16),
-            pltpu.VMEM((3,) + small.shape, f32),
+            pltpu.VMEM((4,) + small.shape, f32),
             pltpu.VMEM((3,) + small.shape, f32),
             pltpu.VMEM((LINE,) + small.shape, f32),
+            pltpu.VMEM((2, 4, rows, split), bf16),
             DMA((LINE, quads, 2)),
             DMA,
             DMA((LINE, quads, 2)),
@@ -1086,12 +1543,13 @@
             DMA((LINE,)),
             DMA((2 + LINE,)),
             DMA((2 + LINE,)),
+            DMA((2,)),
         ],
         compiler_params=pltpu.CompilerParams(
-            collective_id=3, has_side_effects=True, vmem_limit_bytes=64000 * 1024
+            collective_id=3, has_side_effects=True, vmem_limit_bytes=65400 * 1024
         ),
-        name="reduce_attn",
-    )(a, o, gu, small)
+        name="close",
+    )(a, o, gu, w, small, x, dmid, dqkv, gains)
 
 
 def layout(seq_lengths, seq_device, owner, slots):
@@ -1332,124 +1790,31 @@
     w_up,
     w_down,
 ):
-    slots, width = hidden_in.shape
-    groups = H // KVH
-    score_scale = HD ** (-0.5)
-    n = RING * LINE
-    rows = w_query.shape[0]
+    (
+        attn_w, gate_up_w, down_w, tokens, cotangent, hidden, d_gate_up,
+        middle, normed, qkv_raw, queries, keys, values, mixed, gains, rope,
+    ) = forward(
+        hidden_in, out_grad, seq_lengths, seq_device, (attn_gain, mlp_gain, q_gain, k_gain),
+        w_query, w_key, w_value, w_out, w_gate, w_up, w_down,
+    )
+    rows, dim = w_query.shape[0], hidden_in.shape[1]
+    hidden_out, d_middle, d_qkv, small, grad_down, g_gate_up, g_qkv, g_out = turn(
+        gate_up_w.reshape(-1, gate_up_w.shape[-1]),
+        down_w.reshape(-1, dim),
+        tokens.reshape(-1, dim),
+        cotangent.reshape(-1, dim),
+        hidden, d_gate_up, attn_w, middle, normed, qkv_raw, queries, keys, values, mixed, gains, rope,
+    )
+    g_query, g_key, g_value, g_out, g_gate, g_up, small, input_grad = close(
+        g_qkv, g_out, g_gate_up, attn_w, small, hidden_in, d_middle, d_qkv, gains
+    )
     me = lax.axis_index("fsdp")
-    segment, position = layout(seq_lengths, seq_device, me, slots)
-    allowed = allowed_pairs(segment)[None, None]
-    query_width = H * HD
-    qkv_width = query_width + 2 * KVH * HD
-    attn_width = qkv_width + w_out.shape[1]
-
-    def query_path(raw, gain):
-        return rotary(rmsnorm(raw.reshape(slots, H, HD), gain), position)
-
-    def key_path(raw, gain):
-        return rotary(rmsnorm(raw.reshape(slots, KVH, HD), gain), position)
-
-    def swiglu(gate_in, up_in):
-        return jax.nn.silu(gate_in) * up_in
-
-    lane = jnp.arange(128)[None, :]
-
-    def spread(gain, start, share):
-        placed = jnp.tile(gain, 128 // share)[None, :]
-        return jnp.where((lane >= start) & (lane < start + share), placed, 0)
-
-    pair = rows * (me % 2)
-    share = q_gain.shape[0]
-    gains = [spread(attn_gain, pair, rows), spread(mlp_gain, pair, rows)]
-    gains += [spread(q_gain, me * share, share), spread(k_gain, me * share, share)]
-    gains = jnp.pad(jnp.concatenate(gains, axis=0), ((0, rows - 4), (0, 0)))
-    (
-        attn_w, gate_up_w, down_w, tokens, cotangent,
-        middle, normed, qkv_raw, queries, keys, values, mixed, gains,
-    ) = forward(
-        hidden_in, out_grad, seq_lengths, seq_device, gains,
-        w_query, w_key, w_value, w_out, w_gate, w_up, w_down,
-    )
-    gain_attn, gain_mlp = gains[0], gains[1]
-    gain_query, gain_key = gains[2, :HD], gains[3, :HD]
-    attn_w = attn_w.reshape(n * rows, attn_w.shape[2])
-    qkv_w = attn_w[:, :qkv_width]
-    out_w = attn_w[:, qkv_width:attn_width]
-    inputs = hidden_in.astype(f32)
-    query_raw = qkv_raw[:, :query_width]
-    key_raw = qkv_raw[:, query_width : query_width + KVH * HD]
-    queries = queries.reshape(slots, KVH, groups, HD)
-    keys = keys.reshape(slots, KVH, HD)
-    values = values.reshape(slots, KVH, HD)
-    scores = jnp.einsum("qgrd,kgd->grqk", queries, keys, preferred_element_type=f32) * score_scale
-    logits = jnp.where(allowed, scores, masked_score)
-    exponent = jnp.exp(logits - jnp.max(logits, axis=-1, keepdims=True))
-    probs = exponent / jnp.sum(exponent, axis=-1, keepdims=True)
-    weights = probs.astype(bf16)
-
-    gate_up_w = gate_up_w.reshape(n * rows, gate_up_w.shape[-1])
-    down_w = down_w.reshape(-1, down_w.shape[-1])
-    tokens = tokens.reshape(-1, width)
-    cotangent = cotangent.reshape(-1, width)
-    part = gate_up_w.shape[1] // 2
-    gate_up = matmul(tokens, gate_up_w)
-    gate_out, up_out = gate_up[:, :part], gate_up[:, part:]
-    hidden = swiglu(gate_out, up_out).astype(bf16)
-    y_part = matmul(hidden, down_w).astype(bf16)
-    d_hidden = times_cols(cotangent, down_w)
-    unused_out, swiglu_pull = jax.vjp(swiglu, gate_out, up_out)
-    d_gate, d_up = swiglu_pull(d_hidden)
-    d_gate_up = jnp.concatenate([d_gate.astype(bf16), d_up.astype(bf16)], axis=1)
-    ds_part = times_cols(d_gate_up, gate_up_w).astype(bf16)
-    g_gate_up = times_rows(tokens, d_gate_up).astype(bf16)
-    g_down = times_rows(hidden, cotangent).astype(bf16)
-    g_gate_up, grad_down, d_second, y = reduce_mlp(
-        g_gate_up.reshape(LINE, RING, rows, 2 * part),
-        g_down.reshape(RING, w_down.shape[0], width),
-        ds_part.reshape(LINE, slots, width),
-        y_part.reshape(LINE, slots, width),
-    )
-    hidden_out = (middle + y).astype(bf16)
-
-    unused_norm, second_pull = jax.vjp(rmsnorm, middle, gain_mlp)
-    d_middle_norm, grad_gain_mlp = second_pull(d_second)
-    d_middle = out_grad.astype(f32) + d_middle_norm
-    d_branch = d_middle.astype(bf16)
-    g_out = times_rows(mixed, d_branch).astype(bf16)
-    d_mixed = times_cols(d_branch, out_w).astype(bf16).reshape(slots, KVH, groups, HD)
-    d_probs = jnp.einsum("qgrd,kgd->grqk", d_mixed, values, preferred_element_type=f32)
-    d_logits = probs * (d_probs - jnp.sum(probs * d_probs, axis=-1, keepdims=True))
-    d_scores = (d_logits * score_scale).astype(bf16)
-    d_values = jnp.einsum("grqk,qgrd->kgd", weights, d_mixed, preferred_element_type=f32)
-    d_values = d_values.astype(bf16).reshape(slots, KVH * HD)
-    d_queries_rot = jnp.einsum(
-        "grqk,kgd->qgrd", d_scores, keys, preferred_element_type=f32
-    ).reshape(slots, H, HD)
-    d_keys_rot = jnp.einsum("grqk,qgrd->kgd", d_scores, queries, preferred_element_type=f32)
-    unused_query, query_pull = jax.vjp(query_path, query_raw, gain_query)
-    d_query_raw, grad_gain_query = query_pull(d_queries_rot)
-    unused_key, key_pull = jax.vjp(key_path, key_raw, gain_key)
-    d_key_raw, grad_gain_key = key_pull(d_keys_rot)
-    d_qkv = jnp.concatenate([d_query_raw.astype(bf16), d_key_raw.astype(bf16), d_values], axis=1)
-    g_qkv = times_rows(normed, d_qkv).astype(bf16)
-    d_normed = times_cols(d_qkv, qkv_w)
-    unused_first, first_pull = jax.vjp(rmsnorm, inputs, gain_attn)
-    d_input_norm, grad_gain_attn = first_pull(d_normed)
-    input_grad = d_middle + d_input_norm
-    gain_grads = (grad_gain_attn, grad_gain_query, grad_gain_key, grad_gain_mlp)
-    small = jnp.concatenate(gain_grads)
-    small = jnp.pad(small, (0, -small.shape[0] % 1024)).reshape(-1, 128)
-    g_query, g_key, g_value, g_out, g_gate, g_up, small = reduce_attn(
-        g_qkv.reshape(n, rows, qkv_width), g_out.reshape(n, rows, w_out.shape[1]), g_gate_up, small
-    )
-    small = small.reshape(-1)
-    gain_sums = []
-    lo = 0
-    for grad in gain_grads:
-        share = grad.shape[0] // n
-        gain_sums.append(lax.dynamic_slice(small, (lo + me * share,), (share,)))
-        lo += grad.shape[0]
+
+    def share(row, grad_of):
+        count = grad_of.shape[0]
+        return lax.dynamic_slice(small, (row, me * count), (1, count))[0]
+
+    gain_sums = (share(3, attn_gain), share(1, q_gain), share(2, k_gain), share(0, mlp_gain))
     return (
         hidden_out,
         input_grad,

time: 577 us -> 480 us (0.83)
  matrix products: 95.3 us -> 0 us
  Pallas kernels: 429 us -> 463 us
  other arithmetic: 20.6 us -> 0 us
  local copies, waits for them, and re-layouts: 27 us -> 14.2 us
    dot_general x14 -> x0, matrix products: 92.9 us -> none  [the longest x4 34.6 us: times_cols(): lax.dot_general(left, right, contract_cols, preferred_element_type=jnp.fl...]
    pallas_call x2, Pallas kernels: 231 us -> 254 us  [the longest x1 128 us: close(): pl.pallas_call(close_kernel, out_shape=(S((rows, H * HD), f32), S((rows,...]
    pallas_call x1, Pallas kernels: 198 us -> 209 us  [forward(): pl.pallas_call(forward_kernel, out_shape=(S((n, rows, wide), bf16), S((LI...]
    reduce_sum x8 -> x0, other arithmetic: 7.78 us -> none  [the longest x3 6.77 us: rmsnorm(): values * lax.rsqrt(jnp.mean(values * values, axis=-1, keepdims=True) + ep...]
    unnamed x88 -> x23, local copies, waits for them, and re-layouts: 9.58 us -> 11.6 us
where the time goes in v3:
time: 480 us; the launch traced here: 478 us
  Pallas kernels  463 us (96%)
  local copies, waits for them, and re-layouts  14.2 us (3%)
    pallas_call x1, Pallas kernels, forward(): pl.pallas_call(forward_kernel, out_shape=(S((n, rows, wide), bf16), S((LI...  209 us
    pallas_call x1, Pallas kernels, close(): pl.pallas_call(close_kernel, out_shape=(S((rows, H * HD), f32), S((rows,...  128 us
    pallas_call x1, Pallas kernels, turn(): pl.pallas_call(turn_kernel, out_shape=(S((CAP, dim), bf16), S((CAP, dim),...  126 us
    unnamed x23, local copies, waits for them, and re-layouts  11.6 us

profile of v3, /device:TPU:8, one launch (start us, length us, event | category | flops | bytes accessed | tf_op | source)
XLA Modules:
  0.0 478.1 jit_solution(12815757054499598287)
XLA Ops:
  0.7 208.8 %forward.1 = (bf16[32,64,6272]{2,1,0:T(8,128)(2,1)}, bf16[4,8,64,3072]{3,2,1,0:T(8,128)(2,1)}, bf16[8,192,2048]{2,1,0:T(8,128)(2,1)}, bf16[4,128,2048]{2,1,0:T(8...) custom-call(bf16[128,2048]{1,0:T(8,128)(2,1)} %x_ref.3, ...), custom_call_target="tpu_custom_call" | custom-call | tf_op jit(solution)/shard_map/forward/pallas_call | solution.py:651
  209.5 126.3 %turn.1 = (bf16[128,2048]{1,0:T(8,128)(2,1)}, f32[128,2048]{1,0:T(8,128)}, bf16[128,4096]{1,0:T(8,128)(2,1)}, f32[8,2048]{1,0:T(8,128)}, f32[192,2048]{1,0:T(8,1...) custom-call(bf16[2048,3072]{1,0:T(8,128)(2,1)} %bitcast.18, ...), custom_call_target="tpu_custom_call" | custom-call | tf_op jit(solution)/shard_map/turn/pallas_call | solution.py:1199
  335.8 128.0 %close.1 = (f32[64,2048]{1,0:T(8,128)}, f32[64,1024]{1,0:T(8,128)}, f32[64,1024]{1,0:T(8,128)}, f32[64,2048]{1,0:T(8,128)}, f32[64,6144]{1,0:T(8,128)}, /*index=...) custom-call(bf16[32,64,4096]{2,1,0:T(8,128)(2,1)} %get-tuple-element.62.a_ref, ...), custom_call_target="tpu_custom_call" | custom-call | tf_op jit(solution)/shard_map/close/pallas_call | solution.py:1504
  463.8 0.0 copy-start.4
  463.8 1.3 dynamic-slice_bitcast_fusion
  465.1 1.3 dynamic-slice_bitcast_fusion.1
  466.5 0.0 copy-start.6
  466.5 1.9 copy.37
  468.4 0.0 copy-start.5
  468.4 0.0 copy-start.3
  468.4 2.4 copy.38
  470.8 0.0 copy-done.4
  470.8 0.0 copy-start.2
  470.8 0.8 copy.39
  471.6 0.0 copy-done.6
  471.6 0.7 copy.40
  472.3 0.0 copy-done.5
  472.3 0.7 copy.41
  473.0 0.0 copy-done.3
  473.0 0.0 copy-start.1
  473.0 0.8 copy.42
  473.8 0.0 copy-done.2
  473.8 1.1 copy.43
  474.9 0.0 copy-done.1
  474.9 0.0 copy-start
  474.9 1.1 copy.44
  476.1 0.8 copy-done
  476.9 1.1 copy.45
Async XLA Ops:
  463.8 7.0 %copy-start.4 = (f32[64,2048]{1,0:T(8,128)S(1)}, f32[64,2048]{1,0:T(8,128)}, u32[]{:S(2)}) copy-start(f32[64,2048]{1,0:T(8,128)} %get-tuple-element.99) | copy-start | bytes 1572868
  466.5 5.1 %copy-start.6 = (f32[64,1024]{1,0:T(8,128)S(1)}, f32[64,1024]{1,0:T(8,128)}, u32[]{:S(2)}) copy-start(f32[64,1024]{1,0:T(8,128)} %get-tuple-element.100) | copy-start | bytes 786436
  468.4 3.9 copy-start.5
  468.4 4.6 copy-start.3
  470.8 3.0 copy-start.2
  473.0 1.9 copy-start.1
  474.9 2.0 copy-start

commit v4 on v3

--- a/solution.py
+++ b/solution.py
@@ -720,16 +720,18 @@
     )
 
 
-def turn_kernel(
-    gu_ref, wd_ref, tok_ref, cot_ref, hid_ref, dgu_ref, w_ref, middle_ref, normed_ref, raw_ref, q_ref, k_ref, v_ref,
-    mixed_ref, gains_ref, rope_ref,
-    y_out, dmid_out, dqkv_out, small_out, d_out, gu_out, gq_out, go_out,
+def backward_kernel(
+    gu_ref, wd_ref, tok_ref, cot_ref, hid_ref, dgu_ref, w_ref, middle_ref, normed_ref, raw_ref,
+    q_ref, k_ref, v_ref, mixed_ref, x_ref, gains_ref, rope_ref,
+    x_out, small_out, y_out, d_out, a_out, ex_land, gu_out, c_land, s_land, f_land, l_land,
     gu_all, gd_all, gu_sib, gd_sib, gu_sec, gd_sec, gu_fst, gd_fst, t_own, t_land,
+    dmid, dqkv, s_sum, s_got, s_line,
     c_send, c_recv, s_send, s_recv, f_send, f_recv, down_s, down_r, up_s, up_r, load, stream, back,
+    ac_send, ac_recv, as_send, as_recv, af_send, af_recv, ad_send, ad_recv, au_send, au_recv,
+    ex_s, ex_r, small_s, small_r,
 ):
     me, z, first, second, sibling = where_am_i()
-    greet([lax.rem(me + RING, RING * LINE), lax.rem(me + RING * (LINE - 1), RING * LINE)]
-          + [first, second, sibling])
+    greet(line_peers(me) + [first, second, sibling])
     core = me % 2
     mine, fst, sec = (me % RING) // 2, (first % RING) // 2, (second % RING) // 2
     far = ((second + first - me) % RING) // 2
@@ -738,6 +740,11 @@
     tokens, dim = tok_ref.shape
     part = wd_ref.shape[0]
     quad_rows = part // LINE
+    shard_rows = dim // (RING * LINE)
+    piece_cols = gu_all.shape[3]
+    kv0 = H * HD
+    v0 = kv0 + KVH * HD
+    qkv_width = v0 + KVH * HD
     MLP_GU, MLP_D = (0, 0, LINE), (1, LINE, LINE + 2)
 
     def block(gu, d, piece, group):
@@ -806,18 +813,27 @@
         )
         to_first(piece, group).start()
 
-    def finish(piece, group):
+    def finish(piece, group, out=None):
         to_sibling(mine, piece, group).wait_recv()
         to_second(sec, 0, piece, group).wait_recv()
         to_first(piece, group).wait_recv()
         own = own_block(mine, piece, group)
         add_rows(
-            own if group == 0 else block(None, d_out, piece, group),
+            own if group == 0 else block(None, out, piece, group),
             own,
             block(gu_sib.at[mine], gd_sib.at[mine], piece, group),
             block(gu_sec.at[0], gd_sec.at[0], piece, group),
             block(gu_fst, gd_fst, piece, group),
         )
+
+    def drain_sibling(piece, group):
+        for quad in (far, fst, sec, mine):
+            to_sibling(quad, piece, group).wait_send()
+
+    def drain(piece, group):
+        to_second(far, 1, piece, group).wait_send()
+        to_second(sec, 0, piece, group).wait_send()
+        to_first(piece, group).wait_send()
 
     def send_line(src, which, t, up):
         return remote(
@@ -910,7 +926,7 @@
             def fetch(i, slot):
                 return (
                     pltpu.make_async_copy(
-                        gu_ref.at[tile(i, wide)], rows_w.at[slot], stream.at[slot, 0]
+                        gu_ref.at[tile(i, wide)], rows_w.at[slot], stream.at[slot]
                     ),
                 )
 
@@ -948,7 +964,7 @@
             def fetch(i, slot):
                 return (
                     pltpu.make_async_copy(
-                        wd_ref.at[:, tile(i, wide)], cols_w.at[slot], stream.at[slot, 0]
+                        wd_ref.at[:, tile(i, wide)], cols_w.at[slot], stream.at[slot]
                     ),
                 )
 
@@ -969,9 +985,7 @@
         pltpu.VMEM((tokens, 2 * part), bf16),
     )
 
-    def attention(middle, raw, q, k, v, mixed, normed, cot, dsec, dbr, dmix, w_rows, o_stage, q_stage):
-        kv0 = H * HD
-        v0 = kv0 + KVH * HD
+    def attention(dbr, raw, q, k, v, cot, dsec, dmix, middle, w_rows):
         ins = [
             pltpu.make_async_copy(src, dst, load.at[i])
             for i, (src, dst) in enumerate(
@@ -981,8 +995,6 @@
                     (q_ref, q),
                     (k_ref, k),
                     (v_ref, v),
-                    (mixed_ref, mixed),
-                    (normed_ref, normed),
                     (cot_ref.at[tile(z, CAP)], cot),
                 )
             )
@@ -1004,7 +1016,7 @@
             at = tile(i, wide)
             n = middle[:, at] * scale
             ds = dsec[:, at]
-            small_out[0:1, at] = jnp.sum(n * ds, axis=0, keepdims=True)
+            s_sum[3, 0:1, at] = jnp.sum(n * ds, axis=0, keepdims=True)
             return total + lane_sum(n * ds * gains_ref[1:2, at])
 
         mean = lax.fori_loop(0, dim // wide, gather_mean, jnp.zeros((CAP, 1), f32)) / dim
@@ -1014,7 +1026,7 @@
             n = middle[:, at] * scale
             e = dsec[:, at] * gains_ref[1:2, at]
             d_middle = cot[:, at].astype(f32) + scale * (e - n * mean)
-            dmid_out[:, at] = d_middle
+            dmid[:, at] = d_middle
             dbr[:, at] = d_middle.astype(bf16)
             return carry
 
@@ -1025,48 +1037,27 @@
         def w_fetch(i, slot):
             return (
                 pltpu.make_async_copy(
-                    w_ref.at[tile(i, shards), :, pl.ds(v0 + KVH * HD, dim)],
+                    w_ref.at[tile(i, shards), :, pl.ds(qkv_width, dim)],
                     w_rows.at[slot],
-                    stream.at[slot, 0],
+                    stream.at[slot],
                 ),
             )
 
-        def o_back(i, slot):
-            return pltpu.make_async_copy(
-                o_stage.at[slot], go_out.at[tile(i, shards)], back.at[slot]
-            )
-
         def through_out(i, slot):
             dmix[:, tile(i, rows)] = dot_nt(dbr[...], w_rows[slot].reshape(rows, dim)).astype(bf16)
 
-            @pl.when(i > 1)
-            def _():
-                o_back(i - 2, slot).wait()
-
-            def columns(n, carry):
-                at = tile(n, 512)
-                grad = dot_tn(mixed[:, tile(i, rows)], dbr[:, at]).astype(bf16)
-                o_stage[slot, :, :, at] = grad.reshape(shards, rows // shards, 512)
-                return carry
-
-            lax.fori_loop(0, dim // 512, columns, 0)
-            o_back(i, slot).start()
-
-        count = dim // rows
-        streamed(count, w_fetch, through_out)
+        streamed(dim // rows, w_fetch, through_out)
         narrow(1, 0)
         relay(1, 0)
-        for i in (count - 2, count - 1):
-            o_back(i, i % 2).wait()
 
         cosine, sine, bias = rope_ref[0], rope_ref[1], rope_ref[2]
-        small_out[1:8] = jnp.zeros((7, dim), f32)
+        s_sum[3, 1:8] = jnp.zeros((7, dim), f32)
 
         def unrope(raw_v, d_rot, row):
             d_hat = d_rot * cosine - half_turn(d_rot * sine)
             r = rms_scale(raw_v)
             n = raw_v * r
-            small_out[row : row + 1, 0:HD] += jnp.sum(n * d_hat, axis=0, keepdims=True)
+            s_sum[3, row : row + 1, 0:HD] += jnp.sum(n * d_hat, axis=0, keepdims=True)
             e = d_hat * gains_ref[row + 1 : row + 2, 0:HD]
             return (r * (e - n * jnp.mean(n * e, axis=-1, keepdims=True))).astype(bf16)
 
@@ -1087,91 +1078,416 @@
                 d_value = d_value + dot_tn(probs.astype(bf16), d_mix)
                 d_key = d_key + dot_tn(d_scores, query)
                 d_query = jnp.dot(d_scores, key, preferred_element_type=f32)
-                dqkv_out[:, cols] = unrope(raw[:, cols], d_query, 1)
+                dqkv[:, cols] = unrope(raw[:, cols], d_query, 1)
             cols = pl.ds(pl.multiple_of(kv0 + g * HD, HD), HD)
-            dqkv_out[:, cols] = unrope(raw[:, cols], d_key, 2)
-            dqkv_out[:, pl.ds(pl.multiple_of(v0 + g * HD, HD), HD)] = d_value.astype(bf16)
+            dqkv[:, cols] = unrope(raw[:, cols], d_key, 2)
+            dqkv[:, pl.ds(pl.multiple_of(v0 + g * HD, HD), HD)] = d_value.astype(bf16)
             return carry
 
         lax.fori_loop(0, KVH // 2, head, 0)
         narrow(2, 0)
+        lax.fori_loop(KVH // 2, KVH, head, 0)
+
+    order = (
+        last * (1 - z // 2),
+        2 - 2 * z + 5 * (z // 2),
+        1 + z % 2,
+        z,
+    )
+
+    def a_own(t, quad, h):
+        return gu_all.at[t, 2 * quad + (core if h else 1 - core)]
+
+    def sums(dbr, mixed, normed, cbuf, stage, w_rows):
+        ins = [
+            pltpu.make_async_copy(mixed_ref, mixed, load.at[0]),
+            pltpu.make_async_copy(normed_ref, normed, load.at[1]),
+        ]
+        for copy in ins:
+            copy.start()
+        for copy in ins:
+            copy.wait()
+        span = dim // LINE
+
+        def a_sibling(t, quad, h, slot):
+            return remote(
+                cbuf.at[slot, quad],
+                c_land.at[t, h, quad],
+                ac_send.at[slot, quad],
+                ac_recv.at[t, h, quad],
+                sibling,
+            )
+
+        def a_second(t, quad, h, slot):
+            return remote(
+                a_own(t, quad, h),
+                s_land.at[slot, t, h],
+                as_send.at[slot, t, h],
+                as_recv.at[slot, t, h],
+                second,
+            )
+
+        def a_first(t, h):
+            return remote(
+                a_own(t, fst, h), f_land.at[t, h], af_send.at[t, h], af_recv.at[t, h], first
+            )
+
+        def a_line(t, h, upward):
+            src = a_own(t, mine, h)
+            if upward:
+                return remote(
+                    src, l_land.at[1, t, h], au_send.at[t, h], au_recv.at[t, h], me + RING
+                )
+            return remote(src, l_land.at[0, t, h], ad_send.at[t, h], ad_recv.at[t, h], me - RING)
+
+        def absorb(own, *landed):
+            copies = [
+                pltpu.make_async_copy(src, stage.at[i], stream.at[i])
+                for i, src in enumerate(landed)
+            ]
+            for copy in copies:
+                copy.start()
+            for copy in copies:
+                copy.wait()
+            add_rows(own, own, *[stage.at[i] for i in range(len(landed))])
+
+        def compute(k):
+            h, t, slot = k // LINE, order[k % LINE], k % 2
+            if k > 1:
+                for quad in (far, fst, sec, mine):
+                    a_sibling(order[(k - 2) % LINE], quad, (k - 2) // LINE, slot).wait_send()
+            col0 = v0 if h else 0
+            own_core = core if h else 1 - core
+
+            def columns(n, carry, left, right, at):
+                grad = dot_tn(left[:, tile(t, span)], right).astype(bf16)
+                grad = grad.reshape(RING // 2, 2, shard_rows, 512)
+                ours = jnp.where(core == 0, grad[:, 0], grad[:, 1])
+                theirs = jnp.where(core == 0, grad[:, 1], grad[:, 0])
+                for quad in range(RING // 2):
+                    gu_all[t, 2 * quad + own_core, :, at] = ours[quad]
+                cbuf[slot, :, :, at] = theirs
+                return carry
+
+            def from_qkv(n, carry):
+                at = tile(n, 512)
+                right = dqkv[:, pl.ds(pl.multiple_of(col0 + n * 512, 512), 512)]
+                return columns(n, carry, normed, right, at)
+
+            def from_out(n, carry):
+                at = pl.ds(pl.multiple_of(qkv_width - v0 + n * 512, 512), 512)
+                return columns(n, carry, mixed, dbr[:, tile(n, 512)], at)
+
+            if h == 0:
+                lax.fori_loop(0, v0 // 512, from_qkv, 0)
+            else:
+                lax.fori_loop(0, (qkv_width - v0) // 512, from_qkv, 0)
+                lax.fori_loop(0, dim // 512, from_out, 0)
+
+        def share(k):
+            h, t, slot = k // LINE, order[k % LINE], k % 2
+            for quad in (far, fst, sec, mine):
+                a_sibling(t, quad, h, slot).start()
+
+        def spread(k):
+            h, t, slot = k // LINE, order[k % LINE], k % 2
+            for quad, place in ((far, 1), (sec, 0)):
+                a_sibling(t, quad, h, slot).wait_recv()
+                absorb(a_own(t, quad, h), c_land.at[t, h, quad])
+                a_second(t, quad, h, place).start()
+
+        def inward(k):
+            h, t, slot = k // LINE, order[k % LINE], k % 2
+            a_sibling(t, fst, h, slot).wait_recv()
+            a_second(t, far, h, 1).wait_recv()
+            absorb(a_own(t, fst, h), c_land.at[t, h, fst], s_land.at[1, t, h])
+            a_first(t, h).start()
+
+        def collect(k):
+            h, t, slot = k // LINE, order[k % LINE], k % 2
+            a_sibling(t, mine, h, slot).wait_recv()
+            a_second(t, sec, h, 0).wait_recv()
+            a_first(t, h).wait_recv()
+            absorb(a_own(t, mine, h), c_land.at[t, h, mine], s_land.at[0, t, h], f_land.at[t, h])
+
+            @pl.when((t < z) & (z == last))
+            def _():
+                a_line(t, h, False).start()
+
+            @pl.when((t > z) & (z == 0))
+            def _():
+                a_line(t, h, True).start()
+
+        def onward(k):
+            h, t = k // LINE, order[k % LINE]
+
+            @pl.when((t < z) & (z < last))
+            def _():
+                a_line(t, h, False).wait_recv()
+                absorb(a_own(t, mine, h), l_land.at[0, t, h])
+                a_line(t, h, False).start()
+
+            @pl.when((t > z) & (z > 0))
+            def _():
+                a_line(t, h, True).wait_recv()
+                absorb(a_own(t, mine, h), l_land.at[1, t, h])
+                a_line(t, h, True).start()
+
+        def exchange(k):
+            peer_z = lax.rem(z + k, LINE)
+            return remote(
+                gu_out.at[peer_z], ex_land.at[z], ex_s.at[k], ex_r.at[k], me % RING + RING * peer_z
+            )
+
+        def small(step, src, dst, device):
+            return remote(src, dst, small_s.at[step], small_r.at[step], device)
+
+        def first_norm():
+            shards = w_rows.shape[1]
+            wide = 512
+            x_scale = rms_scale(x_ref[...].astype(f32))
+            w_tile = shards * w_rows.shape[2]
+
+            def w_fetch(i, slot):
+                return (
+                    pltpu.make_async_copy(
+                        w_ref.at[tile(i, shards), :, pl.ds(0, qkv_width)],
+                        w_rows.at[slot],
+                        stream.at[slot],
+                    ),
+                )
+
+            def through(i, slot):
+                x_out[:, tile(i, w_tile)] = dot_nt(dqkv[...], w_rows[slot].reshape(w_tile, qkv_width))
+
+            streamed(dim // w_tile, w_fetch, through)
+
+            def gather_mean(i, total):
+                at = tile(i, wide)
+                n = x_ref[:, at].astype(f32) * x_scale
+                s_sum[3, 3:4, at] = jnp.sum(n * x_out[:, at], axis=0, keepdims=True)
+                return total + lane_sum(n * x_out[:, at] * gains_ref[0:1, at])
+
+            mean = lax.fori_loop(0, dim // wide, gather_mean, jnp.zeros((CAP, 1), f32)) / dim
+
+            def spread_mean(i, carry):
+                at = tile(i, wide)
+                n = x_ref[:, at].astype(f32) * x_scale
+                e = x_out[:, at] * gains_ref[0:1, at]
+                x_out[:, at] = dmid[:, at] + x_scale * (e - n * mean)
+                return carry
+
+            lax.fori_loop(0, dim // wide, spread_mean, 0)
+
+        small_c = small(0, s_sum.at[3], s_got.at[0], sibling)
+        each(MLP_GU, drain_sibling)
+        compute(0)
+        share(0)
+        narrow(3, 0)
+        spread(0)
+        compute(1)
+        share(1)
+        spread(1)
         relay(1, 1)
-        lax.fori_loop(KVH // 2, KVH, head, 0)
-        narrow(3, 0)
+        inward(0)
+        compute(2)
+        share(2)
+        spread(2)
+        inward(1)
         relay(1, 2)
-        each(MLP_D, finish)
-
-        q_shards = q_stage.shape[1]
-        q_rows = q_shards * q_stage.shape[2]
-
-        def q_back(i, slot):
-            return pltpu.make_async_copy(
-                q_stage.at[slot], gq_out.at[tile(i, q_shards)], back.at[slot]
-            )
-
-        def rows_of(i, carry):
-            slot = i % 2
-
-            @pl.when(i > 1)
-            def _():
-                q_back(i - 2, slot).wait()
-
-            def columns(n, inner):
-                at = tile(n, 512)
-                grad = dot_tn(normed[:, tile(i, q_rows)], dqkv_out[:, at]).astype(bf16)
-                q_stage[slot, :, :, at] = grad.reshape(q_shards, q_rows // q_shards, 512)
-                return inner
-
-            lax.fori_loop(0, dqkv_out.shape[1] // 512, columns, 0)
-            q_back(i, slot).start()
-            return carry
-
-        count = dim // q_rows
-        lax.fori_loop(0, count, rows_of, 0)
-        for i in (count - 2, count - 1):
-            q_back(i, i % 2).wait()
-        line_sum(1, dsec)
-
-        def last_add(i, carry):
-            at = tile(i, wide)
-            y_out[:, at] = (middle[:, at] + dsec[:, at]).astype(bf16)
-            return carry
-
-        lax.fori_loop(0, dim // wide, last_add, 0)
+        compute(3)
+        share(3)
+        spread(3)
+        each(MLP_GU, finish)
+        gu_back = pltpu.make_async_copy(gu_all.at[:, 2 * mine + core], gu_out, back.at[0])
+        gu_back.start()
+        collect(0)
+        inward(2)
+        gu_back.wait()
+        for k in range(1, LINE):
+            exchange(k).start()
+        ex_in = pltpu.make_async_copy(gu_all.at[z, 2 * mine + core], ex_land.at[z], back.at[1])
+        ex_in.start()
+        each(MLP_GU, drain)
+        ex_in.wait()
+        compute(4)
+        share(4)
+        spread(4)
+        collect(1)
+        onward(0)
+        first_norm()
+        inward(3)
+        small_c.start()
+        compute(5)
+        share(5)
+        spread(5)
+        collect(2)
+        onward(1)
+        small_c.wait()
+        s_sum[0] = s_sum[3] + s_got[0]
+        small_f = small(1, s_sum.at[0], s_got.at[1], first)
+        small_f.start()
+        inward(4)
+        compute(6)
+        share(6)
+        spread(6)
+        collect(3)
+        onward(2)
+        inward(5)
+        small_f.wait()
+        s_sum[1] = s_sum[0] + s_got[1]
+        small_s2 = small(2, s_sum.at[1], s_got.at[2], second)
+        small_s2.start()
+        compute(7)
+        share(7)
+        spread(7)
+        collect(4)
+        inward(6)
+        collect(5)
+        onward(4)
+        inward(7)
+        small_s2.wait()
+        s_sum[2] = s_sum[1] + s_got[2]
+        small_line = [
+            small(2 + k, s_sum.at[2], s_line.at[k], me % RING + RING * lax.rem(z + k, LINE))
+            for k in range(1, LINE)
+        ]
+        for copy in small_line:
+            copy.start()
+        collect(6)
+        onward(5)
+        onward(6)
+        collect(7)
+        for copy in small_line:
+            copy.wait()
+        small_out[...] = (s_sum[2] + s_line[2]) + (s_line[1] + s_line[3])
+        for k in (6, 7):
+            for quad in (far, fst, sec, mine):
+                a_sibling(order[k % LINE], quad, k // LINE, k % 2).wait_send()
+        for k in range(1, LINE):
+            exchange(k).wait_send()
+            src_z = lax.rem(z + LINE - k, LINE)
+            landed = ex_land.at[src_z]
+            remote(landed, landed, ex_s.at[k], ex_r.at[k], sibling).wait_recv()
+        for t in range(LINE):
+            for h in range(2):
+                a_second(t, far, h, 1).wait_send()
+                a_second(t, sec, h, 0).wait_send()
+                a_first(t, h).wait_send()
+
+                @pl.when(t < z)
+                def _(t=t, h=h):
+                    a_line(t, h, False).wait_send()
+
+                @pl.when(t > z)
+                def _(t=t, h=h):
+                    a_line(t, h, True).wait_send()
 
     slots = CAP
     kv = KVH * HD
     rows = gu_all.shape[2]
+
+    def both(dbr):
+        pl.run_scoped(
+            lambda *refs: attention(dbr, *refs),
+            pltpu.VMEM((slots, v0), f32),
+            pltpu.VMEM((slots, dim), bf16),
+            pltpu.VMEM((slots, kv), bf16),
+            pltpu.VMEM((slots, kv), bf16),
+            pltpu.VMEM((slots, dim), bf16),
+            pltpu.VMEM((slots, dim), f32),
+            pltpu.VMEM((slots, dim), bf16),
+            pltpu.VMEM((slots, dim), f32),
+            pltpu.VMEM((2, 4, rows, dim), bf16),
+        )
+        pl.run_scoped(
+            lambda *refs: sums(dbr, *refs),
+            pltpu.VMEM((slots, dim), bf16),
+            pltpu.VMEM((slots, dim), bf16),
+            pltpu.VMEM((2, RING // 2, rows, piece_cols), bf16),
+            pltpu.VMEM((3, rows, piece_cols), bf16),
+            pltpu.VMEM((2, 2, rows, qkv_width), bf16),
+        )
+
+    pl.run_scoped(both, pltpu.VMEM((slots, dim), bf16))
+
+    def a_landed(t, h, upward):
+        landing = l_land.at[1 if upward else 0, t, h]
+        sems = (au_send, au_recv) if upward else (ad_send, ad_recv)
+        return remote(landing, landing, sems[0].at[t, h], sems[1].at[t, h], sibling)
+
+    def results(middle, y, y_half, d_tmp, a_tmp, stage):
+        middle_in = pltpu.make_async_copy(middle_ref, middle, load.at[0])
+        middle_in.start()
+        each(MLP_D, lambda piece, group: finish(piece, group, d_tmp))
+        d_back = pltpu.make_async_copy(d_tmp, d_out, load.at[1])
+        d_back.start()
+        line_sum(1, y)
+        middle_in.wait()
+
+        def last_add(i, carry):
+            at = tile(i, 512)
+            y_half[:, at] = (middle[:, at] + y[:, at]).astype(bf16)
+            return carry
+
+        lax.fori_loop(0, dim // 512, last_add, 0)
+        y_back = pltpu.make_async_copy(y_half, y_out, load.at[2])
+        y_back.start()
+        each(MLP_D, drain_sibling)
+        each(MLP_D, drain)
+
+        for h in range(2):
+
+            @pl.when(z < last)
+            def _(h=h):
+                a_landed(z, h, False).wait_recv()
+
+            @pl.when(z > 0)
+            def _(h=h):
+                a_landed(z, h, True).wait_recv()
+
+        def total(*sides):
+            for h in range(2):
+                copies = [
+                    pltpu.make_async_copy(l_land.at[side, z, h], stage.at[i], stream.at[i])
+                    for i, side in enumerate(sides)
+                ]
+                for copy in copies:
+                    copy.start()
+                for copy in copies:
+                    copy.wait()
+                add_rows(
+                    a_tmp.at[:, pl.ds(h * piece_cols, piece_cols)],
+                    a_own(z, mine, h),
+                    *[stage.at[i] for i in range(len(sides))],
+                )
+
+        @pl.when(z == 0)
+        def _():
+            total(0)
+
+        @pl.when(z == last)
+        def _():
+            total(1)
+
+        @pl.when((z > 0) & (z < last))
+        def _():
+            total(0, 1)
+
+        a_back = pltpu.make_async_copy(a_tmp, a_out, load.at[3])
+        a_back.start()
+        for copy in (d_back, y_back, a_back):
+            copy.wait()
+
     pl.run_scoped(
-        attention,
+        results,
         pltpu.VMEM((slots, dim), f32),
-        pltpu.VMEM((slots, dim + kv), f32),
-        pltpu.VMEM((slots, dim), bf16),
-        pltpu.VMEM((slots, kv), bf16),
-        pltpu.VMEM((slots, kv), bf16),
-        pltpu.VMEM((slots, dim), bf16),
-        pltpu.VMEM((slots, dim), bf16),
-        pltpu.VMEM((slots, dim), bf16),
         pltpu.VMEM((slots, dim), f32),
         pltpu.VMEM((slots, dim), bf16),
-        pltpu.VMEM((slots, dim), bf16),
-        pltpu.VMEM((2, 4, rows, dim), bf16),
-        pltpu.VMEM((2, 4, rows, dim), bf16),
-        pltpu.VMEM((2, 2, rows, dim + 2 * kv), bf16),
+        pltpu.VMEM(gd_fst.shape, f32),
+        pltpu.VMEM((rows, 2 * piece_cols), f32),
+        pltpu.VMEM((2, rows, piece_cols), bf16),
     )
-    each(MLP_GU, finish)
-    gu_back = pltpu.make_async_copy(gu_all.at[:, 2 * mine + core], gu_out, back.at[0])
-    gu_back.start()
-
-    def drain(piece, group):
-        for quad in (far, fst, sec, mine):
-            to_sibling(quad, piece, group).wait_send()
-        to_second(far, 1, piece, group).wait_send()
-        to_second(sec, 0, piece, group).wait_send()
-        to_first(piece, group).wait_send()
-
-    each(MLP_GU, drain)
-    each(MLP_D, drain)
     for which in range(2):
         for k in range(LINE):
 
@@ -1183,33 +1499,33 @@
             def _(which=which, k=k):
                 send_line(t_own.at[which, k], which, k, True).wait_send()
 
-    gu_back.wait()
-
-
-def turn(gu, wd, tok, cot, hid, dgu, w, middle, normed, raw, q, k, v, mixed, gains, rope):
+
+def backward(gu, wd, tok, cot, hid, dgu, w, middle, normed, raw, q, k, v, mixed, x, gains, rope):
     dim = tok.shape[1]
     rows = w.shape[1]
     drows = wd.shape[0] // RING
     cols = gu.shape[1]
     quads = RING // 2
     pieces = LINE + 2
-    n = RING * LINE
     qkv = raw.shape[1]
     S = jax.ShapeDtypeStruct
     return pl.pallas_call(
-        turn_kernel,
+        backward_kernel,
         out_shape=(
+            S((CAP, dim), f32),
+            S((8, dim), f32),
             S((CAP, dim), bf16),
-            S((CAP, dim), f32),
-            S((CAP, qkv), bf16),
-            S((8, dim), f32),
             S((drows, dim), f32),
+            S((rows, qkv + dim), f32),
             S((LINE, rows, cols), bf16),
-            S((n, rows, qkv), bf16),
-            S((n, rows, dim), bf16),
+            S((LINE, rows, cols), bf16),
+            S((LINE, 2, quads, rows, cols), bf16),
+            S((2, LINE, 2, rows, cols), bf16),
+            S((LINE, 2, rows, cols), bf16),
+            S((2, LINE, 2, rows, cols), bf16),
         ),
-        in_specs=[ANY] * 14 + [VMEM] * 2,
-        out_specs=(VMEM,) * 5 + (ANY,) * 3,
+        in_specs=[ANY] * 14 + [VMEM] * 3,
+        out_specs=(VMEM,) * 2 + (ANY,) * 9,
         scratch_shapes=[
             pltpu.VMEM((LINE, RING, rows, cols), bf16),
             pltpu.VMEM((RING, drows, dim), bf16),
@@ -1221,6 +1537,11 @@
             pltpu.VMEM((drows, dim), bf16),
             pltpu.VMEM((2, LINE, CAP, dim), bf16),
             pltpu.VMEM((2, LINE + 1, CAP, dim), bf16),
+            pltpu.VMEM((CAP, dim), f32),
+            pltpu.VMEM((CAP, qkv), bf16),
+            pltpu.VMEM((4, 8, dim), f32),
+            pltpu.VMEM((3, 8, dim), f32),
+            pltpu.VMEM((LINE, 8, dim), f32),
             DMA((quads, pieces)),
             DMA((quads, pieces)),
             DMA((2, pieces)),
@@ -1231,325 +1552,110 @@
             DMA((2, LINE)),
             DMA((2, LINE)),
             DMA((2, LINE)),
-            DMA((8,)),
-            DMA((2, 3)),
+            DMA((6,)),
+            DMA((3,)),
             DMA((2,)),
+            DMA((2, quads)),
+            DMA((LINE, 2, quads)),
+            DMA((2, LINE, 2)),
+            DMA((2, LINE, 2)),
+            DMA((LINE, 2)),
+            DMA((LINE, 2)),
+            DMA((LINE, 2)),
+            DMA((LINE, 2)),
+            DMA((LINE, 2)),
+            DMA((LINE, 2)),
+            DMA((LINE,)),
+            DMA((LINE,)),
+            DMA((2 + LINE,)),
+            DMA((2 + LINE,)),
         ],
         compiler_params=pltpu.CompilerParams(
             collective_id=2, has_side_effects=True, vmem_limit_bytes=65400 * 1024
         ),
-        name="turn",
-    )(gu, wd, tok, cot, hid, dgu, w, middle, normed, raw, q, k, v, mixed, gains, rope)
-
-
-def close_kernel(
-    a_ref, o_ref, gu_ref, w_ref, s_ref, x_ref, dmid_ref, dqkv_ref, gains_ref,
-    q_out, k_out, v_out, o_out, gate_out, up_out, s_out, x_out,
-    own, sib, sec, fst, down, up, ex, s_sum, s_got, s_line, w_rows,
-    load, ex_load, c_send, c_recv, s_send, s_recv, f_send, f_recv, down_s, down_r, up_s, up_r,
-    ex_s, ex_r, small_s, small_r, stream,
+        name="backward",
+    )(gu, wd, tok, cot, hid, dgu, w, middle, normed, raw, q, k, v, mixed, x, gains, rope)
+
+
+def results_kernel(
+    y_ref, x_ref, small_ref, d_ref, a_ref, ex_ref,
+    y_out, x_out, q_out, k_out, v_out, o_out, gate_out, up_out, d_out, ga_out, gq_out, gk_out, gm_out,
+    y_tmp, x_tmp, small, d_tmp, a_tmp, ex_tmp, gate_tmp, up_tmp, sem_in, sem_out,
 ):
-    me, z, first, second, sibling = where_am_i()
-    greet(line_peers(me) + [first, second, sibling])
-    core = me % 2
-    q_mine, q_fst, q_sec = (me % RING) // 2, (first % RING) // 2, (second % RING) // 2
-    q_far = ((second + first - me) % RING) // 2
-    last = LINE - 1
-    split = a_ref.shape[2]
-    parts = ((a_ref, pl.ds(0, split)), (o_ref, pl.ds(split, o_ref.shape[2])))
-    order = (
-        last * (1 - z // 2),
-        2 - 2 * z + 5 * (z // 2),
-        1 + z % 2,
-        z,
-    )
-
-    def to_sibling(t, quad, part):
-        ref, at = parts[part]
-        return remote(
-            ref.at[RING * t + 2 * quad + 1 - core],
-            sib.at[t, quad, :, at],
-            c_send.at[t, quad, part],
-            c_recv.at[t, quad, part],
-            sibling,
-        )
-
-    def loading(t, quad, part):
-        ref, at = parts[part]
-        return pltpu.make_async_copy(
-            ref.at[RING * t + 2 * quad + core], own.at[t, quad, :, at], load.at[t, quad, part]
-        )
-
-    def ready(t, quad):
-        for part in range(2):
-            loading(t, quad, part).wait()
-            to_sibling(t, quad, part).wait_recv()
-
-    def to_second(t, quad, slot):
-        return remote(
-            own.at[t, quad], sec.at[slot, t], s_send.at[slot, t], s_recv.at[slot, t], second
-        )
-
-    def to_first(t):
-        return remote(own.at[t, q_fst], fst.at[t], f_send.at[t], f_recv.at[t], first)
-
-    def send_line(src, t, upward):
-        if upward:
-            return remote(src, up.at[t], up_s.at[t], up_r.at[t], me + RING)
-        return remote(src, down.at[t], down_s.at[t], down_r.at[t], me - RING)
-
-    def exchange(k):
-        peer_z = lax.rem(z + k, LINE)
-        return remote(
-            gu_ref.at[peer_z], ex.at[z], ex_s.at[k], ex_r.at[k], me % RING + RING * peer_z
-        )
-
-    def small(step, src, dst, device):
-        return remote(src, dst, small_s.at[step], small_r.at[step], device)
-
-    small_c = small(0, s_sum.at[3], s_got.at[0], sibling)
-    for k in range(1, LINE):
-        exchange(k).start()
-    ex_in = pltpu.make_async_copy(gu_ref.at[z], ex.at[z], ex_load)
-    ex_in.start()
-    for t in order:
-        for theirs, ours in ((q_far, q_far), (q_fst, q_sec), (q_sec, q_fst), (q_mine, q_mine)):
-            for part in range(2):
-                to_sibling(t, theirs, part).start()
-                loading(t, ours, part).start()
-
-    def spread(t):
-        for quad, slot in ((q_far, 1), (q_sec, 0)):
-            ready(t, quad)
-            add_rows(own.at[t, quad], own.at[t, quad], sib.at[t, quad])
-            to_second(t, quad, slot).start()
-
-    def narrow(t):
-        ready(t, q_fst)
-        to_second(t, q_far, 1).wait_recv()
-        add_rows(own.at[t, q_fst], own.at[t, q_fst], sib.at[t, q_fst], sec.at[1, t])
-        to_first(t).start()
-
-    def collect(t):
-        ready(t, q_mine)
-        to_second(t, q_sec, 0).wait_recv()
-        to_first(t).wait_recv()
-        mine = own.at[t, q_mine]
-        add_rows(mine, mine, sib.at[t, q_mine], sec.at[0, t], fst.at[t])
-
-        @pl.when((t < z) & (z == last))
-        def _():
-            send_line(mine, t, False).start()
-
-        @pl.when((t > z) & (z == 0))
-        def _():
-            send_line(mine, t, True).start()
-
-    def relay(t):
-        @pl.when((t < z) & (z < last))
-        def _():
-            landing = down.at[t]
-            send_line(landing, t, False).wait_recv()
-            add_rows(landing, landing, own.at[t, q_mine])
-            send_line(landing, t, False).start()
-
-        @pl.when((t > z) & (z > 0))
-        def _():
-            landing = up.at[t]
-            send_line(landing, t, True).wait_recv()
-            add_rows(landing, landing, own.at[t, q_mine])
-            send_line(landing, t, True).start()
-
-    shards = w_rows.shape[1]
-    dim = x_ref.shape[1]
-
-    def first_norm():
-        wide = 512
-        x_scale = rms_scale(x_ref[...].astype(f32))
-        w_tile = shards * w_rows.shape[2]
-
-        def w_fetch(i, slot):
-            return (
-                pltpu.make_async_copy(
-                    w_ref.at[tile(i, shards), :, pl.ds(0, split)], w_rows.at[slot], stream.at[slot]
-                ),
-            )
-
-        def through(i, slot):
-            x_out[:, tile(i, w_tile)] = dot_nt(dqkv_ref[...], w_rows[slot].reshape(w_tile, split))
-
-        streamed(dim // w_tile, w_fetch, through)
-        s_sum[3] = s_ref[...]
-
-        def gather_mean(i, total):
-            at = tile(i, wide)
-            n = x_ref[:, at].astype(f32) * x_scale
-            s_sum[3, 3:4, at] = jnp.sum(n * x_out[:, at], axis=0, keepdims=True)
-            return total + lane_sum(n * x_out[:, at] * gains_ref[0:1, at])
-
-        mean = lax.fori_loop(0, dim // wide, gather_mean, jnp.zeros((CAP, 1), f32)) / dim
-
-        def spread_mean(i, carry):
-            at = tile(i, wide)
-            n = x_ref[:, at].astype(f32) * x_scale
-            e = x_out[:, at] * gains_ref[0:1, at]
-            x_out[:, at] = dmid_ref[:, at] + x_scale * (e - n * mean)
-            return carry
-
-        lax.fori_loop(0, dim // wide, spread_mean, 0)
-
-    spread(order[0])
-    first_norm()
-    spread(order[1])
-    small_c.start()
-    narrow(order[0])
-    small_c.wait()
-    s_sum[0] = s_sum[3] + s_got[0]
-    small_f = small(1, s_sum.at[0], s_got.at[1], first)
-    small_f.start()
-    spread(order[2])
-    small_f.wait()
-    s_sum[1] = s_sum[0] + s_got[1]
-    small_s2 = small(2, s_sum.at[1], s_got.at[2], second)
-    small_s2.start()
-    narrow(order[1])
-    collect(order[0])
-    small_s2.wait()
-    s_sum[2] = s_sum[1] + s_got[2]
-    small_line = [
-        small(
-            2 + k, s_sum.at[2], s_line.at[k], me % RING + RING * lax.rem(z + k, LINE)
-        )
-        for k in range(1, LINE)
-    ]
-    for copy in small_line:
+    me = lax.axis_index("fsdp")
+    width = ex_tmp.shape[2] // 2
+    moves = ((small_ref, small), (ex_ref, ex_tmp), (a_ref, a_tmp), (d_ref, d_tmp), (x_ref, x_tmp), (y_ref, y_tmp))
+    ins = [pltpu.make_async_copy(src, dst, sem_in.at[i]) for i, (src, dst) in enumerate(moves)]
+    for copy in ins:
         copy.start()
-    spread(order[3])
-    narrow(order[2])
-    collect(order[1])
-    relay(order[0])
-    narrow(order[3])
-    collect(order[2])
-    relay(order[1])
-    relay(order[2])
-    collect(order[3])
-    ex_in.wait()
-    for k in range(1, LINE):
-        src_z = lax.rem(z + LINE - k, LINE)
-        landed = ex.at[src_z]
-        remote(landed, landed, ex_s.at[k], ex_r.at[k], sibling).wait_recv()
-    width = gate_out.shape[1] // LINE
+    outs = []
+
+    def leave(src, dst):
+        copy = pltpu.make_async_copy(src, dst, sem_out.at[len(outs)])
+        copy.start()
+        outs.append(copy)
+
+    ins[1].wait()
     for k in range(LINE):
-        add_rows(gate_out.at[:, pl.ds(k * width, width)], ex.at[k, :, pl.ds(0, width)])
-        add_rows(up_out.at[:, pl.ds(k * width, width)], ex.at[k, :, pl.ds(width, width)])
-    for copy in small_line:
+        add_rows(gate_tmp.at[:, pl.ds(k * width, width)], ex_tmp.at[k, :, pl.ds(0, width)])
+        add_rows(up_tmp.at[:, pl.ds(k * width, width)], ex_tmp.at[k, :, pl.ds(width, width)])
+    leave(gate_tmp, gate_out)
+    leave(up_tmp, up_out)
+    ins[2].wait()
+    lo = 0
+    for out in (q_out, k_out, v_out, o_out):
+        leave(a_tmp.at[:, pl.ds(lo, out.shape[1])], out)
+        lo += out.shape[1]
+    ins[3].wait()
+    leave(d_tmp, d_out)
+    ins[4].wait()
+    leave(x_tmp, x_out)
+    ins[5].wait()
+    leave(y_tmp, y_out)
+    ins[0].wait()
+    for row, out in ((3, ga_out), (1, gq_out), (2, gk_out), (0, gm_out)):
+        count = out.shape[1]
+        value = jnp.zeros((1, 128), f32)
+        for i in range(small.shape[1] // 128):
+            held = small[row : row + 1, i * 128 : (i + 1) * 128]
+            value = jnp.where((me * count) // 128 == i, held, value)
+        value = pltpu.roll(value, (128 - (me * count) % 128) % 128, 1)
+        out[...] = value[:, 0:count]
+    for copy in outs:
         copy.wait()
-    s_out[...] = (s_sum[2] + s_line[2]) + (s_line[1] + s_line[3])
-    mine, above, below = own.at[z, q_mine], down.at[z], up.at[z]
-
-    @pl.when(z < last)
-    def _():
-        send_line(above, z, False).wait_recv()
-
-    @pl.when(z > 0)
-    def _():
-        send_line(below, z, True).wait_recv()
-
-    def total(*terms):
-        lo = 0
-        for out in (q_out, k_out, v_out, o_out):
-            at = pl.ds(lo, out.shape[1])
-            add_rows(out, *[term.at[:, at] for term in terms])
-            lo += out.shape[1]
-
-    @pl.when(z == 0)
-    def _():
-        total(mine, above)
-
-    @pl.when(z == last)
-    def _():
-        total(mine, below)
-
-    @pl.when((z > 0) & (z < last))
-    def _():
-        total(mine, above, below)
-
-    for k in range(1, LINE):
-        exchange(k).wait_send()
-    for t in range(LINE):
-        for quad in (q_far, q_fst, q_sec, q_mine):
-            for part in range(2):
-                to_sibling(t, quad, part).wait_send()
-        to_second(t, q_far, 1).wait_send()
-        to_second(t, q_sec, 0).wait_send()
-        to_first(t).wait_send()
-
-        @pl.when(t < z)
-        def _(t=t):
-            send_line(down.at[t], t, False).wait_send()
-
-        @pl.when(t > z)
-        def _(t=t):
-            send_line(up.at[t], t, True).wait_send()
-
-
-def close(a, o, gu, w, small, x, dmid, dqkv, gains):
-    rows, split = a.shape[1:]
-    owide = o.shape[2]
-    wide = split + owide
-    quads = RING // 2
-    width = gu.shape[2] // 2
-    kv = KVH * HD
+
+
+def results(y, x, small, d, a, ex, widths, shares):
+    rows = a.shape[0]
+    wide = LINE * ex.shape[2] // 2
     S = jax.ShapeDtypeStruct
     return pl.pallas_call(
-        close_kernel,
+        results_kernel,
         out_shape=(
-            S((rows, H * HD), f32),
-            S((rows, kv), f32),
-            S((rows, kv), f32),
-            S((rows, owide), f32),
-            S((rows, LINE * width), f32),
-            S((rows, LINE * width), f32),
-            S(small.shape, f32),
+            S(y.shape, bf16),
             S(x.shape, f32),
+            *[S((rows, w), f32) for w in widths],
+            S((rows, wide), f32),
+            S((rows, wide), f32),
+            S(d.shape, f32),
+            *[S((1, s), f32) for s in shares],
         ),
-        in_specs=[ANY] * 4 + [VMEM] * 5,
-        out_specs=(VMEM,) * 8,
+        in_specs=[ANY] * 6,
+        out_specs=(ANY,) * 9 + (VMEM,) * 4,
         scratch_shapes=[
-            pltpu.VMEM((LINE, quads, rows, wide), bf16),
-            pltpu.VMEM((LINE, quads, rows, wide), bf16),
-            pltpu.VMEM((2, LINE, rows, wide), bf16),
-            pltpu.VMEM((LINE, rows, wide), bf16),
-            pltpu.VMEM((LINE, rows, wide), bf16),
-            pltpu.VMEM((LINE, rows, wide), bf16),
-            pltpu.VMEM((LINE, rows, 2 * width), bf16),
-            pltpu.VMEM((4,) + small.shape, f32),
-            pltpu.VMEM((3,) + small.shape, f32),
-            pltpu.VMEM((LINE,) + small.shape, f32),
-            pltpu.VMEM((2, 4, rows, split), bf16),
-            DMA((LINE, quads, 2)),
-            DMA,
-            DMA((LINE, quads, 2)),
-            DMA((LINE, quads, 2)),
-            DMA((2, LINE)),
-            DMA((2, LINE)),
-            DMA((LINE,)),
-            DMA((LINE,)),
-            DMA((LINE,)),
-            DMA((LINE,)),
-            DMA((LINE,)),
-            DMA((LINE,)),
-            DMA((LINE,)),
-            DMA((LINE,)),
-            DMA((2 + LINE,)),
-            DMA((2 + LINE,)),
-            DMA((2,)),
+            pltpu.VMEM(y.shape, bf16),
+            pltpu.VMEM(x.shape, f32),
+            pltpu.VMEM(small.shape, f32),
+            pltpu.VMEM(d.shape, f32),
+            pltpu.VMEM(a.shape, f32),
+            pltpu.VMEM(ex.shape, bf16),
+            pltpu.VMEM((rows, wide), f32),
+            pltpu.VMEM((rows, wide), f32),
+            DMA((6,)),
+            DMA((9,)),
         ],
-        compiler_params=pltpu.CompilerParams(
-            collective_id=3, has_side_effects=True, vmem_limit_bytes=65400 * 1024
-        ),
-        name="close",
-    )(a, o, gu, w, small, x, dmid, dqkv, gains)
+        name="results",
+    )(y, x, small, d, a, ex)
 
 
 def layout(seq_lengths, seq_device, owner, slots):
@@ -1797,38 +1903,37 @@
         hidden_in, out_grad, seq_lengths, seq_device, (attn_gain, mlp_gain, q_gain, k_gain),
         w_query, w_key, w_value, w_out, w_gate, w_up, w_down,
     )
-    rows, dim = w_query.shape[0], hidden_in.shape[1]
-    hidden_out, d_middle, d_qkv, small, grad_down, g_gate_up, g_qkv, g_out = turn(
+    dim = hidden_in.shape[1]
+    x, small, y, grad_down, attn_sums, exchanged, *unused = backward(
         gate_up_w.reshape(-1, gate_up_w.shape[-1]),
         down_w.reshape(-1, dim),
         tokens.reshape(-1, dim),
         cotangent.reshape(-1, dim),
-        hidden, d_gate_up, attn_w, middle, normed, qkv_raw, queries, keys, values, mixed, gains, rope,
+        hidden, d_gate_up, attn_w, middle, normed, qkv_raw, queries, keys, values, mixed,
+        hidden_in, gains, rope,
     )
-    g_query, g_key, g_value, g_out, g_gate, g_up, small, input_grad = close(
-        g_qkv, g_out, g_gate_up, attn_w, small, hidden_in, d_middle, d_qkv, gains
+    (
+        hidden_out, input_grad, g_query, g_key, g_value, g_out, g_gate, g_up, g_down,
+        g_attn_gain, g_q_gain, g_k_gain, g_mlp_gain,
+    ) = results(
+        y, x, small, grad_down, attn_sums, exchanged,
+        [w.shape[1] for w in (w_query, w_key, w_value, w_out)],
+        [g.shape[0] for g in (attn_gain, q_gain, k_gain, mlp_gain)],
     )
-    me = lax.axis_index("fsdp")
-
-    def share(row, grad_of):
-        count = grad_of.shape[0]
-        return lax.dynamic_slice(small, (row, me * count), (1, count))[0]
-
-    gain_sums = (share(3, attn_gain), share(1, q_gain), share(2, k_gain), share(0, mlp_gain))
     return (
         hidden_out,
         input_grad,
-        gain_sums[0],
-        gain_sums[1],
-        gain_sums[2],
+        g_attn_gain[0],
+        g_q_gain[0],
+        g_k_gain[0],
         g_query,
         g_key,
         g_value,
         g_out,
-        gain_sums[3],
+        g_mlp_gain[0],
         g_gate,
         g_up,
-        grad_down,
+        g_down,
     )
 
 

time: 480 us -> 453 us (0.944)
  local copies, waits for them, and re-layouts: 14.2 us -> 0 us
  Pallas kernels: 463 us -> 449 us
    pallas_call x2, Pallas kernels: 254 us -> 240 us  [the longest x1 235 us: backward(): pl.pallas_call(backward_kernel, out_shape=(S((CAP, dim), f32), S((8, dim)...]
    unnamed x23 -> x0, local copies, waits for them, and re-layouts: 11.6 us -> none
where the time goes in v4:
time: 453 us; the launch traced here: 450 us
  Pallas kernels  449 us (99%)
    pallas_call x1, Pallas kernels, backward(): pl.pallas_call(backward_kernel, out_shape=(S((CAP, dim), f32), S((8, dim)...  235 us
    pallas_call x1, Pallas kernels, forward(): pl.pallas_call(forward_kernel, out_shape=(S((n, rows, wide), bf16), S((LI...  209 us

profile of v4, /device:TPU:8, one launch (start us, length us, event | category | flops | bytes accessed | tf_op | source)
XLA Modules:
  0.0 450.0 jit_solution(16179062844962519397)
XLA Ops:
  0.7 208.9 %forward.1 = (bf16[32,64,6272]{2,1,0:T(8,128)(2,1)}, bf16[4,8,64,3072]{3,2,1,0:T(8,128)(2,1)}, bf16[8,192,2048]{2,1,0:T(8,128)(2,1)}, bf16[4,128,2048]{2,1,0:T(8...) custom-call(bf16[128,2048]{1,0:T(8,128)(2,1)} %x_ref.3, ...), custom_call_target="tpu_custom_call" | custom-call | tf_op jit(solution)/shard_map/forward/pallas_call | solution.py:651
  209.5 234.7 %backward.1 = (f32[128,2048]{1,0:T(8,128)}, f32[8,2048]{1,0:T(8,128)}, bf16[128,2048]{1,0:T(8,128)(2,1)}, f32[192,2048]{1,0:T(8,128)}, f32[64,6144]{1,0:T(8,128)...) custom-call(bf16[2048,3072]{1,0:T(8,128)(2,1)} %bitcast.14, ...), custom_call_target="tpu_custom_call" | custom-call | tf_op jit(solution)/shard_map/backward/pallas_call | solution.py:1512
  444.3 5.6 %results.1 = (bf16[128,2048]{1,0:T(8,128)(2,1)}, f32[128,2048]{1,0:T(8,128)}, f32[64,2048]{1,0:T(8,128)}, f32[64,1024]{1,0:T(8,128)}, f32[64,1024]{1,0:T(8,128)}...) custom-call(bf16[128,2048]{1,0:T(8,128)(2,1)} %get-tuple-element.64., ...), custom_call_target="tpu_custom_call" | custom-call | tf_op jit(solution)/shard_map/results/pallas_call | solution.py:1632

commit v5 on v4

--- a/solution.py
+++ b/solution.py
@@ -161,15 +161,14 @@
 
 def forward_kernel(
     x_ref, len_ref, dev_ref, ga_ref, gm_ref, gq_ref, gk_ref, cot_ref,
-    wq_ref, wk_ref, wv_ref, wo_ref, gate_ref, up_ref, wd_ref,
-    w_out, gu_out, d_out, tok_out, cot_out,
-    hid_out, dgu_out,
+    wq_ref, wk_ref, wv_ref, wo_ref, gate_ref, up_ref,
+    w_out, gu_out, tok_out, cot_out, hid_out, pre_out,
     middle_out, normed_out, raw_out, q_out, k_out, v_out, mixed_out, gains_out, rope_out,
-    w_tmp, p_tmp, d_tmp, cot_tmp, second_tmp, chunk, ow_all, gain_tmp, gain_own,
-    tok_all, cot_all, gate_up, dhid, m_chunk, wd_rows, hid, dgu,
+    w_tmp, p_tmp, cot_tmp, second_tmp, chunk, ow_all, gain_tmp, gain_own,
+    tok_all, gate_up, m_chunk, hid,
     local, up_s, down_s, first_s, second_s, sib_s, recv, ex_send, ex_recv,
     m_first_s, m_second_s, m_sib_s, m_recv, line_up, line_down, line_r, w_load, o_load, g_load,
-    stream, act_out,
+    act_out,
 ):
     me, z, first, second, sibling = where_am_i()
     col, fcol, scol = me % RING, first % RING, second % RING
@@ -179,7 +178,7 @@
     qkv_width = raw_out.shape[1]
     attn_width = qkv_width + wo_ref.shape[1]
     last = LINE - 1
-    pieces = LINE + 1
+    pieces = LINE
 
     w_in = []
     lo = 0
@@ -195,9 +194,8 @@
         )
         for which, ref in enumerate((gate_ref, up_ref))
     ]
-    d_in = pltpu.make_async_copy(wd_ref, d_tmp, local.at[7])
     cot_in = pltpu.make_async_copy(cot_ref, cot_tmp, local.at[8])
-    for copy in w_in + p_in + [d_in, cot_in]:
+    for copy in w_in + p_in + [cot_in]:
         copy.start()
     gain_own[...] = jnp.zeros_like(gain_own)
     for i, ref in enumerate((ga_ref, gm_ref, gq_ref, gk_ref)):
@@ -222,8 +220,15 @@
         dst = p_tmp.at[z, :, pl.ds(which * width, width)]
         return remote(src, dst, ex_send.at[k, which], ex_recv.at[k, which], col + RING * peer_z)
 
+    token_half = second_tmp.shape[1] // 2
+
+    def line_spot(which, shard):
+        if which == 1:
+            return cot_out.at[shard]
+        return tok_out.at[shard, :, pl.ds(token_half * (which // 2), token_half)]
+
     def line_send(src, which, shard, sems, device):
-        landing = (tok_out, cot_out)[which].at[shard]
+        landing = line_spot(which, shard)
         return remote(src, landing, sems.at[which, shard], line_r.at[which, shard], device)
 
     def line_own(which, src):
@@ -238,7 +243,7 @@
     def line_relay(which, k):
         def body(step):
             shard = z + step
-            src = (tok_out, cot_out)[which].at[shard]
+            src = line_spot(which, shard)
             line_send(src, which, shard, line_up, second).wait_recv()
             if step < 0:
 
@@ -379,7 +384,7 @@
     other(sfcol, 1, False)
     group(1)
 
-    for copy in p_in + [d_in]:
+    for copy in p_in:
         copy.wait()
     for k in range(1, LINE):
         for which in range(2):
@@ -388,10 +393,10 @@
             remote(landed, landed, ex_send.at[k, which], ex_recv.at[k, which], second).wait_recv()
 
     def spot(piece, shard):
-        return gu_out.at[piece, shard] if piece < LINE else d_out.at[shard]
+        return gu_out.at[piece, shard]
 
     def source(piece):
-        return p_tmp.at[piece] if piece < LINE else d_tmp
+        return p_tmp.at[piece]
 
     def m_send(src, piece, shard, sems, device):
         return remote(
@@ -401,26 +406,29 @@
     def m_arrived(piece, shard):
         m_send(spot(piece, shard), piece, shard, m_sib_s, sibling).wait_recv()
 
+    def m_own_second(piece):
+        m_send(source(piece), piece, col, m_second_s, second).start()
+
+    def m_own_first(piece):
+        m_send(source(piece), piece, col, m_first_s, first).start()
+        m_send(source(piece), piece, col, m_sib_s, sibling).start()
+
     def m_own(piece):
-        m_send(source(piece), piece, col, m_first_s, first).start()
-        m_send(source(piece), piece, col, m_second_s, second).start()
-        m_send(source(piece), piece, col, m_sib_s, sibling).start()
-
-    m_own(LINE)
-    m_own(0)
-    backs = [
-        pltpu.make_async_copy(p_tmp, gu_out.at[:, col], local.at[11]),
-        pltpu.make_async_copy(d_tmp, d_out.at[col], local.at[12]),
-    ]
-    for copy in backs:
-        copy.start()
+        m_own_second(piece)
+        m_own_first(piece)
+
+    m_own_second(0)
+    m_own_second(1)
+    p_back = pltpu.make_async_copy(p_tmp, gu_out.at[:, col], local.at[11])
+    p_back.start()
     line_relay(1, 1)
     other(scol, 3, False)
     other(sfcol, 2, False)
     group(2)
     other(sfcol, 3, False)
+    m_own_first(0)
+    m_own_first(1)
     group(3)
-    line_relay(1, 2)
 
     small = jnp.zeros((16, 128), f32)
     for zz in range(LINE):
@@ -458,7 +466,7 @@
             mixed_out[:, where] = mixed.astype(bf16)
         return carry
 
-    lax.fori_loop(0, KVH, head, 0)
+    lax.fori_loop(0, KVH, head, 0, unroll=2)
     for zz in range(LINE):
         pltpu.make_async_copy(
             w_out.at[pl.ds(RING * zz, RING), :, pl.ds(qkv_width, attn_width - qkv_width)],
@@ -495,36 +503,26 @@
         for k in range(RING // 2):
             m_arrived(piece, 2 * k + sibling % 2)
 
-    part = dhid.shape[1]
-    dim = tok_out.shape[2]
-    wide = wd_rows.shape[2]
-
-    def down_back(lo, hi):
-        def fetch(i, slot):
-            j = lo + i
-            return (
-                pltpu.make_async_copy(
-                    d_out.at[tile(j, 2)], wd_rows.at[slot], stream.at[slot]
-                ),
-            )
-
-        def body(i, slot):
-            right = wd_rows[slot].reshape(wide * 2, dim)
-            dhid[:, tile(lo + i, 2 * wide)] = dot_nt(cot_all[...].reshape(LINE * CAP, dim), right)
-
-        streamed(hi - lo, fetch, body)
+    part = width
+
+    def gate_up_copy(piece):
+        return pltpu.make_async_copy(
+            gu_out.at[piece], m_chunk.at[piece % 2], act_out.at[piece % 2, 0]
+        )
+
+    def gate_up_load(piece):
+        m_whole(piece)
+        gate_up_copy(piece).start()
 
     def gate_up_rows(piece):
-        m_whole(piece)
-        copy = pltpu.make_async_copy(gu_out.at[piece], m_chunk, stream.at[0])
-        copy.start()
-        copy.wait()
+        gate_up_copy(piece).wait()
         span = RING * rows
         left = tok_all[:, :, pl.ds(piece * span, span)].reshape(LINE * CAP, span)
 
         def columns(n, carry):
             at = tile(n, 512)
-            term = jnp.dot(left, m_chunk[:, :, at].reshape(span, 512), preferred_element_type=f32)
+            right = m_chunk[piece % 2, :, :, at].reshape(span, 512)
+            term = jnp.dot(left, right, preferred_element_type=f32)
             if piece == 0:
                 gate_up[:, at] = term
             else:
@@ -533,80 +531,87 @@
 
         lax.fori_loop(0, 2 * part // 512, columns, 0)
 
-    m_other(LINE, fcol, True)
-    line_own(0, second_tmp)
+    m_own(2)
+    line_own(0, second_tmp.at[:, pl.ds(0, token_half)])
+    line_own(2, second_tmp.at[:, pl.ds(token_half, token_half)])
     tok_back = pltpu.make_async_copy(second_tmp, tok_out.at[z], local.at[13])
     tok_back.start()
-    m_own(1)
-    m_other(LINE, scol, False)
+    line_relay(1, 2)
     m_other(0, fcol, True)
-    m_own(2)
     m_other(0, scol, False)
+    m_own(3)
+    line_relay(0, 1)
+    line_relay(2, 1)
+    m_other(1, fcol, True)
     line_relay(1, 3)
-    cot_back.wait()
-    cot_in = pltpu.make_async_copy(cot_out, cot_all, local.at[8])
-    cot_in.start()
-    m_other(LINE, sfcol, False)
-    line_relay(0, 1)
-    m_other(1, fcol, True)
-    m_own(3)
     m_other(1, scol, False)
-    m_whole(LINE)
-    for copy in backs:
-        copy.wait()
-    cot_in.wait()
-    down_back(0, RING // 4)
     m_other(0, sfcol, False)
     line_relay(0, 2)
+    line_relay(2, 2)
     m_other(2, fcol, True)
     m_other(2, scol, False)
-    down_back(RING // 4, RING // 2)
     m_other(1, sfcol, False)
+    p_back.wait()
+    gate_up_load(0)
+    m_other(3, fcol, True)
+    m_other(3, scol, False)
     line_relay(0, 3)
     tok_back.wait()
-    tok_in = pltpu.make_async_copy(tok_out, tok_all, local.at[10])
-    tok_in.start()
-    m_other(3, fcol, True)
-    m_other(3, scol, False)
-    tok_in.wait()
+    cot_back.wait()
+    tok_in = []
+    for half in range(2):
+        at = pl.ds(half * token_half, token_half)
+        tok_in.append(
+            pltpu.make_async_copy(
+                tok_out.at[:, :, at], tok_all.at[:, :, at], local.at[10 if half else 12]
+            )
+        )
+    tok_in[0].start()
+    gate_up_load(1)
+    tok_in[0].wait()
     gate_up_rows(0)
     m_other(2, sfcol, False)
+    gate_up_load(2)
     gate_up_rows(1)
+    line_relay(2, 3)
+    tok_in[1].start()
+    tok_in[1].wait()
     m_other(3, sfcol, False)
+    gate_up_load(3)
     gate_up_rows(2)
     gate_up_rows(3)
 
-    def act_copies(n):
+    def hid_copy(n):
+        at = tile(n, 256)
+        return pltpu.make_async_copy(hid.at[:, at], hid_out.at[:, at], act_out.at[n, 0])
+
+    def pre_copies(n):
         up_at = pl.ds(pl.multiple_of(part + n * 256, 256), 256)
-        return (
-            pltpu.make_async_copy(hid.at[:, tile(n, 256)], hid_out.at[:, tile(n, 256)], act_out.at[n, 0]),
-            pltpu.make_async_copy(dgu.at[:, tile(n, 256)], dgu_out.at[:, tile(n, 256)], act_out.at[n, 1]),
-            pltpu.make_async_copy(dgu.at[:, up_at], dgu_out.at[:, up_at], act_out.at[n, 2]),
-        )
+        return [
+            pltpu.make_async_copy(gate_up.at[:, at], pre_out.at[:, at], act_out.at[n, i])
+            for i, at in ((1, tile(n, 256)), (2, up_at))
+        ]
 
     def units(n, carry):
         at = tile(n, 256)
         up_at = pl.ds(pl.multiple_of(part + n * 256, 256), 256)
+        for copy in pre_copies(n):
+            copy.start()
 
         def act(r, inner):
             some = tile(r, 32)
-            gate, up, back = gate_up[some, at], gate_up[some, up_at], dhid[some, at]
-            sig = jax.nn.sigmoid(gate)
-            silu = gate * sig
-            hid[some, at] = (silu * up).astype(bf16)
-            dgu[some, at] = (back * up * (sig * (1.0 + gate * (1.0 - sig)))).astype(bf16)
-            dgu[some, up_at] = (back * silu).astype(bf16)
+            gate, up = gate_up[some, at], gate_up[some, up_at]
+            hid[some, at] = (gate * jax.nn.sigmoid(gate) * up).astype(bf16)
             return inner
 
         lax.fori_loop(0, LINE * CAP // 32, act, 0)
-        for copy in act_copies(n):
-            copy.start()
+        hid_copy(n).start()
         return carry
 
     lax.fori_loop(0, part // 256, units, 0)
 
     for n in range(part // 256):
-        for copy in act_copies(n):
+        for copy in [hid_copy(n)] + pre_copies(n):
             copy.wait()
     for k in range(1, LINE):
         for which in range(2):
@@ -616,14 +621,14 @@
         @pl.when((z < last) & (k <= z))
         def _(k=k):
             send(w_tmp, col + RING * k, up_s, me + RING).wait_send()
-            for which in range(2):
-                line_send(cot_tmp, which, k, line_up, me + RING).wait_send()
+            for which in range(3):
+                line_send(line_spot(which, k), which, k, line_up, me + RING).wait_send()
 
         @pl.when((z > 0) & (k >= z))
         def _(k=k):
             send(w_tmp, col + RING * k, down_s, me - RING).wait_send()
-            for which in range(2):
-                line_send(cot_tmp, which, k, line_down, me - RING).wait_send()
+            for which in range(3):
+                line_send(line_spot(which, k), which, k, line_down, me - RING).wait_send()
 
         send(w_tmp, col + RING * k, first_s, first).wait_send()
         send(w_tmp, col + RING * k, second_s, second).wait_send()
@@ -639,25 +644,24 @@
             m_send(src, piece, base, m_sib_s, sibling).wait_send()
 
 
-def forward(hidden_in, out_grad, seq_lengths, seq_device, gains, wq, wk, wv, wo, gate, up, wd):
+def forward(hidden_in, out_grad, seq_lengths, seq_device, gains, wq, wk, wv, wo, gate, up):
     slots, dim = hidden_in.shape
     rows = wq.shape[0]
     n = RING * LINE
     width = gate.shape[1] // LINE
     qkv_width = wq.shape[1] + wk.shape[1] + wv.shape[1]
     wide = qkv_width + wo.shape[1] + 128
-    pieces = LINE + 1
+    pieces = LINE
     S = jax.ShapeDtypeStruct
     return pl.pallas_call(
         forward_kernel,
         out_shape=(
             S((n, rows, wide), bf16),
             S((LINE, RING, rows, 2 * width), bf16),
-            S((RING,) + wd.shape, bf16),
             S((LINE, slots, dim), bf16),
             S((LINE, slots, dim), bf16),
             S((LINE * slots, width), bf16),
-            S((LINE * slots, 2 * width), bf16),
+            S((LINE * slots, 2 * width), f32),
             S((slots, dim), f32),
             S((slots, dim), bf16),
             S((slots, qkv_width), f32),
@@ -668,12 +672,11 @@
             S((8, dim), f32),
             S((3, slots, HD), f32),
         ),
-        in_specs=[VMEM] * 7 + [ANY] * 8,
-        out_specs=(ANY,) * 7 + (VMEM,) * 9,
+        in_specs=[VMEM] * 7 + [ANY] * 7,
+        out_specs=(ANY,) * 6 + (VMEM,) * 9,
         scratch_shapes=[
             pltpu.VMEM((rows, wide), bf16),
             pltpu.VMEM((LINE, rows, 2 * width), bf16),
-            pltpu.VMEM(wd.shape, bf16),
             pltpu.VMEM((slots, dim), bf16),
             pltpu.VMEM((slots, dim), bf16),
             pltpu.VMEM((RING, rows, qkv_width), bf16),
@@ -681,13 +684,9 @@
             pltpu.VMEM((LINE, RING, 16, 128), bf16),
             pltpu.VMEM((16, 128), f32),
             pltpu.VMEM((LINE, slots, dim), bf16),
-            pltpu.VMEM((LINE, slots, dim), bf16),
             pltpu.VMEM((LINE * slots, 2 * width), f32),
-            pltpu.VMEM((LINE * slots, width), f32),
-            pltpu.VMEM((RING, rows, 2 * width), bf16),
-            pltpu.VMEM((2, 2) + wd.shape, bf16),
+            pltpu.VMEM((2, RING, rows, 2 * width), bf16),
             pltpu.VMEM((LINE * slots, width), bf16),
-            pltpu.VMEM((LINE * slots, 2 * width), bf16),
             DMA((14,)),
             DMA((n,)),
             DMA((n,)),
@@ -701,13 +700,12 @@
             DMA((pieces, RING)),
             DMA((pieces, RING)),
             DMA((pieces, RING)),
-            DMA((2, LINE)),
-            DMA((2, LINE)),
-            DMA((2, LINE)),
+            DMA((3, LINE)),
+            DMA((3, LINE)),
+            DMA((3, LINE)),
             DMA,
             DMA((LINE,)),
             DMA,
-            DMA((2,)),
             DMA((width // 256, 3)),
         ],
         compiler_params=pltpu.CompilerParams(
@@ -716,29 +714,32 @@
         name="forward",
     )(
         hidden_in, seq_lengths[None, :], seq_device[None, :], *[g[None, :] for g in gains],
-        out_grad, wq, wk, wv, wo, gate, up, wd,
+        out_grad, wq, wk, wv, wo, gate, up,
     )
 
 
 def backward_kernel(
-    gu_ref, wd_ref, tok_ref, cot_ref, hid_ref, dgu_ref, w_ref, middle_ref, normed_ref, raw_ref,
+    gu_ref, down_ref, tok_ref, cot_ref, hid_ref, pre_ref, w_ref, middle_ref, normed_ref, raw_ref,
     q_ref, k_ref, v_ref, mixed_ref, x_ref, gains_ref, rope_ref,
-    x_out, small_out, y_out, d_out, a_out, ex_land, gu_out, c_land, s_land, f_land, l_land,
+    x_out, small_out, y_out, d_out, a_out, ex_land, gu_out, c_land, s_land, f_land, l_land, wd_ref,
     gu_all, gd_all, gu_sib, gd_sib, gu_sec, gd_sec, gu_fst, gd_fst, t_own, t_land,
     dmid, dqkv, s_sum, s_got, s_line,
     c_send, c_recv, s_send, s_recv, f_send, f_recv, down_s, down_r, up_s, up_r, load, stream, back,
     ac_send, ac_recv, as_send, as_recv, af_send, af_recv, ad_send, ad_recv, au_send, au_recv,
-    ex_s, ex_r, small_s, small_r,
+    ex_s, ex_r, small_s, small_r, w_first, w_second, w_sib, w_recv, units_in,
+    a_load,
 ):
     me, z, first, second, sibling = where_am_i()
     greet(line_peers(me) + [first, second, sibling])
     core = me % 2
+    col, fcol, scol = me % RING, first % RING, second % RING
+    sfcol = (second + first - me) % RING
     mine, fst, sec = (me % RING) // 2, (first % RING) // 2, (second % RING) // 2
     far = ((second + first - me) % RING) // 2
     half = gd_fst.shape[0] // 2
     last = LINE - 1
     tokens, dim = tok_ref.shape
-    part = wd_ref.shape[0]
+    part = hid_ref.shape[1]
     quad_rows = part // LINE
     shard_rows = dim // (RING * LINE)
     piece_cols = gu_all.shape[3]
@@ -894,11 +895,36 @@
         def _():
             add_rows(out, own, above, below)
 
-    def mlp(tok, cot, hid, dgu):
+    def w_spot(shard, piece):
+        return wd_ref.at[pl.ds(pl.multiple_of(shard * 2 * half + piece * half, half), half)]
+
+    def w_send(src, shard, piece, sems, device):
+        return remote(
+            src, w_spot(shard, piece), sems.at[shard, piece], w_recv.at[shard, piece], device
+        )
+
+    def w_arrived(shard, piece):
+        w_send(w_spot(shard, piece), shard, piece, w_sib, sibling).wait_recv()
+
+    def w_other(shard, onward):
+        for piece in range(2):
+            w_arrived(shard, piece)
+            src = w_spot(shard, piece)
+            if onward:
+                w_send(src, shard, piece, w_second, second).start()
+            w_send(src, shard, piece, w_sib, sibling).start()
+
+    for piece in range(2):
+        src = down_ref.at[pl.ds(piece * half, half)]
+        w_send(src, col, piece, w_first, first).start()
+        w_send(src, col, piece, w_second, second).start()
+        w_send(src, col, piece, w_sib, sibling).start()
+
+    def mlp(tok, cot, hid, dgu, down_own):
         ins = [
             pltpu.make_async_copy(hid_ref, hid, load.at[0]),
             pltpu.make_async_copy(cot_ref, cot, load.at[1]),
-            pltpu.make_async_copy(dgu_ref, dgu, load.at[2]),
+            pltpu.make_async_copy(down_ref, down_own, load.at[2]),
             pltpu.make_async_copy(tok_ref, tok, load.at[3]),
         ]
         for copy in ins:
@@ -921,6 +947,58 @@
             if previous is not None:
                 each(MLP_D, lambda piece, group, q=previous: to_sibling(q, piece, group).start())
             previous = quad
+        ins[2].wait()
+        down_back = pltpu.make_async_copy(
+            down_own, wd_ref.at[tile(col, 2 * half)], load.at[4]
+        )
+        down_back.start()
+        each(MLP_D, lambda piece, group, q=previous: to_sibling(q, piece, group).start())
+        w_other(fcol, True)
+        w_other(scol, False)
+        each(MLP_D, pass_on)
+        w_other(sfcol, False)
+        for piece in range(2):
+            for k in range(RING // 2):
+                w_arrived(2 * k + sibling % 2, piece)
+        down_back.wait()
+
+        def units(gate_t, up_t, down_w, dhid_t):
+            def fetch(i, slot):
+                up_at = pl.ds(pl.multiple_of(part + i * wide, wide), wide)
+                return (
+                    pltpu.make_async_copy(
+                        pre_ref.at[:, tile(i, wide)], gate_t.at[slot], units_in.at[slot, 0]
+                    ),
+                    pltpu.make_async_copy(pre_ref.at[:, up_at], up_t.at[slot], units_in.at[slot, 1]),
+                    pltpu.make_async_copy(
+                        wd_ref.at[tile(i, wide)], down_w.at[slot], units_in.at[slot, 2]
+                    ),
+                )
+
+            def body(i, slot):
+                dhid_t[...] = dot_nt(cot[...], down_w[slot])
+
+                def act(r, carry):
+                    at = tile(r, 32)
+                    gate, up, dhid = gate_t[slot, at], up_t[slot, at], dhid_t[at]
+                    sig = jax.nn.sigmoid(gate)
+                    dgate = dhid * up * (sig * (1.0 + gate * (1.0 - sig)))
+                    dgu[at, tile(i, wide)] = dgate.astype(bf16)
+                    up_at = pl.ds(pl.multiple_of(part + i * wide, wide), wide)
+                    dgu[at, up_at] = (dhid * (gate * sig)).astype(bf16)
+                    return carry
+
+                lax.fori_loop(0, tokens // 32, act, 0)
+
+            streamed(part // wide, fetch, body)
+
+        pl.run_scoped(
+            units,
+            pltpu.VMEM((2, tokens, wide), f32),
+            pltpu.VMEM((2, tokens, wide), f32),
+            pltpu.VMEM((2, wide, dim), bf16),
+            pltpu.VMEM((tokens, wide), f32),
+        )
 
         def back_through(rows_w):
             def fetch(i, slot):
@@ -936,12 +1014,8 @@
 
             streamed(dim // wide, fetch, body)
 
-        each(MLP_D, lambda piece, group, q=previous: to_sibling(q, piece, group).start())
-        for copy in ins[2:]:
-            copy.wait()
+        ins[3].wait()
         pl.run_scoped(back_through, pltpu.VMEM((2, wide, 2 * part), bf16))
-        each(MLP_D, pass_on)
-        line_own(0)
 
         rows = dim // LINE
         for piece in range(LINE):
@@ -953,7 +1027,9 @@
                 return carry
 
             lax.fori_loop(0, 2 * part // 512, columns, 0)
-            if piece > 0:
+            if piece == 0:
+                line_own(0)
+            else:
                 pass_on(piece - 1, 0)
             for quad in (far, fst, sec, mine):
                 to_sibling(quad, piece, 0).start()
@@ -983,9 +1059,17 @@
         pltpu.VMEM((tokens, dim), bf16),
         pltpu.VMEM((tokens, part), bf16),
         pltpu.VMEM((tokens, 2 * part), bf16),
+        pltpu.VMEM((2 * half, dim), bf16),
     )
-
-    def attention(dbr, raw, q, k, v, cot, dsec, dmix, middle, w_rows):
+    for piece in range(2):
+        src = down_ref.at[pl.ds(piece * half, half)]
+        w_send(src, col, piece, w_first, first).wait_send()
+        w_send(src, col, piece, w_second, second).wait_send()
+        w_send(src, fcol, piece, w_second, second).wait_send()
+        for base in (col, fcol, scol, sfcol):
+            w_send(src, base, piece, w_sib, sibling).wait_send()
+
+    def attention(dbr, mixed, normed, raw, q, k, v, cot, dsec, dmix, middle, w_rows):
         ins = [
             pltpu.make_async_copy(src, dst, load.at[i])
             for i, (src, dst) in enumerate(
@@ -996,6 +1080,8 @@
                     (k_ref, k),
                     (v_ref, v),
                     (cot_ref.at[tile(z, CAP)], cot),
+                    (mixed_ref, mixed),
+                    (normed_ref, normed),
                 )
             )
         ]
@@ -1084,9 +1170,9 @@
             dqkv[:, pl.ds(pl.multiple_of(v0 + g * HD, HD), HD)] = d_value.astype(bf16)
             return carry
 
-        lax.fori_loop(0, KVH // 2, head, 0)
+        lax.fori_loop(0, KVH // 2, head, 0, unroll=2)
         narrow(2, 0)
-        lax.fori_loop(KVH // 2, KVH, head, 0)
+        lax.fori_loop(KVH // 2, KVH, head, 0, unroll=2)
 
     order = (
         last * (1 - z // 2),
@@ -1098,15 +1184,7 @@
     def a_own(t, quad, h):
         return gu_all.at[t, 2 * quad + (core if h else 1 - core)]
 
-    def sums(dbr, mixed, normed, cbuf, stage, w_rows):
-        ins = [
-            pltpu.make_async_copy(mixed_ref, mixed, load.at[0]),
-            pltpu.make_async_copy(normed_ref, normed, load.at[1]),
-        ]
-        for copy in ins:
-            copy.start()
-        for copy in ins:
-            copy.wait()
+    def sums(dbr, mixed, normed, cbuf, stage):
         span = dim // LINE
 
         def a_sibling(t, quad, h, slot):
@@ -1140,16 +1218,20 @@
                 )
             return remote(src, l_land.at[0, t, h], ad_send.at[t, h], ad_recv.at[t, h], me - RING)
 
-        def absorb(own, *landed):
-            copies = [
-                pltpu.make_async_copy(src, stage.at[i], stream.at[i])
+        def staged(lo, *landed):
+            return [
+                pltpu.make_async_copy(src, stage.at[lo + i], a_load.at[lo + i])
                 for i, src in enumerate(landed)
             ]
+
+        def begin(copies):
             for copy in copies:
                 copy.start()
+
+        def add_staged(own, copies, lo):
             for copy in copies:
                 copy.wait()
-            add_rows(own, own, *[stage.at[i] for i in range(len(landed))])
+            add_rows(own, own, *[stage.at[lo + i] for i in range(len(copies))])
 
         def compute(k):
             h, t, slot = k // LINE, order[k % LINE], k % 2
@@ -1189,26 +1271,52 @@
             for quad in (far, fst, sec, mine):
                 a_sibling(t, quad, h, slot).start()
 
+        def spread_in(k):
+            t, h = order[k % LINE], k // LINE
+            return staged(0, c_land.at[t, h, far], c_land.at[t, h, sec])
+
+        def spread_begin(k):
+            h, t, slot = k // LINE, order[k % LINE], k % 2
+            for quad in (far, sec):
+                a_sibling(t, quad, h, slot).wait_recv()
+            begin(spread_in(k))
+
         def spread(k):
-            h, t, slot = k // LINE, order[k % LINE], k % 2
-            for quad, place in ((far, 1), (sec, 0)):
-                a_sibling(t, quad, h, slot).wait_recv()
-                absorb(a_own(t, quad, h), c_land.at[t, h, quad])
+            h, t = k // LINE, order[k % LINE]
+            copies = spread_in(k)
+            for i, (quad, place) in enumerate(((far, 1), (sec, 0))):
+                add_staged(a_own(t, quad, h), copies[i : i + 1], i)
                 a_second(t, quad, h, place).start()
 
-        def inward(k):
+        def inward_in(k):
+            t, h = order[k % LINE], k // LINE
+            return staged(2, c_land.at[t, h, fst], s_land.at[1, t, h])
+
+        def inward_begin(k):
             h, t, slot = k // LINE, order[k % LINE], k % 2
             a_sibling(t, fst, h, slot).wait_recv()
             a_second(t, far, h, 1).wait_recv()
-            absorb(a_own(t, fst, h), c_land.at[t, h, fst], s_land.at[1, t, h])
+            begin(inward_in(k))
+
+        def inward(k):
+            h, t = k // LINE, order[k % LINE]
+            add_staged(a_own(t, fst, h), inward_in(k), 2)
             a_first(t, h).start()
 
-        def collect(k):
+        def collect_in(k):
+            t, h = order[k % LINE], k // LINE
+            return staged(4, c_land.at[t, h, mine], s_land.at[0, t, h], f_land.at[t, h])
+
+        def collect_begin(k):
             h, t, slot = k // LINE, order[k % LINE], k % 2
             a_sibling(t, mine, h, slot).wait_recv()
             a_second(t, sec, h, 0).wait_recv()
             a_first(t, h).wait_recv()
-            absorb(a_own(t, mine, h), c_land.at[t, h, mine], s_land.at[0, t, h], f_land.at[t, h])
+            begin(collect_in(k))
+
+        def collect(k):
+            h, t = k // LINE, order[k % LINE]
+            add_staged(a_own(t, mine, h), collect_in(k), 4)
 
             @pl.when((t < z) & (z == last))
             def _():
@@ -1224,13 +1332,17 @@
             @pl.when((t < z) & (z < last))
             def _():
                 a_line(t, h, False).wait_recv()
-                absorb(a_own(t, mine, h), l_land.at[0, t, h])
+                copies = staged(7, l_land.at[0, t, h])
+                begin(copies)
+                add_staged(a_own(t, mine, h), copies, 7)
                 a_line(t, h, False).start()
 
             @pl.when((t > z) & (z > 0))
             def _():
                 a_line(t, h, True).wait_recv()
-                absorb(a_own(t, mine, h), l_land.at[1, t, h])
+                copies = staged(7, l_land.at[1, t, h])
+                begin(copies)
+                add_staged(a_own(t, mine, h), copies, 7)
                 a_line(t, h, True).start()
 
         def exchange(k):
@@ -1242,7 +1354,7 @@
         def small(step, src, dst, device):
             return remote(src, dst, small_s.at[step], small_r.at[step], device)
 
-        def first_norm():
+        def first_norm(w_rows):
             shards = w_rows.shape[1]
             wide = 512
             x_scale = rms_scale(x_ref[...].astype(f32))
@@ -1279,73 +1391,123 @@
 
             lax.fori_loop(0, dim // wide, spread_mean, 0)
 
+        def mlp_results(d_tmp, middle, y, y_half):
+            middle_in = pltpu.make_async_copy(middle_ref, middle, load.at[0])
+            middle_in.start()
+            each(MLP_D, lambda piece, group: finish(piece, group, d_tmp))
+            d_back = pltpu.make_async_copy(d_tmp, d_out, load.at[1])
+            d_back.start()
+            line_sum(1, y)
+            middle_in.wait()
+
+            def last_add(i, carry):
+                at = tile(i, 512)
+                y_half[:, at] = (middle[:, at] + y[:, at]).astype(bf16)
+                return carry
+
+            lax.fori_loop(0, dim // 512, last_add, 0)
+            y_back = pltpu.make_async_copy(y_half, y_out, load.at[2])
+            y_back.start()
+            each(MLP_D, drain_sibling)
+            each(MLP_D, drain)
+            d_back.wait()
+            y_back.wait()
+
         small_c = small(0, s_sum.at[3], s_got.at[0], sibling)
         each(MLP_GU, drain_sibling)
         compute(0)
         share(0)
         narrow(3, 0)
-        spread(0)
         compute(1)
         share(1)
-        spread(1)
-        relay(1, 1)
-        inward(0)
+        spread_begin(0)
         compute(2)
         share(2)
-        spread(2)
-        inward(1)
-        relay(1, 2)
+        spread(0)
+        spread_begin(1)
+        relay(1, 1)
         compute(3)
         share(3)
-        spread(3)
+        spread(1)
+        spread_begin(2)
+        inward_begin(0)
+        spread(2)
+        spread_begin(3)
+        inward(0)
         each(MLP_GU, finish)
         gu_back = pltpu.make_async_copy(gu_all.at[:, 2 * mine + core], gu_out, back.at[0])
         gu_back.start()
-        collect(0)
-        inward(2)
-        gu_back.wait()
-        for k in range(1, LINE):
-            exchange(k).start()
         ex_in = pltpu.make_async_copy(gu_all.at[z, 2 * mine + core], ex_land.at[z], back.at[1])
         ex_in.start()
+        spread(3)
         each(MLP_GU, drain)
+        gu_back.wait()
+        exchange(2).start()
+        exchange(1).start()
         ex_in.wait()
         compute(4)
         share(4)
-        spread(4)
-        collect(1)
-        onward(0)
-        first_norm()
-        inward(3)
+        pl.run_scoped(first_norm, pltpu.VMEM((2, 4, shard_rows, qkv_width), bf16))
         small_c.start()
+        inward_begin(1)
         compute(5)
         share(5)
-        spread(5)
-        collect(2)
-        onward(1)
+        inward(1)
         small_c.wait()
         s_sum[0] = s_sum[3] + s_got[0]
         small_f = small(1, s_sum.at[0], s_got.at[1], first)
         small_f.start()
-        inward(4)
+        spread_begin(4)
+        relay(1, 2)
         compute(6)
         share(6)
-        spread(6)
-        collect(3)
-        onward(2)
-        inward(5)
+        spread(4)
+        spread_begin(5)
+        inward_begin(2)
+        compute(7)
+        share(7)
+        inward(2)
+        spread(5)
+        spread_begin(6)
         small_f.wait()
         s_sum[1] = s_sum[0] + s_got[1]
         small_s2 = small(2, s_sum.at[1], s_got.at[2], second)
         small_s2.start()
-        compute(7)
-        share(7)
+        spread(6)
+        spread_begin(7)
+        collect_begin(0)
         spread(7)
+        collect(0)
+        collect_begin(1)
+        inward_begin(3)
+        collect(1)
+        inward(3)
+        collect_begin(2)
+        collect(2)
+        onward(0)
+        onward(2)
+        collect_begin(3)
+        inward_begin(4)
+        collect(3)
+        inward(4)
+        exchange(3).start()
+        onward(1)
+        pl.run_scoped(
+            mlp_results,
+            pltpu.VMEM(gd_fst.shape, f32),
+            pltpu.VMEM((CAP, dim), f32),
+            pltpu.VMEM((CAP, dim), f32),
+            pltpu.VMEM((CAP, dim), bf16),
+        )
+        inward_begin(5)
+        collect_begin(4)
+        inward(5)
         collect(4)
+        inward_begin(6)
+        collect_begin(5)
         inward(6)
         collect(5)
         onward(4)
-        inward(7)
         small_s2.wait()
         s_sum[2] = s_sum[1] + s_got[2]
         small_line = [
@@ -1354,9 +1516,13 @@
         ]
         for copy in small_line:
             copy.start()
+        onward(5)
+        inward_begin(7)
+        collect_begin(6)
+        inward(7)
         collect(6)
-        onward(5)
         onward(6)
+        collect_begin(7)
         collect(7)
         for copy in small_line:
             copy.wait()
@@ -1387,9 +1553,9 @@
     kv = KVH * HD
     rows = gu_all.shape[2]
 
-    def both(dbr):
+    def both(dbr, mixed, normed):
         pl.run_scoped(
-            lambda *refs: attention(dbr, *refs),
+            lambda *refs: attention(dbr, mixed, normed, *refs),
             pltpu.VMEM((slots, v0), f32),
             pltpu.VMEM((slots, dim), bf16),
             pltpu.VMEM((slots, kv), bf16),
@@ -1401,41 +1567,24 @@
             pltpu.VMEM((2, 4, rows, dim), bf16),
         )
         pl.run_scoped(
-            lambda *refs: sums(dbr, *refs),
-            pltpu.VMEM((slots, dim), bf16),
-            pltpu.VMEM((slots, dim), bf16),
+            lambda *refs: sums(dbr, mixed, normed, *refs),
             pltpu.VMEM((2, RING // 2, rows, piece_cols), bf16),
-            pltpu.VMEM((3, rows, piece_cols), bf16),
-            pltpu.VMEM((2, 2, rows, qkv_width), bf16),
+            pltpu.VMEM((8, rows, piece_cols), bf16),
         )
 
-    pl.run_scoped(both, pltpu.VMEM((slots, dim), bf16))
+    pl.run_scoped(
+        both,
+        pltpu.VMEM((slots, dim), bf16),
+        pltpu.VMEM((slots, dim), bf16),
+        pltpu.VMEM((slots, dim), bf16),
+    )
 
     def a_landed(t, h, upward):
         landing = l_land.at[1 if upward else 0, t, h]
         sems = (au_send, au_recv) if upward else (ad_send, ad_recv)
         return remote(landing, landing, sems[0].at[t, h], sems[1].at[t, h], sibling)
 
-    def results(middle, y, y_half, d_tmp, a_tmp, stage):
-        middle_in = pltpu.make_async_copy(middle_ref, middle, load.at[0])
-        middle_in.start()
-        each(MLP_D, lambda piece, group: finish(piece, group, d_tmp))
-        d_back = pltpu.make_async_copy(d_tmp, d_out, load.at[1])
-        d_back.start()
-        line_sum(1, y)
-        middle_in.wait()
-
-        def last_add(i, carry):
-            at = tile(i, 512)
-            y_half[:, at] = (middle[:, at] + y[:, at]).astype(bf16)
-            return carry
-
-        lax.fori_loop(0, dim // 512, last_add, 0)
-        y_back = pltpu.make_async_copy(y_half, y_out, load.at[2])
-        y_back.start()
-        each(MLP_D, drain_sibling)
-        each(MLP_D, drain)
-
+    def results(a_tmp, stage):
         for h in range(2):
 
             @pl.when(z < last)
@@ -1476,15 +1625,10 @@
 
         a_back = pltpu.make_async_copy(a_tmp, a_out, load.at[3])
         a_back.start()
-        for copy in (d_back, y_back, a_back):
-            copy.wait()
+        a_back.wait()
 
     pl.run_scoped(
         results,
-        pltpu.VMEM((slots, dim), f32),
-        pltpu.VMEM((slots, dim), f32),
-        pltpu.VMEM((slots, dim), bf16),
-        pltpu.VMEM(gd_fst.shape, f32),
         pltpu.VMEM((rows, 2 * piece_cols), f32),
         pltpu.VMEM((2, rows, piece_cols), bf16),
     )
@@ -1500,10 +1644,10 @@
                 send_line(t_own.at[which, k], which, k, True).wait_send()
 
 
-def backward(gu, wd, tok, cot, hid, dgu, w, middle, normed, raw, q, k, v, mixed, x, gains, rope):
+def backward(gu, down, tok, cot, hid, pre, w, middle, normed, raw, q, k, v, mixed, x, gains, rope):
     dim = tok.shape[1]
     rows = w.shape[1]
-    drows = wd.shape[0] // RING
+    drows = down.shape[0]
     cols = gu.shape[1]
     quads = RING // 2
     pieces = LINE + 2
@@ -1523,9 +1667,10 @@
             S((2, LINE, 2, rows, cols), bf16),
             S((LINE, 2, rows, cols), bf16),
             S((2, LINE, 2, rows, cols), bf16),
+            S((RING * drows, dim), bf16),
         ),
         in_specs=[ANY] * 14 + [VMEM] * 3,
-        out_specs=(VMEM,) * 2 + (ANY,) * 9,
+        out_specs=(VMEM,) * 2 + (ANY,) * 10,
         scratch_shapes=[
             pltpu.VMEM((LINE, RING, rows, cols), bf16),
             pltpu.VMEM((RING, drows, dim), bf16),
@@ -1552,7 +1697,7 @@
             DMA((2, LINE)),
             DMA((2, LINE)),
             DMA((2, LINE)),
-            DMA((6,)),
+            DMA((8,)),
             DMA((3,)),
             DMA((2,)),
             DMA((2, quads)),
@@ -1569,12 +1714,18 @@
             DMA((LINE,)),
             DMA((2 + LINE,)),
             DMA((2 + LINE,)),
+            DMA((RING, 2)),
+            DMA((RING, 2)),
+            DMA((RING, 2)),
+            DMA((RING, 2)),
+            DMA((2, 3)),
+            DMA((8,)),
         ],
         compiler_params=pltpu.CompilerParams(
             collective_id=2, has_side_effects=True, vmem_limit_bytes=65400 * 1024
         ),
         name="backward",
-    )(gu, wd, tok, cot, hid, dgu, w, middle, normed, raw, q, k, v, mixed, x, gains, rope)
+    )(gu, down, tok, cot, hid, pre, w, middle, normed, raw, q, k, v, mixed, x, gains, rope)
 
 
 def results_kernel(
@@ -1897,19 +2048,19 @@
     w_down,
 ):
     (
-        attn_w, gate_up_w, down_w, tokens, cotangent, hidden, d_gate_up,
+        attn_w, gate_up_w, tokens, cotangent, hidden, gate_up,
         middle, normed, qkv_raw, queries, keys, values, mixed, gains, rope,
     ) = forward(
         hidden_in, out_grad, seq_lengths, seq_device, (attn_gain, mlp_gain, q_gain, k_gain),
-        w_query, w_key, w_value, w_out, w_gate, w_up, w_down,
+        w_query, w_key, w_value, w_out, w_gate, w_up,
     )
     dim = hidden_in.shape[1]
     x, small, y, grad_down, attn_sums, exchanged, *unused = backward(
         gate_up_w.reshape(-1, gate_up_w.shape[-1]),
-        down_w.reshape(-1, dim),
+        w_down,
         tokens.reshape(-1, dim),
         cotangent.reshape(-1, dim),
-        hidden, d_gate_up, attn_w, middle, normed, qkv_raw, queries, keys, values, mixed,
+        hidden, gate_up, attn_w, middle, normed, qkv_raw, queries, keys, values, mixed,
         hidden_in, gains, rope,
     )
     (

time: 453 us -> 440 us (0.971)
  Pallas kernels: 449 us -> 437 us
    pallas_call x1, Pallas kernels: 209 us -> 183 us  [forward(): pl.pallas_call(forward_kernel, out_shape=(S((n, rows, wide), bf16), S((LI...]
    pallas_call x1, Pallas kernels: 235 us -> 249 us  [backward(): pl.pallas_call(backward_kernel, out_shape=(S((CAP, dim), f32), S((8, dim)...]
where the time goes in v5:
time: 440 us; the launch traced here: 438 us
  Pallas kernels  437 us (99%)
    pallas_call x1, Pallas kernels, backward(): pl.pallas_call(backward_kernel, out_shape=(S((CAP, dim), f32), S((8, dim)...  249 us
    pallas_call x1, Pallas kernels, forward(): pl.pallas_call(forward_kernel, out_shape=(S((n, rows, wide), bf16), S((LI...  183 us

profile of v5, /device:TPU:8, one launch (start us, length us, event | category | flops | bytes accessed | tf_op | source)
XLA Modules:
  0.0 438.1 jit_solution(8156824651157242989)
XLA Ops:
  0.6 182.8 %forward.1 = (bf16[32,64,6272]{2,1,0:T(8,128)(2,1)}, bf16[4,8,64,3072]{3,2,1,0:T(8,128)(2,1)}, bf16[4,128,2048]{2,1,0:T(8,128)(2,1)}, bf16[4,128,2048]{2,1,0:T(8...) custom-call(bf16[128,2048]{1,0:T(8,128)(2,1)} %x_ref.3, ...), custom_call_target="tpu_custom_call" | custom-call | tf_op jit(solution)/shard_map/forward/pallas_call | solution.py:656
  183.5 248.9 %backward.1 = (f32[128,2048]{1,0:T(8,128)}, f32[8,2048]{1,0:T(8,128)}, bf16[128,2048]{1,0:T(8,128)(2,1)}, f32[192,2048]{1,0:T(8,128)}, f32[64,6144]{1,0:T(8,128)...) custom-call(bf16[2048,3072]{1,0:T(8,128)(2,1)} %bitcast.13, ...), custom_call_target="tpu_custom_call" | custom-call | tf_op jit(solution)/shard_map/backward/pallas_call | solution.py:1656
  432.4 5.6 %results.1 = (bf16[128,2048]{1,0:T(8,128)(2,1)}, f32[128,2048]{1,0:T(8,128)}, f32[64,2048]{1,0:T(8,128)}, f32[64,1024]{1,0:T(8,128)}, f32[64,1024]{1,0:T(8,128)}...) custom-call(bf16[128,2048]{1,0:T(8,128)(2,1)} %get-tuple-element.62., ...), custom_call_target="tpu_custom_call" | custom-call | tf_op jit(solution)/shard_map/results/pallas_call | solution.py:1783

commit v6 on v5

--- a/solution.py
+++ b/solution.py
@@ -161,10 +161,10 @@
 
 def forward_kernel(
     x_ref, len_ref, dev_ref, ga_ref, gm_ref, gq_ref, gk_ref, cot_ref,
-    wq_ref, wk_ref, wv_ref, wo_ref, gate_ref, up_ref,
-    w_out, gu_out, tok_out, cot_out, hid_out, pre_out,
+    wq_ref, wk_ref, wv_ref, wo_ref, gate_ref, up_ref, wd_ref,
+    w_out, gu_out, d_out, tok_out, cot_out, hid_out, pre_out,
     middle_out, normed_out, raw_out, q_out, k_out, v_out, mixed_out, gains_out, rope_out,
-    w_tmp, p_tmp, cot_tmp, second_tmp, chunk, ow_all, gain_tmp, gain_own,
+    w_tmp, p_tmp, d_tmp, cot_tmp, second_tmp, chunk, ow_all, gain_tmp, gain_own,
     tok_all, gate_up, m_chunk, hid,
     local, up_s, down_s, first_s, second_s, sib_s, recv, ex_send, ex_recv,
     m_first_s, m_second_s, m_sib_s, m_recv, line_up, line_down, line_r, w_load, o_load, g_load,
@@ -178,7 +178,7 @@
     qkv_width = raw_out.shape[1]
     attn_width = qkv_width + wo_ref.shape[1]
     last = LINE - 1
-    pieces = LINE
+    pieces = LINE + 1
 
     w_in = []
     lo = 0
@@ -195,7 +195,8 @@
         for which, ref in enumerate((gate_ref, up_ref))
     ]
     cot_in = pltpu.make_async_copy(cot_ref, cot_tmp, local.at[8])
-    for copy in w_in + p_in + [cot_in]:
+    d_in = pltpu.make_async_copy(wd_ref, d_tmp, local.at[7])
+    for copy in w_in + p_in + [d_in, cot_in]:
         copy.start()
     gain_own[...] = jnp.zeros_like(gain_own)
     for i, ref in enumerate((ga_ref, gm_ref, gq_ref, gk_ref)):
@@ -378,13 +379,12 @@
     other(scol, 1, False)
     other(sfcol, 0, False)
     w_back.wait()
+    line_relay(1, 1)
     group(0)
     other(fcol, 3, True)
     other(scol, 2, False)
     other(sfcol, 1, False)
-    group(1)
-
-    for copy in p_in:
+    for copy in p_in + [d_in]:
         copy.wait()
     for k in range(1, LINE):
         for which in range(2):
@@ -393,10 +393,10 @@
             remote(landed, landed, ex_send.at[k, which], ex_recv.at[k, which], second).wait_recv()
 
     def spot(piece, shard):
-        return gu_out.at[piece, shard]
+        return gu_out.at[piece, shard] if piece < LINE else d_out.at[shard]
 
     def source(piece):
-        return p_tmp.at[piece]
+        return p_tmp.at[piece] if piece < LINE else d_tmp
 
     def m_send(src, piece, shard, sems, device):
         return remote(
@@ -419,15 +419,22 @@
 
     m_own_second(0)
     m_own_second(1)
+    m_own_second(LINE)
     p_back = pltpu.make_async_copy(p_tmp, gu_out.at[:, col], local.at[11])
     p_back.start()
-    line_relay(1, 1)
+    d_back = pltpu.make_async_copy(d_tmp, d_out.at[col], local.at[4])
+    d_back.start()
+    line_relay(1, 2)
+    group(1)
+
     other(scol, 3, False)
     other(sfcol, 2, False)
     group(2)
     other(sfcol, 3, False)
     m_own_first(0)
     m_own_first(1)
+    m_own_first(LINE)
+    line_relay(1, 3)
     group(3)
 
     small = jnp.zeros((16, 128), f32)
@@ -536,14 +543,12 @@
     line_own(2, second_tmp.at[:, pl.ds(token_half, token_half)])
     tok_back = pltpu.make_async_copy(second_tmp, tok_out.at[z], local.at[13])
     tok_back.start()
-    line_relay(1, 2)
     m_other(0, fcol, True)
     m_other(0, scol, False)
     m_own(3)
     line_relay(0, 1)
     line_relay(2, 1)
     m_other(1, fcol, True)
-    line_relay(1, 3)
     m_other(1, scol, False)
     m_other(0, sfcol, False)
     line_relay(0, 2)
@@ -555,6 +560,8 @@
     gate_up_load(0)
     m_other(3, fcol, True)
     m_other(3, scol, False)
+    m_other(LINE, fcol, True)
+    m_other(LINE, scol, False)
     line_relay(0, 3)
     tok_back.wait()
     cot_back.wait()
@@ -609,6 +616,9 @@
         return carry
 
     lax.fori_loop(0, part // 256, units, 0)
+    m_other(LINE, sfcol, False)
+    d_back.wait()
+    m_whole(LINE)
 
     for n in range(part // 256):
         for copy in [hid_copy(n)] + pre_copies(n):
@@ -644,20 +654,21 @@
             m_send(src, piece, base, m_sib_s, sibling).wait_send()
 
 
-def forward(hidden_in, out_grad, seq_lengths, seq_device, gains, wq, wk, wv, wo, gate, up):
+def forward(hidden_in, out_grad, seq_lengths, seq_device, gains, wq, wk, wv, wo, gate, up, wd):
     slots, dim = hidden_in.shape
     rows = wq.shape[0]
     n = RING * LINE
     width = gate.shape[1] // LINE
     qkv_width = wq.shape[1] + wk.shape[1] + wv.shape[1]
     wide = qkv_width + wo.shape[1] + 128
-    pieces = LINE
+    pieces = LINE + 1
     S = jax.ShapeDtypeStruct
     return pl.pallas_call(
         forward_kernel,
         out_shape=(
             S((n, rows, wide), bf16),
             S((LINE, RING, rows, 2 * width), bf16),
+            S((RING,) + wd.shape, bf16),
             S((LINE, slots, dim), bf16),
             S((LINE, slots, dim), bf16),
             S((LINE * slots, width), bf16),
@@ -672,11 +683,12 @@
             S((8, dim), f32),
             S((3, slots, HD), f32),
         ),
-        in_specs=[VMEM] * 7 + [ANY] * 7,
-        out_specs=(ANY,) * 6 + (VMEM,) * 9,
+        in_specs=[VMEM] * 7 + [ANY] * 8,
+        out_specs=(ANY,) * 7 + (VMEM,) * 9,
         scratch_shapes=[
             pltpu.VMEM((rows, wide), bf16),
             pltpu.VMEM((LINE, rows, 2 * width), bf16),
+            pltpu.VMEM(wd.shape, bf16),
             pltpu.VMEM((slots, dim), bf16),
             pltpu.VMEM((slots, dim), bf16),
             pltpu.VMEM((RING, rows, qkv_width), bf16),
@@ -714,26 +726,24 @@
         name="forward",
     )(
         hidden_in, seq_lengths[None, :], seq_device[None, :], *[g[None, :] for g in gains],
-        out_grad, wq, wk, wv, wo, gate, up,
+        out_grad, wq, wk, wv, wo, gate, up, wd,
     )
 
 
 def backward_kernel(
-    gu_ref, down_ref, tok_ref, cot_ref, hid_ref, pre_ref, w_ref, middle_ref, normed_ref, raw_ref,
+    gu_ref, wd_ref, tok_ref, cot_ref, hid_ref, pre_ref, w_ref, middle_ref, normed_ref, raw_ref,
     q_ref, k_ref, v_ref, mixed_ref, x_ref, gains_ref, rope_ref,
-    x_out, small_out, y_out, d_out, a_out, ex_land, gu_out, c_land, s_land, f_land, l_land, wd_ref,
+    x_out, small_out, y_out, d_out, a_out, ex_land, gu_out, c_land, s_land, f_land, l_land,
     gu_all, gd_all, gu_sib, gd_sib, gu_sec, gd_sec, gu_fst, gd_fst, t_own, t_land,
     dmid, dqkv, s_sum, s_got, s_line,
     c_send, c_recv, s_send, s_recv, f_send, f_recv, down_s, down_r, up_s, up_r, load, stream, back,
     ac_send, ac_recv, as_send, as_recv, af_send, af_recv, ad_send, ad_recv, au_send, au_recv,
-    ex_s, ex_r, small_s, small_r, w_first, w_second, w_sib, w_recv, units_in,
+    ex_s, ex_r, small_s, small_r, units_in,
     a_load,
 ):
     me, z, first, second, sibling = where_am_i()
     greet(line_peers(me) + [first, second, sibling])
     core = me % 2
-    col, fcol, scol = me % RING, first % RING, second % RING
-    sfcol = (second + first - me) % RING
     mine, fst, sec = (me % RING) // 2, (first % RING) // 2, (second % RING) // 2
     far = ((second + first - me) % RING) // 2
     half = gd_fst.shape[0] // 2
@@ -895,36 +905,10 @@
         def _():
             add_rows(out, own, above, below)
 
-    def w_spot(shard, piece):
-        return wd_ref.at[pl.ds(pl.multiple_of(shard * 2 * half + piece * half, half), half)]
-
-    def w_send(src, shard, piece, sems, device):
-        return remote(
-            src, w_spot(shard, piece), sems.at[shard, piece], w_recv.at[shard, piece], device
-        )
-
-    def w_arrived(shard, piece):
-        w_send(w_spot(shard, piece), shard, piece, w_sib, sibling).wait_recv()
-
-    def w_other(shard, onward):
-        for piece in range(2):
-            w_arrived(shard, piece)
-            src = w_spot(shard, piece)
-            if onward:
-                w_send(src, shard, piece, w_second, second).start()
-            w_send(src, shard, piece, w_sib, sibling).start()
-
-    for piece in range(2):
-        src = down_ref.at[pl.ds(piece * half, half)]
-        w_send(src, col, piece, w_first, first).start()
-        w_send(src, col, piece, w_second, second).start()
-        w_send(src, col, piece, w_sib, sibling).start()
-
-    def mlp(tok, cot, hid, dgu, down_own):
+    def mlp(tok, cot, hid, dgu):
         ins = [
             pltpu.make_async_copy(hid_ref, hid, load.at[0]),
             pltpu.make_async_copy(cot_ref, cot, load.at[1]),
-            pltpu.make_async_copy(down_ref, down_own, load.at[2]),
             pltpu.make_async_copy(tok_ref, tok, load.at[3]),
         ]
         for copy in ins:
@@ -947,20 +931,8 @@
             if previous is not None:
                 each(MLP_D, lambda piece, group, q=previous: to_sibling(q, piece, group).start())
             previous = quad
-        ins[2].wait()
-        down_back = pltpu.make_async_copy(
-            down_own, wd_ref.at[tile(col, 2 * half)], load.at[4]
-        )
-        down_back.start()
         each(MLP_D, lambda piece, group, q=previous: to_sibling(q, piece, group).start())
-        w_other(fcol, True)
-        w_other(scol, False)
         each(MLP_D, pass_on)
-        w_other(sfcol, False)
-        for piece in range(2):
-            for k in range(RING // 2):
-                w_arrived(2 * k + sibling % 2, piece)
-        down_back.wait()
 
         def units(gate_t, up_t, down_w, dhid_t):
             def fetch(i, slot):
@@ -1014,8 +986,9 @@
 
             streamed(dim // wide, fetch, body)
 
-        ins[3].wait()
         pl.run_scoped(back_through, pltpu.VMEM((2, wide, 2 * part), bf16))
+        ins[2].wait()
+        line_own(0)
 
         rows = dim // LINE
         for piece in range(LINE):
@@ -1027,14 +1000,14 @@
                 return carry
 
             lax.fori_loop(0, 2 * part // 512, columns, 0)
-            if piece == 0:
-                line_own(0)
-            else:
+            if piece > 0:
                 pass_on(piece - 1, 0)
             for quad in (far, fst, sec, mine):
                 to_sibling(quad, piece, 0).start()
+            if piece == 2:
+                relay(0, 0)
+        pass_on(LINE - 1, 0)
         each(MLP_D, narrow)
-        relay(0, 0)
 
         def out_through(cols_w):
             def fetch(i, slot):
@@ -1048,9 +1021,16 @@
                 out = jnp.dot(hid[...], cols_w[slot], preferred_element_type=f32).astype(bf16)
                 t_own[1, :, :, tile(i, wide)] = out.reshape(LINE, CAP, wide)
 
+                @pl.when(i == 3)
+                def _():
+                    relay(0, 1)
+
+                @pl.when(i == 5)
+                def _():
+                    relay(0, 2)
+
             streamed(dim // wide, fetch, body)
 
-        pass_on(LINE - 1, 0)
         pl.run_scoped(out_through, pltpu.VMEM((2, part, wide), bf16))
 
     pl.run_scoped(
@@ -1059,16 +1039,7 @@
         pltpu.VMEM((tokens, dim), bf16),
         pltpu.VMEM((tokens, part), bf16),
         pltpu.VMEM((tokens, 2 * part), bf16),
-        pltpu.VMEM((2 * half, dim), bf16),
     )
-    for piece in range(2):
-        src = down_ref.at[pl.ds(piece * half, half)]
-        w_send(src, col, piece, w_first, first).wait_send()
-        w_send(src, col, piece, w_second, second).wait_send()
-        w_send(src, fcol, piece, w_second, second).wait_send()
-        for base in (col, fcol, scol, sfcol):
-            w_send(src, base, piece, w_sib, sibling).wait_send()
-
     def attention(dbr, mixed, normed, raw, q, k, v, cot, dsec, dmix, middle, w_rows):
         ins = [
             pltpu.make_async_copy(src, dst, load.at[i])
@@ -1087,9 +1058,7 @@
         ]
         for copy in ins:
             copy.start()
-        relay(0, 1)
         narrow(0, 0)
-        relay(0, 2)
         line_own(1)
         for copy in ins:
             copy.wait()
@@ -1644,10 +1613,10 @@
                 send_line(t_own.at[which, k], which, k, True).wait_send()
 
 
-def backward(gu, down, tok, cot, hid, pre, w, middle, normed, raw, q, k, v, mixed, x, gains, rope):
+def backward(gu, wd, tok, cot, hid, pre, w, middle, normed, raw, q, k, v, mixed, x, gains, rope):
     dim = tok.shape[1]
     rows = w.shape[1]
-    drows = down.shape[0]
+    drows = wd.shape[0] // RING
     cols = gu.shape[1]
     quads = RING // 2
     pieces = LINE + 2
@@ -1667,10 +1636,9 @@
             S((2, LINE, 2, rows, cols), bf16),
             S((LINE, 2, rows, cols), bf16),
             S((2, LINE, 2, rows, cols), bf16),
-            S((RING * drows, dim), bf16),
         ),
         in_specs=[ANY] * 14 + [VMEM] * 3,
-        out_specs=(VMEM,) * 2 + (ANY,) * 10,
+        out_specs=(VMEM,) * 2 + (ANY,) * 9,
         scratch_shapes=[
             pltpu.VMEM((LINE, RING, rows, cols), bf16),
             pltpu.VMEM((RING, drows, dim), bf16),
@@ -1714,10 +1682,6 @@
             DMA((LINE,)),
             DMA((2 + LINE,)),
             DMA((2 + LINE,)),
-            DMA((RING, 2)),
-            DMA((RING, 2)),
-            DMA((RING, 2)),
-            DMA((RING, 2)),
             DMA((2, 3)),
             DMA((8,)),
         ],
@@ -1725,7 +1689,7 @@
             collective_id=2, has_side_effects=True, vmem_limit_bytes=65400 * 1024
         ),
         name="backward",
-    )(gu, down, tok, cot, hid, pre, w, middle, normed, raw, q, k, v, mixed, x, gains, rope)
+    )(gu, wd, tok, cot, hid, pre, w, middle, normed, raw, q, k, v, mixed, x, gains, rope)
 
 
 def results_kernel(
@@ -2048,16 +2012,16 @@
     w_down,
 ):
     (
-        attn_w, gate_up_w, tokens, cotangent, hidden, gate_up,
+        attn_w, gate_up_w, down_w, tokens, cotangent, hidden, gate_up,
         middle, normed, qkv_raw, queries, keys, values, mixed, gains, rope,
     ) = forward(
         hidden_in, out_grad, seq_lengths, seq_device, (attn_gain, mlp_gain, q_gain, k_gain),
-        w_query, w_key, w_value, w_out, w_gate, w_up,
+        w_query, w_key, w_value, w_out, w_gate, w_up, w_down,
     )
     dim = hidden_in.shape[1]
     x, small, y, grad_down, attn_sums, exchanged, *unused = backward(
         gate_up_w.reshape(-1, gate_up_w.shape[-1]),
-        w_down,
+        down_w.reshape(-1, dim),
         tokens.reshape(-1, dim),
         cotangent.reshape(-1, dim),
         hidden, gate_up, attn_w, middle, normed, qkv_raw, queries, keys, values, mixed,

time: 440 us -> 423 us (0.961)
  Pallas kernels: 437 us -> 421 us
    pallas_call x1, Pallas kernels: 249 us -> 217 us  [backward(): pl.pallas_call(backward_kernel, out_shape=(S((CAP, dim), f32), S((8, dim)...]
    pallas_call x1, Pallas kernels: 183 us -> 199 us  [forward(): pl.pallas_call(forward_kernel, out_shape=(S((n, rows, wide), bf16), S((LI...]
where the time goes in v6:
time: 423 us; the launch traced here: 422 us
  Pallas kernels  421 us (100%)
    pallas_call x1, Pallas kernels, backward(): pl.pallas_call(backward_kernel, out_shape=(S((CAP, dim), f32), S((8, dim)...  217 us
    pallas_call x1, Pallas kernels, forward(): pl.pallas_call(forward_kernel, out_shape=(S((n, rows, wide), bf16), S((LI...  199 us

profile of v6, /device:TPU:8, one launch (start us, length us, event | category | flops | bytes accessed | tf_op | source)
XLA Modules:
  0.0 421.9 jit_solution(10006900804035665142)
XLA Ops:
  0.7 198.6 %forward.1 = (bf16[32,64,6272]{2,1,0:T(8,128)(2,1)}, bf16[4,8,64,3072]{3,2,1,0:T(8,128)(2,1)}, bf16[8,192,2048]{2,1,0:T(8,128)(2,1)}, bf16[4,128,2048]{2,1,0:T(8...) custom-call(bf16[128,2048]{1,0:T(8,128)(2,1)} %x_ref.3, ...), custom_call_target="tpu_custom_call" | custom-call | tf_op jit(solution)/shard_map/forward/pallas_call | solution.py:666
  199.3 216.9 %backward.1 = (f32[128,2048]{1,0:T(8,128)}, f32[8,2048]{1,0:T(8,128)}, bf16[128,2048]{1,0:T(8,128)(2,1)}, f32[192,2048]{1,0:T(8,128)}, f32[64,6144]{1,0:T(8,128)...) custom-call(bf16[2048,3072]{1,0:T(8,128)(2,1)} %bitcast.14, ...), custom_call_target="tpu_custom_call" | custom-call | tf_op jit(solution)/shard_map/backward/pallas_call | solution.py:1625
  416.2 5.6 %results.1 = (bf16[128,2048]{1,0:T(8,128)(2,1)}, f32[128,2048]{1,0:T(8,128)}, f32[64,2048]{1,0:T(8,128)}, f32[64,1024]{1,0:T(8,128)}, f32[64,1024]{1,0:T(8,128)}...) custom-call(bf16[128,2048]{1,0:T(8,128)(2,1)} %get-tuple-element.64., ...), custom_call_target="tpu_custom_call" | custom-call | tf_op jit(solution)/shard_map/results/pallas_call | solution.py:1747

commit v7 on v6

--- a/solution.py
+++ b/solution.py
@@ -611,7 +611,7 @@
             hid[some, at] = (gate * jax.nn.sigmoid(gate) * up).astype(bf16)
             return inner
 
-        lax.fori_loop(0, LINE * CAP // 32, act, 0)
+        lax.fori_loop(0, LINE * CAP // 32, act, 0, unroll=4)
         hid_copy(n).start()
         return carry
 
@@ -960,7 +960,7 @@
                     dgu[at, up_at] = (dhid * (gate * sig)).astype(bf16)
                     return carry
 
-                lax.fori_loop(0, tokens // 32, act, 0)
+                lax.fori_loop(0, tokens // 32, act, 0, unroll=4)
 
             streamed(part // wide, fetch, body)
 

time: 423 us -> 422 us (level)
  no operation moved by 1% of the time
where the time goes in v7:
time: 422 us; the launch traced here: 421 us
  Pallas kernels  420 us (100%)
    pallas_call x1, Pallas kernels, backward(): pl.pallas_call(backward_kernel, out_shape=(S((CAP, dim), f32), S((8, dim)...  217 us
    pallas_call x1, Pallas kernels, forward(): pl.pallas_call(forward_kernel, out_shape=(S((n, rows, wide), bf16), S((LI...  198 us

profile of v7, /device:TPU:8, one launch (start us, length us, event | category | flops | bytes accessed | tf_op | source)
XLA Modules:
  0.0 421.0 jit_solution(2057870278846023679)
XLA Ops:
  0.7 197.9 %forward.1 = (bf16[32,64,6272]{2,1,0:T(8,128)(2,1)}, bf16[4,8,64,3072]{3,2,1,0:T(8,128)(2,1)}, bf16[8,192,2048]{2,1,0:T(8,128)(2,1)}, bf16[4,128,2048]{2,1,0:T(8...) custom-call(bf16[128,2048]{1,0:T(8,128)(2,1)} %x_ref.3, ...), custom_call_target="tpu_custom_call" | custom-call | tf_op jit(solution)/shard_map/forward/pallas_call | solution.py:666
  198.6 216.7 %backward.1 = (f32[128,2048]{1,0:T(8,128)}, f32[8,2048]{1,0:T(8,128)}, bf16[128,2048]{1,0:T(8,128)(2,1)}, f32[192,2048]{1,0:T(8,128)}, f32[64,6144]{1,0:T(8,128)...) custom-call(bf16[2048,3072]{1,0:T(8,128)(2,1)} %bitcast.14, ...), custom_call_target="tpu_custom_call" | custom-call | tf_op jit(solution)/shard_map/backward/pallas_call | solution.py:1625
  415.3 5.6 %results.1 = (bf16[128,2048]{1,0:T(8,128)(2,1)}, f32[128,2048]{1,0:T(8,128)}, f32[64,2048]{1,0:T(8,128)}, f32[64,1024]{1,0:T(8,128)}, f32[64,1024]{1,0:T(8,128)}...) custom-call(bf16[128,2048]{1,0:T(8,128)(2,1)} %get-tuple-element.64., ...), custom_call_target="tpu_custom_call" | custom-call | tf_op jit(solution)/shard_map/results/pallas_call | solution.py:1747

commit v8 on v7

--- a/solution.py
+++ b/solution.py
@@ -111,7 +111,7 @@
         out[at, :] = total.astype(out.dtype)
         return carry
 
-    lax.fori_loop(0, rows // 16, body, 0)
+    lax.fori_loop(0, rows // 16, body, 0, unroll=2)
 
 
 def lane_sum(x):

time: 422 us -> 422 us (level)
  no operation moved by 1% of the time
where the time goes in v8:
time: 422 us; the launch traced here: 421 us
  Pallas kernels  420 us (100%)
    pallas_call x1, Pallas kernels, backward(): pl.pallas_call(backward_kernel, out_shape=(S((CAP, dim), f32), S((8, dim)...  216 us
    pallas_call x1, Pallas kernels, forward(): pl.pallas_call(forward_kernel, out_shape=(S((n, rows, wide), bf16), S((LI...  198 us

profile of v8, /device:TPU:8, one launch (start us, length us, event | category | flops | bytes accessed | tf_op | source)
XLA Modules:
  0.0 420.7 jit_solution(12315529895570956594)
XLA Ops:
  0.7 197.9 %forward.1 = (bf16[32,64,6272]{2,1,0:T(8,128)(2,1)}, bf16[4,8,64,3072]{3,2,1,0:T(8,128)(2,1)}, bf16[8,192,2048]{2,1,0:T(8,128)(2,1)}, bf16[4,128,2048]{2,1,0:T(8...) custom-call(bf16[128,2048]{1,0:T(8,128)(2,1)} %x_ref.3, ...), custom_call_target="tpu_custom_call" | custom-call | tf_op jit(solution)/shard_map/forward/pallas_call | solution.py:666
  198.6 216.5 %backward.1 = (f32[128,2048]{1,0:T(8,128)}, f32[8,2048]{1,0:T(8,128)}, bf16[128,2048]{1,0:T(8,128)(2,1)}, f32[192,2048]{1,0:T(8,128)}, f32[64,6144]{1,0:T(8,128)...) custom-call(bf16[2048,3072]{1,0:T(8,128)(2,1)} %bitcast.14, ...), custom_call_target="tpu_custom_call" | custom-call | tf_op jit(solution)/shard_map/backward/pallas_call | solution.py:1625
  415.1 5.5 %results.1 = (bf16[128,2048]{1,0:T(8,128)(2,1)}, f32[128,2048]{1,0:T(8,128)}, f32[64,2048]{1,0:T(8,128)}, f32[64,1024]{1,0:T(8,128)}, f32[64,1024]{1,0:T(8,128)}...) custom-call(bf16[128,2048]{1,0:T(8,128)(2,1)} %get-tuple-element.64., ...), custom_call_target="tpu_custom_call" | custom-call | tf_op jit(solution)/shard_map/results/pallas_call | solution.py:1747
